TPU v7x, 32 devices: a whole 2x2x4 slice. The times are simulated.
32 devices in a mesh: depth: 8 (over z, x), tile: 4 (over y, core).
Axes of the slice: x: 2, y: 2, z: 4, core: 2. Of those that a mesh axis runs over, the one named last changes fastest.
Arguments:
- volume: bfloat16 [64, 256, 4096], P('depth', 'tile'), may hold values from -6 to 6
- shear: int32 [64], replicated, may hold values from -64 to 64, as said below
- footprint: int32 [8, 2], P('depth'), may hold values from 0 to 4096, as said below
Outputs:
- frame: float32 [4, 256, 4096], P(None, 'tile', 'depth')
Inputs may be any that keep to these rules, and one draw needn't show every extreme that they name: Offsets follow a linear tilt over the slices with small jitter; shear[0] and shear[63] are the two ends of the range, in either order. footprint[b, 0] < 1024 and footprint[b, 1] > 3072 for every brick.
All inputs are finite; a program needn't handle non-finite values.
Results may differ from a plain program's by a relative error of at most 0.00085.
Values may be sent and summed in bfloat16 or wider, within the bound.
No kernel may reach another device: no remote copies, remote signals or barrier semaphores. Data moves between devices by JAX's collectives and lax.ppermute only.
A program may use at most 64 MiB of HBM per device.

v0:
```python
import functools

import jax
import jax.numpy as jnp
from jax import lax
from jax.experimental import pallas as pl
from jax.experimental.pallas import tpu as pltpu
from jax.sharding import PartitionSpec as P


LANES = 128
ROWS = 16
LOG2E = 1.4426950408889634
LINK = jnp.int16
INNER_MIB = 48
OUTER_MIB = 24


def params(mib):
    return pltpu.CompilerParams(vmem_limit_bytes=mib << 20)


def shade_slice(field, moved_v, moved_s, where, shift, base, r, narrow):
    tiles = field.shape[1]
    lane = lax.broadcasted_iota(jnp.int32, (ROWS, LANES), 1)
    leftmost, rightmost = lane == 0, lane == LANES - 1
    turn = jnp.where(shift < 0, shift + LANES, shift)
    here, up, down = pl.ds(r + 8, ROWS), pl.ds(r + 7, ROWS), pl.ds(r + 9, ROWS)
    zero = jnp.zeros((ROWS, LANES), jnp.float32)
    v = field[where, 0, here, :]
    ahead = pltpu.roll(v, LANES - 1, 1)
    behind_last = zero
    for t in range(tiles):
        v_next = field[where, t + 1, here, :] if t + 1 < tiles else zero
        ahead_next = pltpu.roll(v_next, LANES - 1, 1) if t + 1 < tiles else zero
        behind = pltpu.roll(v, 1, 1)
        dy = jnp.where(rightmost, ahead_next, ahead) - jnp.where(leftmost, behind_last, behind)
        dz = field[where + 1, t, here, :] - field[where - 1, t, here, :]
        dx = field[where, t, down, :] - field[where, t, up, :]
        squares = (dx * dx + dy * dy) + (dz * dz + 4.0)
        along = (0.35 * 0.48) * dx + (0.35 * 0.6) * dy + (0.35 * 0.64) * dz
        moved_s[base, t + 1] = 0.15 + jnp.abs(along) * lax.rsqrt(squares)
        v, ahead, behind_last = v_next, ahead_next, behind

    def turn_step(once, carry):
        for t in range(tiles):
            moved_v[base, t + 1] = pltpu.roll(narrow(t), turn, 1).astype(jnp.float32)
            moved_s[base, t + 1] = pltpu.roll(moved_s[base, t + 1], turn, 1)
        return carry

    lax.fori_loop(0, 1 + jnp.minimum(turn, 0), turn_step, 0)


def blend(state, moved_v, moved_s, index, shift, first, count, rate):
    lane = lax.broadcasted_iota(jnp.int32, (ROWS, LANES), 1)
    turn = jnp.where(shift < 0, shift + LANES, shift)
    start = first + jnp.where(shift < 0, 1, 0)
    keep = lane < turn
    values = [moved_v[index, start + j] for j in range(count + 1)]
    shades = [moved_s[index, start + j] for j in range(count + 1)]
    result = []
    for j in range(count):
        clear, total, colours = state[j]
        v = jnp.where(keep, values[j], values[j + 1])
        half = jnp.where(keep, shades[j], shades[j + 1])
        left = clear * jnp.exp2(v * v * rate[j])
        weight = (clear - left) * half
        arguments = (0.6 * v + 0.1, -0.4 * v, 0.25 * v - 0.15)
        colours = [colours[c] + weight * jnp.tanh(arguments[c]) for c in range(3)]
        result.append((left, total + weight, colours))
    return result


def rates(absorb, footprint, first, count):
    lane = lax.broadcasted_iota(jnp.int32, (ROWS, LANES), 1)
    found = []
    for j in range(count):
        column = lane + (first + j) * LANES
        inside = (column >= footprint[0, 0]) & (column < footprint[0, 1])
        found.append(jnp.where(inside, -absorb * LOG2E, 0.0))
    return found


def fresh(count):
    zero = jnp.zeros((ROWS, LANES), jnp.float32)
    return [(zero + 1.0, zero, [zero] * 3) for _ in range(count)]


def widen(field, index, line, place):
    line = line.astype(jnp.float32)
    for t in range(field.shape[1]):
        field[index, t, place : place + line.shape[0], :] = line[:, t * LANES : (t + 1) * LANES]


def set_row(field, index, place, line):
    for t in range(field.shape[1]):
        field[index, t, place : place + 1, :] = line[:, t * LANES : (t + 1) * LANES]


def set_edges(field, slices, strip, strips, up, down, edges):
    for index, block, _ in slices:
        widen(field, index, up[block], 0)
        widen(field, index, down[block], 8 + ROWS)
    if not edges:
        return
    for edge, last, place in ((edges[0], 0, 7), (edges[1], strips - 1, 8 + ROWS)):

        @pl.when(strip == last)
        def _(edge=edge, place=place):
            line = edge[...].astype(jnp.float32)
            for index, _, s in slices:
                set_row(field, index, place, line[s : s + 1])


def clear_edges(moved_v, moved_s):
    @pl.when(pl.program_id(0) == 0)
    def _():
        tiles = moved_v.shape[1] - 2
        zero = jnp.zeros((moved_v.shape[0], ROWS, LANES), jnp.float32)
        for t in (0, tiles + 1):
            moved_v[:, t] = zero
            moved_s[:, t] = zero


def emit(state, outs, slot, group, part, count):
    for j in range(count):
        at = pl.ds(pl.multiple_of((part * count + j) * LANES, LANES), LANES)
        clear, total, colours = state[j]
        for c in range(3):
            outs[slot][group, c, :, at] = (total + colours[c]).astype(jnp.bfloat16)
        outs[slot][group, 3, :, at] = (1.0 - clear).astype(jnp.bfloat16)


def over_columns(outs, me, inner, body):
    groups, _, _, width = outs[0].shape
    per = width // LANES
    count = min(2, per)
    for slot in range(inner):
        column = lax.rem(lax.rem(me, inner) + slot, inner)

        def column_step(i, carry, slot=slot, column=column):
            group, part = i // (per // count), lax.rem(i, per // count)
            first = (group * inner + column) * per + part * count
            emit(body(first, count), outs, slot, group, part, count)
            return carry

        lax.fori_loop(0, groups * (per // count), column_step, 0)


def inner_kernel(absorb, strip_of, strips, shear, footprint, vol, up, down, *refs):
    edges, (out, field, moved_v, moved_s) = refs[:-4], refs[-4:]
    slices, _, ny = vol.shape
    me = lax.axis_index("depth")
    flip = shear[0] > shear[shear.shape[0] - 1]
    clear_edges(moved_v, moved_s)
    centre = [(s, s, s) for s in range(1, slices - 1)]
    set_edges(field, centre, strip_of(pl.program_id(0)), strips, up, down, edges)

    def widen_step(s, carry):
        widen(field, s, vol[s], 8)
        return carry

    lax.fori_loop(0, slices, widen_step, 0)

    def shade_step(i, carry):
        narrow = lambda t: vol[i + 1, :, t * LANES : (t + 1) * LANES]
        shift = shear[me * slices + i + 1]
        shade_slice(field, moved_v, moved_s, i + 1, shift, i, 0, narrow)
        return carry

    lax.fori_loop(0, slices - 2, shade_step, 0)

    def column_step(pair, carry):
        first = 2 * pair
        rate = rates(absorb, footprint, first, 2)
        state = fresh(2)
        for step in range(slices - 2):
            i = jnp.where(flip, slices - 3 - step, step)
            shift = shear[me * slices + i + 1]
            state = blend(state, moved_v, moved_s, i, shift, first, 2, rate)
        for j in range(2):
            at = pl.ds(pl.multiple_of((first + j) * LANES, LANES), LANES)
            clear, total, colours = state[j]
            for c in range(3):
                out[c, :, at] = total + colours[c]
            out[3, :, at] = clear
        return carry

    lax.fori_loop(0, ny // LANES // 2, column_step, 0)


def outer_kernel(absorb, inner, strip_of, strips, shear, footprint, *refs):
    front, back, front_up, front_down, back_up, back_down, prev, nxt, mid = refs[:9]
    edges, outs, (field, moved_v, moved_s) = refs[9 : -3 - inner], refs[-3 - inner : -3], refs[-3:]
    me = lax.axis_index("depth")
    flip = shear[0] > shear[shear.shape[0] - 1]
    slices = shear.shape[0] // lax.axis_size("depth")
    strip = strip_of(pl.program_id(0))
    clear_edges(moved_v, moved_s)
    set_edges(field, [(1, 0, 0)], strip, strips, front_up, front_down, edges)
    set_edges(field, [(4, 0, slices - 1)], strip, strips, back_up, back_down, edges)
    for index, line in enumerate((prev, front.at[0], front.at[1], back.at[0], back.at[1], nxt)):
        widen(field, index, line[...], 8)
    for i, ref in ((0, front.at[0]), (1, back.at[1])):
        narrow = lambda t, ref=ref: ref[:, t * LANES : (t + 1) * LANES]
        shift = shear[me * slices + i * (slices - 1)]
        shade_slice(field, moved_v, moved_s, 1 + 3 * i, shift, i, 0, narrow)

    def column(first, count):
        rate = rates(absorb, footprint, first, count)
        state = fresh(count)
        for step in range(2):
            i = jnp.where(flip, 1 - step, step)
            shift = shear[me * slices + i * (slices - 1)]
            state = blend(state, moved_v, moved_s, i, shift, first, count, rate)
            if step == 0:
                for j in range(count):
                    at = pl.ds(pl.multiple_of((first + j) * LANES, LANES), LANES)
                    clear, total, colours = state[j]
                    colours = [colours[c] + clear * mid[c, :, at] for c in range(3)]
                    state[j] = (clear * mid[3, :, at], total, colours)
        return state

    over_columns(outs, me, inner, column)


def full_kernel(absorb, inner, strip_of, strips, shear, footprint, vol, up, down, prev, nxt, *refs):
    edges, outs, (field, moved_v, moved_s) = refs[: -3 - inner], refs[-3 - inner : -3], refs[-3:]
    slices = vol.shape[0]
    me = lax.axis_index("depth")
    flip = shear[0] > shear[shear.shape[0] - 1]
    clear_edges(moved_v, moved_s)
    centre = [(s + 1, s, s) for s in range(slices)]
    set_edges(field, centre, strip_of(pl.program_id(0)), strips, up, down, edges)

    def widen_step(s, carry):
        widen(field, s + 1, vol[s], 8)
        return carry

    lax.fori_loop(0, slices, widen_step, 0)
    widen(field, 0, prev[...], 8)
    widen(field, slices + 1, nxt[...], 8)

    def shade_step(i, carry):
        narrow = lambda t: vol[i, :, t * LANES : (t + 1) * LANES]
        shade_slice(field, moved_v, moved_s, i + 1, shear[me * slices + i], i, 0, narrow)
        return carry

    lax.fori_loop(0, slices, shade_step, 0)

    def column(first, count):
        rate = rates(absorb, footprint, first, count)
        state = fresh(count)
        for step in range(slices):
            i = jnp.where(flip, slices - 1 - step, step)
            shift = shear[me * slices + i]
            state = blend(state, moved_v, moved_s, i, shift, first, count, rate)
        return state

    over_columns(outs, me, inner, column)


def encode(x):
    x = jnp.maximum(x, 1e-30)
    code = (x * lax.rsqrt(x) * 65535.0 + 0.5).astype(jnp.int32) - 32768
    return code.astype(LINK)


def decode(code):
    root = (code.astype(jnp.int32) + 32768).astype(jnp.float32) * (1.0 / 65535.0)
    return root * root


def over(pieces):
    image = pieces[0]
    for piece in pieces[1:]:
        clear = 1.0 - image[3]
        image = [image[c] + clear * piece[c] for c in range(4)]
    return image


def ordered(count, mine, flip, body):
    cases = {}
    for position in range(count):
        for turned in (False, True):
            order = tuple((position - p) % count for p in range(count))
            cases.setdefault(order[::-1] if turned else order, []).append((position, turned))
    for order, where in cases.items():
        chosen = functools.reduce(
            jnp.logical_or, [(mine == position) & (flip == turned) for position, turned in where]
        )
        pl.when(chosen)(functools.partial(body, order))


def group_kernel(inner, shear, *refs):
    sources, outs = refs[:inner], refs[inner:]
    me = lax.axis_index("depth")
    flip = shear[0] > shear[shear.shape[0] - 1]
    groups = len(outs)

    def body(order):
        for k in range(groups):
            target = lax.rem(lax.div(me, inner) + k, groups)
            pieces = [
                [sources[shift][target, c].astype(jnp.float32) for c in range(4)]
                for shift in order
            ]
            for c, value in enumerate(over(pieces)):
                outs[k][c] = encode(value)

    ordered(inner, lax.rem(me, inner), flip, body)


def frame_kernel(inner, aliased, shear, *refs):
    sources, out = refs[:-1], refs[-1]
    if aliased:
        sources = sources[:-1]
    me = lax.axis_index("depth")
    flip = shear[0] > shear[shear.shape[0] - 1]

    def body(order):
        pieces = [[decode(sources[shift][c]) for c in range(4)] for shift in order]
        for c, value in enumerate(over(pieces)):
            out[c] = value

    ordered(len(sources), lax.div(me, inner), flip, body)


def shards(volume, shear, footprint):
    slices, rows, ny = volume.shape
    bricks = lax.axis_size("depth")
    crosswise = lax.axis_size("tile")
    absorb = 2.0 / (slices * bricks)
    inner = 1
    while 4 * inner * inner <= bricks:
        inner *= 2
    groups = bricks // inner
    width = ny // bricks
    tiles = ny // LANES
    strips = rows // ROWS

    def line(length):
        return [(i, i + 1) for i in range(length - 1)], [(i + 1, i) for i in range(length - 1)]

    depth_up, depth_down = line(bricks)
    row_up, row_down = line(crosswise)

    parts = [(1, strips - 2)] if strips > 2 else []
    parts += [(s, 1) for s in sorted({0, strips - 1})]

    prev = lax.ppermute(volume[slices - 1], "depth", depth_up)
    nxt = lax.ppermute(volume[0], "depth", depth_down)
    above = lax.ppermute(volume[:, rows - 1, :], "tile", row_up)
    below = lax.ppermute(volume[:, 0, :], "tile", row_down)

    vmem = pl.BlockSpec(memory_space=pltpu.VMEM)
    smem = pl.BlockSpec(memory_space=pltpu.SMEM)
    anywhere = pl.BlockSpec(memory_space=pl.ANY)
    moved = lambda n: pltpu.VMEM((n, tiles + 2, ROWS, LANES), jnp.float32)
    field = lambda n: pltpu.VMEM((n, tiles, ROWS + 20, LANES), jnp.float32)
    received = []
    for part in parts:
        first, count = part
        chunk = count * ROWS
        strip_of = lambda i, first=first: first + i
        flat = pl.BlockSpec((ROWS, ny), lambda i, first=first: (first + i, 0))
        edges = [above, below] if first == 0 or first + count == strips else []

        def slab(size, s, move=0, strip_of=strip_of):
            if move == 0:
                return pl.BlockSpec((size, ROWS, ny), lambda i: (s, strip_of(i), 0))
            offset = -1 if move < 0 else ROWS // 8

            def index(i):
                return s, jnp.clip(strip_of(i) * (ROWS // 8) + offset, 0, rows // 8 - 1), 0

            return pl.BlockSpec((size, 8, ny), index)

        def cost(per, chunk=chunk):
            return pl.CostEstimate(
                flops=per * chunk * ny, bytes_accessed=chunk * ny * 32, transcendentals=0
            )

        side_shape = [jax.ShapeDtypeStruct((groups, 4, chunk, width), jnp.bfloat16)] * inner
        side_spec = [pl.BlockSpec((groups, 4, ROWS, width), lambda i: (0, 0, i, 0))] * inner
        whole = [slab(slices, 0), slab(slices, 0, -1), slab(slices, 0, 1)]
        if not edges:
            middle = pl.BlockSpec((4, ROWS, ny), lambda i: (0, i, 0))
            mid = pl.pallas_call(
                functools.partial(inner_kernel, absorb, strip_of, strips),
                out_shape=jax.ShapeDtypeStruct((4, chunk, ny), jnp.float32),
                grid=(count,),
                in_specs=[smem, smem] + whole + [vmem] * len(edges),
                out_specs=middle,
                scratch_shapes=[field(slices), moved(slices - 2), moved(slices - 2)],
                cost_estimate=cost(800),
                compiler_params=params(INNER_MIB),
                name="inner",
            )(shear, footprint, *[volume] * 3, *edges)
            sides = pl.pallas_call(
                functools.partial(outer_kernel, absorb, inner, strip_of, strips),
                out_shape=side_shape,
                grid=(count,),
                in_specs=[smem, smem, slab(2, 0), slab(2, slices // 2 - 1)]
                + [slab(1, 0, -1), slab(1, 0, 1), slab(1, slices - 1, -1), slab(1, slices - 1, 1)]
                + [flat, flat, middle]
                + [vmem] * len(edges),
                out_specs=side_spec,
                scratch_shapes=[field(6), moved(2), moved(2)],
                cost_estimate=cost(400),
                compiler_params=params(OUTER_MIB),
                name="outer",
            )(shear, footprint, *[volume] * 6, prev, nxt, mid, *edges)
        else:
            sides = pl.pallas_call(
                functools.partial(full_kernel, absorb, inner, strip_of, strips),
                out_shape=side_shape,
                grid=(count,),
                in_specs=[smem, smem] + whole + [flat, flat] + [vmem] * len(edges),
                out_specs=side_spec,
                scratch_shapes=[field(slices + 2), moved(slices), moved(slices)],
                cost_estimate=cost(1100),
                compiler_params=params(OUTER_MIB),
                name="full",
            )(shear, footprint, *[volume] * 3, prev, nxt, *edges)
        sides = list(sides)
        for k in range(1, inner):
            pairs = [
                (g * inner + x, g * inner + (x + k) % inner)
                for g in range(groups)
                for x in range(inner)
            ]
            sides[k] = lax.ppermute(sides[k], "depth", pairs)
        received.append(sides)

    frame = None
    for (first, count), sides in zip(parts, received):
        chunk = count * ROWS
        pieces = pl.pallas_call(
            functools.partial(group_kernel, inner),
            out_shape=[jax.ShapeDtypeStruct((4, chunk, width), LINK)] * groups,
            grid=(count,),
            in_specs=[smem]
            + [pl.BlockSpec((groups, 4, ROWS, width), lambda i: (0, 0, i, 0))] * inner,
            out_specs=[pl.BlockSpec((4, ROWS, width), lambda i: (0, i, 0))] * groups,
            cost_estimate=pl.CostEstimate(
                flops=20 * chunk * ny, bytes_accessed=2 << 20, transcendentals=0
            ),
            compiler_params=params(16),
            name="group",
        )(shear, *sides)
        pieces = list(pieces)
        for k in range(1, groups):
            pairs = [
                (g * inner + x, (g + k) % groups * inner + x)
                for g in range(groups)
                for x in range(inner)
            ]
            pieces[k] = lax.ppermute(pieces[k], "depth", pairs)
        frame = pl.pallas_call(
            functools.partial(frame_kernel, inner, frame is not None),
            out_shape=jax.ShapeDtypeStruct((4, rows, width), jnp.float32),
            grid=(count,),
            in_specs=[smem]
            + [pl.BlockSpec((4, ROWS, width), lambda i: (0, i, 0))] * groups
            + [anywhere] * (frame is not None),
            out_specs=pl.BlockSpec(
                (4, ROWS, width), lambda i, first=first: (0, first + i, 0)
            ),
            input_output_aliases={} if frame is None else {1 + groups: 0},
            cost_estimate=pl.CostEstimate(
                flops=20 * chunk * width, bytes_accessed=2 << 20, transcendentals=0
            ),
            compiler_params=params(16),
            name="frame",
        )(shear, *pieces, *([] if frame is None else [frame]))
    return frame


def solution(mesh):
    placed = (P("depth", "tile", None), P(), P("depth", None))
    return jax.shard_map(
        shards, mesh=mesh, in_specs=placed, out_specs=P(None, "tile", "depth"), check_vma=False
    )
```

profile of v0, /device:TPU:1, one launch (start us, length us, event | category | flops | bytes accessed | tf_op | source)
XLA Modules:
  0.0 88.2 jit_solution(17777806296680852542)
XLA Ops:
  0.0 1.3 %slice_bitcast_fusion = (bf16[64,4096]{1,0:T(8,128)(2,1)S(1)}, bf16[64,4096]{1,0:T(8,128)(2,1)S(1)}) fusion(bf16[8,64,4096]{2,1,0:T(8,128)(2,1)} %refs_5_.1), kind=kLoop, calls=%fused_computation | loop fusion | bytes 2097152 | tf_op jit(solution)/shard_map/squeeze | solution.py:352
  1.3 4.0 %collective-permute-start = (bf16[64,4096]{1,0:T(8,128)(2,1)S(1)}, bf16[64,4096]{1,0:T(8,128)(2,1)S(1)}, u32[]{:S(2)}, u32[]{:S(2)}) collective-permute-start(bf16[64,4096]{1,0:T(8,128)(2,1)S(1)} %get-tuple-element.44), channel_id=1, source_target_pairs={{0,4},{4,8},{8,12},{12,16},{16,20},{20,24},{24,28},{1,5},{5,9},{9,... | collective-permute-start | bytes 1572872 | tf_op jit(solution)/shard_map/ppermute | solution.py:351
  5.2 0.0 copy-start
  5.3 1.6 %collective-permute-start.1 = (bf16[64,4096]{1,0:T(8,128)(2,1)S(1)}, bf16[64,4096]{1,0:T(8,128)(2,1)S(1)}, u32[]{:S(2)}, u32[]{:S(2)}) collective-permute-start(bf16[64,4096]{1,0:T(8,128)(2,1)S(1)} %get-tuple-element.43), channel_id=1, source_target_pairs={{4,0},{8,4},{12,8},{16,12},{20,16},{24,20},{28,24},{5,1},{9,5},{13... | collective-permute-start | bytes 1572872 | tf_op jit(solution)/shard_map/ppermute | solution.py:352
  6.8 0.0 copy-start.1
  6.8 0.6 copy-done.1
  7.5 0.7 copy-done.2
  8.1 10.2 %inner.1.refs_8_ = f32[4,32,4096]{2,1,0:T(8,128)S(1)} custom-call(s32[64]{0:T(128)S(1)} %copy-done.1, s32[1,2]{1,0:T(1,128)S(1)} %copy-done.2, bf16[8,64,4096]{2,1,0:T(8,128)(2,1)} %refs_5_.1, bf16[8,64,4096]{2,1,0:T(8,128)(2,1)} %refs_5_.1, bf16[8,64,4096]{2,1,0:T(8,128)(2,1)} %refs_5_.1), custom_call_target="tpu_custom_call" | custom-call | flops 104857600 | bytes 4194304 | tf_op jit(solution)/shard_map/inner/pallas_call | solution.py:389
  18.4 8.7 %collective-permute-done.prev.refs_6_ = bf16[64,4096]{1,0:T(8,128)(2,1)S(1)} collective-permute-done((bf16[64,4096]{1,0:T(8,128)(2,1)S(1)}, bf16[64,4096]{1,0:T(8,128)(2,1)S(1)}, u32[]{:S(2)}, u32[]{:S(2)}) %collective-permute-start) | collective-permute-done | bytes 524320 | tf_op jit(solution)/shard_map/ppermute | solution.py:351
  27.0 0.0 collective-permute-done.1.nxt.refs_7_
  27.0 4.2 %outer.1 = (bf16[4,4,32,512]{3,2,1,0:T(8,128)(2,1)S(1)}, bf16[4,4,32,512]{3,2,1,0:T(8,128)(2,1)S(1)}) custom-call(s32[64]{0:T(128)S(1)} %copy-done.1, s32[1,2]{1,0:T(1,128)S(1)} %copy-done.2, bf16[8,64,4096]{2,1,0:T(8,128)(2,1)S(1)} %copy-done, bf16[8,64,4096]{2,1,0:T(8,128)(2,1)S(1)} %copy-done, bf16[8,64,4096]{2,1,0:T(8,128)(2,1)S(1)} %copy-done, ...), custom_call_target="tpu_custom_call" | custom-call | flops 52428800 | bytes 4194304 | tf_op jit(solution)/shard_map/outer/pallas_call | solution.py:400
  31.3 2.3 %collective-permute-start.12 = (bf16[4,4,32,512]{3,2,1,0:T(8,128)(2,1)S(1)}, bf16[4,4,32,512]{3,2,1,0:T(8,128)(2,1)S(1)}, u32[]{:S(2)}, u32[]{:S(2)}) collective-permute-start(bf16[4,4,32,512]{3,2,1,0:T(8,128)(2,1)S(1)} %get-tuple-element.36), channel_id=1, source_target_pairs={{0,4},{4,0},{8,12},{12,8},{16,20},{20,16},{24,28},{28,24},{1,5},{5... | collective-permute-start | bytes 1572872 | tf_op jit(solution)/shard_map/ppermute | solution.py:433
  33.6 0.3 fusion
  33.8 0.1 copy.13
  33.9 4.8 %collective-permute-start.2 = (bf16[8,4096]{1,0:T(8,128)(2,1)S(1)}, bf16[8,4096]{1,0:T(8,128)(2,1)S(1)}, u32[]{:S(2)}, u32[]{:S(2)}) collective-permute-start(bf16[8,4096]{1,0:T(8,128)(2,1)S(1)} %bitcast.10), channel_id=1, source_target_pairs={{0,1},{1,2},{2,3},{4,5},{5,6},{6,7},{8,9},{9,10},{10,11},{12,13},{... | collective-permute-start | bytes 196616 | tf_op jit(solution)/shard_map/ppermute | solution.py:353
  38.8 0.1 copy.12
  38.8 1.9 %collective-permute-start.3 = (bf16[8,4096]{1,0:T(8,128)(2,1)S(1)}, bf16[8,4096]{1,0:T(8,128)(2,1)S(1)}, u32[]{:S(2)}, u32[]{:S(2)}) collective-permute-start(bf16[8,4096]{1,0:T(8,128)(2,1)S(1)} %bitcast.11), channel_id=1, source_target_pairs={{1,0},{2,1},{3,2},{5,4},{6,5},{7,6},{9,8},{10,9},{11,10},{13,12},{... | collective-permute-start | bytes 196616 | tf_op jit(solution)/shard_map/ppermute | solution.py:354
  40.8 0.0 collective-permute-done.2.refs_0_
  40.8 3.9 %collective-permute-done.3.refs_1_ = bf16[8,4096]{1,0:T(8,128)(2,1)S(1)} collective-permute-done((bf16[8,4096]{1,0:T(8,128)(2,1)S(1)}, bf16[8,4096]{1,0:T(8,128)(2,1)S(1)}, u32[]{:S(2)}, u32[]{:S(2)}) %collective-permute-start.3) | collective-permute-done | bytes 65568 | tf_op jit(solution)/shard_map/ppermute | solution.py:354
  44.7 6.2 %full.3 = (bf16[4,4,16,512]{3,2,1,0:T(8,128)(2,1)S(1)}, bf16[4,4,16,512]{3,2,1,0:T(8,128)(2,1)S(1)}) custom-call(s32[64]{0:T(128)S(1)} %copy-done.1, s32[1,2]{1,0:T(1,128)S(1)} %copy-done.2, bf16[8,64,4096]{2,1,0:T(8,128)(2,1)S(1)} %copy-done, bf16[8,64,4096]{2,1,0:T(8,128)(2,1)S(1)} %copy-done, bf16[8,64,4096]{2,1,0:T(8,128)(2,1)S(1)} %copy-done, ...), custom_call_target="tpu_custom_call" | custom-call | flops 72089600 | bytes 2097152 | tf_op jit(solution)/shard_map/full/pallas_call | solution.py:415
  50.9 0.1 collective-permute-start.8
  51.0 6.2 %full.2 = (bf16[4,4,16,512]{3,2,1,0:T(8,128)(2,1)S(1)}, bf16[4,4,16,512]{3,2,1,0:T(8,128)(2,1)S(1)}) custom-call(s32[64]{0:T(128)S(1)} %copy-done.1, s32[1,2]{1,0:T(1,128)S(1)} %copy-done.2, bf16[8,64,4096]{2,1,0:T(8,128)(2,1)S(1)} %copy-done, bf16[8,64,4096]{2,1,0:T(8,128)(2,1)S(1)} %copy-done, bf16[8,64,4096]{2,1,0:T(8,128)(2,1)S(1)} %copy-done, ...), custom_call_target="tpu_custom_call" | custom-call | flops 72089600 | bytes 2097152 | tf_op jit(solution)/shard_map/full/pallas_call | solution.py:415
  57.2 1.5 %collective-permute-start.4 = (bf16[4,4,16,512]{3,2,1,0:T(8,128)(2,1)S(1)}, bf16[4,4,16,512]{3,2,1,0:T(8,128)(2,1)S(1)}, u32[]{:S(2)}, u32[]{:S(2)}) collective-permute-start(bf16[4,4,16,512]{3,2,1,0:T(8,128)(2,1)S(1)} %get-tuple-element.24), channel_id=1, source_target_pairs={{0,4},{4,0},{8,12},{12,8},{16,20},{20,16},{24,28},{28,24},{1,5},{5... | collective-permute-start | bytes 786440 | tf_op jit(solution)/shard_map/ppermute | solution.py:433
  58.7 0.0 collective-permute-done.12.refs_1_
  58.7 1.2 %group.5 = (s16[4,32,512]{2,1,0:T(8,128)(2,1)S(1)}, s16[4,32,512]{2,1,0:T(8,128)(2,1)S(1)}, s16[4,32,512]{2,1,0:T(8,128)(2,1)S(1)}, s16[4,32,512]{2,1,0:T(8,128)(2,1)S(1)}) custom-call(s32[64]{0:T(128)S(1)} %copy-done.1, bf16[4,4,32,512]{3,2,1,0:T(8,128)(2,1)S(1)} %get-tuple-element.35.refs_0_, bf16[4,4,32,512]{3,2,1,0:T(8,128)(2,1)S(1)} %collective-permute-done.12.refs_1_), custom_call_target="tpu_custom_call" | custom-call | flops 2621440 | bytes 2097152 | tf_op jit(solution)/shard_map/group/pallas_call | solution.py:439
  59.9 1.3 %collective-permute-start.13 = (s16[4,32,512]{2,1,0:T(8,128)(2,1)S(1)}, s16[4,32,512]{2,1,0:T(8,128)(2,1)S(1)}, u32[]{:S(2)}, u32[]{:S(2)}) collective-permute-start(s16[4,32,512]{2,1,0:T(8,128)(2,1)S(1)} %get-tuple-element.38), channel_id=1, source_target_pairs={{0,8},{4,12},{8,16},{12,20},{16,24},{20,28},{24,0},{28,4},{1,9},{5... | collective-permute-start | bytes 393224 | tf_op jit(solution)/shard_map/ppermute | solution.py:459
  61.3 2.0 %collective-permute-start.14 = (s16[4,32,512]{2,1,0:T(8,128)(2,1)S(1)}, s16[4,32,512]{2,1,0:T(8,128)(2,1)S(1)}, u32[]{:S(2)}, u32[]{:S(2)}) collective-permute-start(s16[4,32,512]{2,1,0:T(8,128)(2,1)S(1)} %get-tuple-element.39), channel_id=1, source_target_pairs={{0,16},{4,20},{8,24},{12,28},{16,0},{20,4},{24,8},{28,12},{1,17},{... | collective-permute-start | bytes 393224 | tf_op jit(solution)/shard_map/ppermute | solution.py:459
  63.3 1.3 %collective-permute-start.15 = (s16[4,32,512]{2,1,0:T(8,128)(2,1)S(1)}, s16[4,32,512]{2,1,0:T(8,128)(2,1)S(1)}, u32[]{:S(2)}, u32[]{:S(2)}) collective-permute-start(s16[4,32,512]{2,1,0:T(8,128)(2,1)S(1)} %get-tuple-element.40), channel_id=1, source_target_pairs={{0,24},{4,28},{8,0},{12,4},{16,8},{20,12},{24,16},{28,20},{1,25},{... | collective-permute-start | bytes 393224 | tf_op jit(solution)/shard_map/ppermute | solution.py:459
  64.6 0.0 collective-permute-done.8.refs_1_
  64.7 0.8 group.4
  65.4 0.1 collective-permute-start.10
  65.6 0.0 collective-permute-done.4.refs_1_
  65.6 2.5 %collective-permute-start.11 = (s16[4,16,512]{2,1,0:T(8,128)(2,1)S(1)}, s16[4,16,512]{2,1,0:T(8,128)(2,1)S(1)}, u32[]{:S(2)}, u32[]{:S(2)}) collective-permute-start(s16[4,16,512]{2,1,0:T(8,128)(2,1)S(1)} %get-tuple-element.34), channel_id=1, source_target_pairs={{0,24},{4,28},{8,0},{12,4},{16,8},{20,12},{24,16},{28,20},{1,25},{... | collective-permute-start | bytes 196616 | tf_op jit(solution)/shard_map/ppermute | solution.py:459
  68.1 0.8 group.3
  68.9 7.9 %collective-permute-done.10.refs_2_ = s16[4,16,512]{2,1,0:T(8,128)(2,1)S(1)} collective-permute-done((s16[4,16,512]{2,1,0:T(8,128)(2,1)S(1)}, s16[4,16,512]{2,1,0:T(8,128)(2,1)S(1)}, u32[]{:S(2)}, u32[]{:S(2)}) %collective-permute-start.10) | collective-permute-done | bytes 65568 | tf_op jit(solution)/shard_map/ppermute | solution.py:459
  76.8 0.0 collective-permute-start.9
  76.8 0.0 collective-permute-start.5
  76.8 0.0 collective-permute-done.14.refs_2_
  76.8 3.5 %collective-permute-start.6 = (s16[4,16,512]{2,1,0:T(8,128)(2,1)S(1)}, s16[4,16,512]{2,1,0:T(8,128)(2,1)S(1)}, u32[]{:S(2)}, u32[]{:S(2)}) collective-permute-start(s16[4,16,512]{2,1,0:T(8,128)(2,1)S(1)} %get-tuple-element.27), channel_id=1, source_target_pairs={{0,16},{4,20},{8,24},{12,28},{16,0},{20,4},{24,8},{28,12},{1,17},{... | collective-permute-start | bytes 196616 | tf_op jit(solution)/shard_map/ppermute | solution.py:459
  80.4 0.0 collective-permute-done.15.refs_3_
  80.4 1.6 %collective-permute-start.7 = (s16[4,16,512]{2,1,0:T(8,128)(2,1)S(1)}, s16[4,16,512]{2,1,0:T(8,128)(2,1)S(1)}, u32[]{:S(2)}, u32[]{:S(2)}) collective-permute-start(s16[4,16,512]{2,1,0:T(8,128)(2,1)S(1)} %get-tuple-element.28), channel_id=1, source_target_pairs={{0,24},{4,28},{8,0},{12,4},{16,8},{20,12},{24,16},{28,20},{1,25},{... | collective-permute-start | bytes 196616 | tf_op jit(solution)/shard_map/ppermute | solution.py:459
  82.0 1.6 %frame.3.refs_4_ = f32[4,64,512]{2,1,0:T(8,128)} custom-call(s32[64]{0:T(128)S(1)} %copy-done.1, s16[4,32,512]{2,1,0:T(8,128)(2,1)S(1)} %get-tuple-element.37.refs_0_, s16[4,32,512]{2,1,0:T(8,128)(2,1)S(1)} %collective-permute-done.13.refs_1_, s16[4,32,512]{2,1,0:T(8,128)(2,1)S(1)} %collective-permute-done.14.refs_2_, ...), custom_call_target="tpu_custom_call" | custom-call | flops 327680 | bytes 2097152 | tf_op jit(solution)/shard_map/frame/pallas_call | solution.py:460
  83.6 0.0 collective-permute-done.9.refs_1_
  83.6 1.4 %frame.4.refs_4_ = f32[4,64,512]{2,1,0:T(8,128)} custom-call(s32[64]{0:T(128)S(1)} %copy-done.1, s16[4,16,512]{2,1,0:T(8,128)(2,1)S(1)} %get-tuple-element.31.refs_0_, s16[4,16,512]{2,1,0:T(8,128)(2,1)S(1)} %collective-permute-done.9.refs_1_, s16[4,16,512]{2,1,0:T(8,128)(2,1)S(1)} %collective-permute-done.10.refs_2_, ...), custom_call_target="tpu_custom_call", output_to_operand_aliasing={{}: (5, {})} | custom-call | flops 163840 | bytes 2097152 | tf_op jit(solution)/shard_map/frame/pallas_call | solution.py:460
  85.0 0.0 collective-permute-done.5.refs_1_
  85.0 1.9 %collective-permute-done.6.refs_2_ = s16[4,16,512]{2,1,0:T(8,128)(2,1)S(1)} collective-permute-done((s16[4,16,512]{2,1,0:T(8,128)(2,1)S(1)}, s16[4,16,512]{2,1,0:T(8,128)(2,1)S(1)}, u32[]{:S(2)}, u32[]{:S(2)}) %collective-permute-start.6) | collective-permute-done | bytes 65568 | tf_op jit(solution)/shard_map/ppermute | solution.py:459
  86.9 0.0 collective-permute-done.7.refs_3_
  86.9 1.4 %frame.5 = f32[4,64,512]{2,1,0:T(8,128)} custom-call(s32[64]{0:T(128)S(1)} %copy-done.1, s16[4,16,512]{2,1,0:T(8,128)(2,1)S(1)} %get-tuple-element.25.refs_0_, s16[4,16,512]{2,1,0:T(8,128)(2,1)S(1)} %collective-permute-done.5.refs_1_, s16[4,16,512]{2,1,0:T(8,128)(2,1)S(1)} %collective-permute-done.6.refs_2_, ...), custom_call_target="tpu_custom_call", output_to_operand_aliasing={{}: (5, {})} | custom-call | flops 163840 | bytes 2097152 | tf_op jit(solution)/shard_map/frame/pallas_call | solution.py:460
  (4 shorter events, 0.0 us)
Async XLA Ops:
  1.3 25.8 %collective-permute-start = (bf16[64,4096]{1,0:T(8,128)(2,1)S(1)}, bf16[64,4096]{1,0:T(8,128)(2,1)S(1)}, u32[]{:S(2)}, u32[]{:S(2)}) collective-permute-start(bf16[64,4096]{1,0:T(8,128)(2,1)S(1)} %get-tuple-element.44), channel_id=1, source_target_pairs={{0,4},{4,8},{8,12},{12,16},{16,20},{20,24},{24,28},{1,5},{5,9},{9,... | collective-permute-start | bytes 1572872 | tf_op jit(solution)/shard_map/ppermute | solution.py:351
  5.2 21.8 %copy-start = (bf16[8,64,4096]{2,1,0:T(8,128)(2,1)S(1)}, bf16[8,64,4096]{2,1,0:T(8,128)(2,1)}, u32[]{:S(2)}) copy-start(bf16[8,64,4096]{2,1,0:T(8,128)(2,1)} %refs_5_.1) | copy-start | bytes 12582916
  5.3 21.8 %collective-permute-start.1 = (bf16[64,4096]{1,0:T(8,128)(2,1)S(1)}, bf16[64,4096]{1,0:T(8,128)(2,1)S(1)}, u32[]{:S(2)}, u32[]{:S(2)}) collective-permute-start(bf16[64,4096]{1,0:T(8,128)(2,1)S(1)} %get-tuple-element.43), channel_id=1, source_target_pairs={{4,0},{8,4},{12,8},{16,12},{20,16},{24,20},{28,24},{5,1},{9,5},{13... | collective-permute-start | bytes 1572872 | tf_op jit(solution)/shard_map/ppermute | solution.py:352
  6.8 0.7 copy-start.1
  7.5 0.7 copy-start.2
  31.3 27.4 %collective-permute-start.12 = (bf16[4,4,32,512]{3,2,1,0:T(8,128)(2,1)S(1)}, bf16[4,4,32,512]{3,2,1,0:T(8,128)(2,1)S(1)}, u32[]{:S(2)}, u32[]{:S(2)}) collective-permute-start(bf16[4,4,32,512]{3,2,1,0:T(8,128)(2,1)S(1)} %get-tuple-element.36), channel_id=1, source_target_pairs={{0,4},{4,0},{8,12},{12,8},{16,20},{20,16},{24,28},{28,24},{1,5},{5... | collective-permute-start | bytes 1572872 | tf_op jit(solution)/shard_map/ppermute | solution.py:433
  33.9 6.9 %collective-permute-start.2 = (bf16[8,4096]{1,0:T(8,128)(2,1)S(1)}, bf16[8,4096]{1,0:T(8,128)(2,1)S(1)}, u32[]{:S(2)}, u32[]{:S(2)}) collective-permute-start(bf16[8,4096]{1,0:T(8,128)(2,1)S(1)} %bitcast.10), channel_id=1, source_target_pairs={{0,1},{1,2},{2,3},{4,5},{5,6},{6,7},{8,9},{9,10},{10,11},{12,13},{... | collective-permute-start | bytes 196616 | tf_op jit(solution)/shard_map/ppermute | solution.py:353
  38.8 5.9 %collective-permute-start.3 = (bf16[8,4096]{1,0:T(8,128)(2,1)S(1)}, bf16[8,4096]{1,0:T(8,128)(2,1)S(1)}, u32[]{:S(2)}, u32[]{:S(2)}) collective-permute-start(bf16[8,4096]{1,0:T(8,128)(2,1)S(1)} %bitcast.11), channel_id=1, source_target_pairs={{1,0},{2,1},{3,2},{5,4},{6,5},{7,6},{9,8},{10,9},{11,10},{13,12},{... | collective-permute-start | bytes 196616 | tf_op jit(solution)/shard_map/ppermute | solution.py:354
  50.9 13.7 %collective-permute-start.8 = (bf16[4,4,16,512]{3,2,1,0:T(8,128)(2,1)S(1)}, bf16[4,4,16,512]{3,2,1,0:T(8,128)(2,1)S(1)}, u32[]{:S(2)}, u32[]{:S(2)}) collective-permute-start(bf16[4,4,16,512]{3,2,1,0:T(8,128)(2,1)S(1)} %get-tuple-element.30), channel_id=1, source_target_pairs={{0,4},{4,0},{8,12},{12,8},{16,20},{20,16},{24,28},{28,24},{1,5},{5... | collective-permute-start | bytes 786440 | tf_op jit(solution)/shard_map/ppermute | solution.py:433
  57.2 8.4 %collective-permute-start.4 = (bf16[4,4,16,512]{3,2,1,0:T(8,128)(2,1)S(1)}, bf16[4,4,16,512]{3,2,1,0:T(8,128)(2,1)S(1)}, u32[]{:S(2)}, u32[]{:S(2)}) collective-permute-start(bf16[4,4,16,512]{3,2,1,0:T(8,128)(2,1)S(1)} %get-tuple-element.24), channel_id=1, source_target_pairs={{0,4},{4,0},{8,12},{12,8},{16,20},{20,16},{24,28},{28,24},{1,5},{5... | collective-permute-start | bytes 786440 | tf_op jit(solution)/shard_map/ppermute | solution.py:433
  59.9 16.9 %collective-permute-start.13 = (s16[4,32,512]{2,1,0:T(8,128)(2,1)S(1)}, s16[4,32,512]{2,1,0:T(8,128)(2,1)S(1)}, u32[]{:S(2)}, u32[]{:S(2)}) collective-permute-start(s16[4,32,512]{2,1,0:T(8,128)(2,1)S(1)} %get-tuple-element.38), channel_id=1, source_target_pairs={{0,8},{4,12},{8,16},{12,20},{16,24},{20,28},{24,0},{28,4},{1,9},{5... | collective-permute-start | bytes 393224 | tf_op jit(solution)/shard_map/ppermute | solution.py:459
  61.3 15.6 %collective-permute-start.14 = (s16[4,32,512]{2,1,0:T(8,128)(2,1)S(1)}, s16[4,32,512]{2,1,0:T(8,128)(2,1)S(1)}, u32[]{:S(2)}, u32[]{:S(2)}) collective-permute-start(s16[4,32,512]{2,1,0:T(8,128)(2,1)S(1)} %get-tuple-element.39), channel_id=1, source_target_pairs={{0,16},{4,20},{8,24},{12,28},{16,0},{20,4},{24,8},{28,12},{1,17},{... | collective-permute-start | bytes 393224 | tf_op jit(solution)/shard_map/ppermute | solution.py:459
  63.3 17.1 %collective-permute-start.15 = (s16[4,32,512]{2,1,0:T(8,128)(2,1)S(1)}, s16[4,32,512]{2,1,0:T(8,128)(2,1)S(1)}, u32[]{:S(2)}, u32[]{:S(2)}) collective-permute-start(s16[4,32,512]{2,1,0:T(8,128)(2,1)S(1)} %get-tuple-element.40), channel_id=1, source_target_pairs={{0,24},{4,28},{8,0},{12,4},{16,8},{20,12},{24,16},{28,20},{1,25},{... | collective-permute-start | bytes 393224 | tf_op jit(solution)/shard_map/ppermute | solution.py:459
  65.4 11.4 %collective-permute-start.10 = (s16[4,16,512]{2,1,0:T(8,128)(2,1)S(1)}, s16[4,16,512]{2,1,0:T(8,128)(2,1)S(1)}, u32[]{:S(2)}, u32[]{:S(2)}) collective-permute-start(s16[4,16,512]{2,1,0:T(8,128)(2,1)S(1)} %get-tuple-element.33), channel_id=1, source_target_pairs={{0,16},{4,20},{8,24},{12,28},{16,0},{20,4},{24,8},{28,12},{1,17},{... | collective-permute-start | bytes 196616 | tf_op jit(solution)/shard_map/ppermute | solution.py:459
  65.6 18.0 %collective-permute-start.11 = (s16[4,16,512]{2,1,0:T(8,128)(2,1)S(1)}, s16[4,16,512]{2,1,0:T(8,128)(2,1)S(1)}, u32[]{:S(2)}, u32[]{:S(2)}) collective-permute-start(s16[4,16,512]{2,1,0:T(8,128)(2,1)S(1)} %get-tuple-element.34), channel_id=1, source_target_pairs={{0,24},{4,28},{8,0},{12,4},{16,8},{20,12},{24,16},{28,20},{1,25},{... | collective-permute-start | bytes 196616 | tf_op jit(solution)/shard_map/ppermute | solution.py:459
  76.8 6.8 %collective-permute-start.9 = (s16[4,16,512]{2,1,0:T(8,128)(2,1)S(1)}, s16[4,16,512]{2,1,0:T(8,128)(2,1)S(1)}, u32[]{:S(2)}, u32[]{:S(2)}) collective-permute-start(s16[4,16,512]{2,1,0:T(8,128)(2,1)S(1)} %get-tuple-element.32), channel_id=1, source_target_pairs={{0,8},{4,12},{8,16},{12,20},{16,24},{20,28},{24,0},{28,4},{1,9},{5... | collective-permute-start | bytes 196616 | tf_op jit(solution)/shard_map/ppermute | solution.py:459
  76.8 8.2 %collective-permute-start.5 = (s16[4,16,512]{2,1,0:T(8,128)(2,1)S(1)}, s16[4,16,512]{2,1,0:T(8,128)(2,1)S(1)}, u32[]{:S(2)}, u32[]{:S(2)}) collective-permute-start(s16[4,16,512]{2,1,0:T(8,128)(2,1)S(1)} %get-tuple-element.26), channel_id=1, source_target_pairs={{0,8},{4,12},{8,16},{12,20},{16,24},{20,28},{24,0},{28,4},{1,9},{5... | collective-permute-start | bytes 196616 | tf_op jit(solution)/shard_map/ppermute | solution.py:459
  76.8 10.0 %collective-permute-start.6 = (s16[4,16,512]{2,1,0:T(8,128)(2,1)S(1)}, s16[4,16,512]{2,1,0:T(8,128)(2,1)S(1)}, u32[]{:S(2)}, u32[]{:S(2)}) collective-permute-start(s16[4,16,512]{2,1,0:T(8,128)(2,1)S(1)} %get-tuple-element.27), channel_id=1, source_target_pairs={{0,16},{4,20},{8,24},{12,28},{16,0},{20,4},{24,8},{28,12},{1,17},{... | collective-permute-start | bytes 196616 | tf_op jit(solution)/shard_map/ppermute | solution.py:459
  80.4 6.5 %collective-permute-start.7 = (s16[4,16,512]{2,1,0:T(8,128)(2,1)S(1)}, s16[4,16,512]{2,1,0:T(8,128)(2,1)S(1)}, u32[]{:S(2)}, u32[]{:S(2)}) collective-permute-start(s16[4,16,512]{2,1,0:T(8,128)(2,1)S(1)} %get-tuple-element.28), channel_id=1, source_target_pairs={{0,24},{4,28},{8,0},{12,4},{16,8},{20,12},{24,16},{28,20},{1,25},{... | collective-permute-start | bytes 196616 | tf_op jit(solution)/shard_map/ppermute | solution.py:459
where the time goes:
time: 89 us; the launch traced here: 88.2 us
  Pallas kernels  34 us (38%)
  starting transfers between devices  28.7 us (32%)
  waiting for transfers between devices  22.4 us (25%)
  local copies, waits for them, and re-layouts  2.99 us (3%)
    ppermute x9, starting transfers between devices, shards(): pieces[k] = lax.ppermute(pieces[k], 'depth', pairs)  12.5 us
    pallas_call x2, Pallas kernels, shards(): pl.pallas_call(functools.partial(full_kernel, absorb, inner, strip_of, st...  12.4 us
    pallas_call x1, Pallas kernels, shards(): pl.pallas_call(functools.partial(inner_kernel, absorb, strip_of, strips),...  10.2 us
    ppermute x9, waiting for transfers between devices, shards(): pieces[k] = lax.ppermute(pieces[k], 'depth', pairs)  9.81 us
    ppermute x1, waiting for transfers between devices, shards(): prev = lax.ppermute(volume[slices - 1], 'depth', depth_up)  8.67 us
    ppermute x1, starting transfers between devices, shards(): above = lax.ppermute(volume[:, rows - 1, :], 'tile', row_up)  4.84 us
    pallas_call x3, Pallas kernels, shards(): pl.pallas_call(functools.partial(frame_kernel, inner, frame is not None),...  4.35 us
    pallas_call x1, Pallas kernels, shards(): pl.pallas_call(functools.partial(outer_kernel, absorb, inner, strip_of, s...  4.25 us
  transfers between devices with their start and end apart: 16, of which 4 were waited for; matrix products, arithmetic and copies ran while one was open for 0% of the time, Pallas kernels for 32%

commit v1 on v0

--- a/solution.py
+++ b/solution.py
@@ -20,35 +20,46 @@
     return pltpu.CompilerParams(vmem_limit_bytes=mib << 20)
 
 
-def shade_slice(field, moved_v, moved_s, where, shift, base, r, narrow):
-    tiles = field.shape[1]
-    lane = lax.broadcasted_iota(jnp.int32, (ROWS, LANES), 1)
-    leftmost, rightmost = lane == 0, lane == LANES - 1
+def difference(across, steps, narrow):
+    tiles = across.shape[0]
+    none = jnp.zeros((ROWS, LANES), jnp.bfloat16)
+    line = [none] + [narrow(t) for t in range(tiles)] + [none]
+    windows = [jnp.concatenate(line[t : t + 4], axis=1) for t in range(0, tiles, 2)]
+    found = jnp.dot(
+        jnp.concatenate(windows, axis=0), steps[...], preferred_element_type=jnp.float32
+    )
+    for t in range(tiles):
+        row, column = t // 2 * ROWS, t % 2 * LANES
+        across[t] = found[row : row + ROWS, column : column + LANES]
+
+
+def shade(field, moved_v, moved_s, across, where, shift, base, narrow):
     turn = jnp.where(shift < 0, shift + LANES, shift)
-    here, up, down = pl.ds(r + 8, ROWS), pl.ds(r + 7, ROWS), pl.ds(r + 9, ROWS)
-    zero = jnp.zeros((ROWS, LANES), jnp.float32)
-    v = field[where, 0, here, :]
-    ahead = pltpu.roll(v, LANES - 1, 1)
-    behind_last = zero
-    for t in range(tiles):
-        v_next = field[where, t + 1, here, :] if t + 1 < tiles else zero
-        ahead_next = pltpu.roll(v_next, LANES - 1, 1) if t + 1 < tiles else zero
-        behind = pltpu.roll(v, 1, 1)
-        dy = jnp.where(rightmost, ahead_next, ahead) - jnp.where(leftmost, behind_last, behind)
+    here, up, down = pl.ds(8, ROWS), pl.ds(7, ROWS), pl.ds(9, ROWS)
+    for t in range(field.shape[1]):
+        dy = across[t]
         dz = field[where + 1, t, here, :] - field[where - 1, t, here, :]
         dx = field[where, t, down, :] - field[where, t, up, :]
         squares = (dx * dx + dy * dy) + (dz * dz + 4.0)
         along = (0.35 * 0.48) * dx + (0.35 * 0.6) * dy + (0.35 * 0.64) * dz
-        moved_s[base, t + 1] = 0.15 + jnp.abs(along) * lax.rsqrt(squares)
-        v, ahead, behind_last = v_next, ahead_next, behind
-
-    def turn_step(once, carry):
-        for t in range(tiles):
-            moved_v[base, t + 1] = pltpu.roll(narrow(t), turn, 1).astype(jnp.float32)
-            moved_s[base, t + 1] = pltpu.roll(moved_s[base, t + 1], turn, 1)
+        half = 0.15 + jnp.abs(along) * lax.rsqrt(squares)
+        moved_s[base, t + 1] = pltpu.roll(half, turn, 1)
+        moved_v[base, t + 1] = pltpu.roll(narrow(t), turn, 1).astype(jnp.float32)
+
+
+def shade_all(field, moved_v, moved_s, across, steps, count, where, shift, narrow):
+    even, odd = across
+    difference(even, steps, narrow(0))
+
+    def pair_step(pair, carry):
+        i = 2 * pair
+        difference(odd, steps, narrow(i + 1))
+        shade(field, moved_v, moved_s, even, where(i), shift(i), i, narrow(i))
+        difference(even, steps, narrow(jnp.minimum(i + 2, count - 1)))
+        shade(field, moved_v, moved_s, odd, where(i + 1), shift(i + 1), i + 1, narrow(i + 1))
         return carry
 
-    lax.fori_loop(0, 1 + jnp.minimum(turn, 0), turn_step, 0)
+    lax.fori_loop(0, count // 2, pair_step, 0)
 
 
 def blend(state, moved_v, moved_s, index, shift, first, count, rate):
@@ -112,9 +123,13 @@
                 set_row(field, index, place, line[s : s + 1])
 
 
-def clear_edges(moved_v, moved_s):
+def prepare(moved_v, moved_s, steps):
     @pl.when(pl.program_id(0) == 0)
     def _():
+        at = lax.broadcasted_iota(jnp.int32, steps.shape, 0)
+        to = lax.broadcasted_iota(jnp.int32, steps.shape, 1) + LANES
+        ahead = jnp.where(at == to + 1, 1.0, 0.0)
+        steps[...] = jnp.where(at == to - 1, -1.0, ahead).astype(jnp.bfloat16)
         tiles = moved_v.shape[1] - 2
         zero = jnp.zeros((moved_v.shape[0], ROWS, LANES), jnp.float32)
         for t in (0, tiles + 1):
@@ -148,11 +163,11 @@
 
 
 def inner_kernel(absorb, strip_of, strips, shear, footprint, vol, up, down, *refs):
-    edges, (out, field, moved_v, moved_s) = refs[:-4], refs[-4:]
+    edges, (out, field, moved_v, moved_s, *across, steps) = refs[:-7], refs[-7:]
     slices, _, ny = vol.shape
     me = lax.axis_index("depth")
     flip = shear[0] > shear[shear.shape[0] - 1]
-    clear_edges(moved_v, moved_s)
+    prepare(moved_v, moved_s, steps)
     centre = [(s, s, s) for s in range(1, slices - 1)]
     set_edges(field, centre, strip_of(pl.program_id(0)), strips, up, down, edges)
 
@@ -162,13 +177,17 @@
 
     lax.fori_loop(0, slices, widen_step, 0)
 
-    def shade_step(i, carry):
-        narrow = lambda t: vol[i + 1, :, t * LANES : (t + 1) * LANES]
-        shift = shear[me * slices + i + 1]
-        shade_slice(field, moved_v, moved_s, i + 1, shift, i, 0, narrow)
-        return carry
-
-    lax.fori_loop(0, slices - 2, shade_step, 0)
+    shade_all(
+        field,
+        moved_v,
+        moved_s,
+        across,
+        steps,
+        slices - 2,
+        lambda i: i + 1,
+        lambda i: shear[me * slices + i + 1],
+        lambda i: lambda t: vol[i + 1, :, t * LANES : (t + 1) * LANES],
+    )
 
     def column_step(pair, carry):
         first = 2 * pair
@@ -191,20 +210,23 @@
 
 def outer_kernel(absorb, inner, strip_of, strips, shear, footprint, *refs):
     front, back, front_up, front_down, back_up, back_down, prev, nxt, mid = refs[:9]
-    edges, outs, (field, moved_v, moved_s) = refs[9 : -3 - inner], refs[-3 - inner : -3], refs[-3:]
+    edges, outs, (field, moved_v, moved_s, *across, steps) = refs[9 : -6 - inner], refs[-6 - inner : -6], refs[-6:]
     me = lax.axis_index("depth")
     flip = shear[0] > shear[shear.shape[0] - 1]
     slices = shear.shape[0] // lax.axis_size("depth")
     strip = strip_of(pl.program_id(0))
-    clear_edges(moved_v, moved_s)
+    prepare(moved_v, moved_s, steps)
     set_edges(field, [(1, 0, 0)], strip, strips, front_up, front_down, edges)
     set_edges(field, [(4, 0, slices - 1)], strip, strips, back_up, back_down, edges)
     for index, line in enumerate((prev, front.at[0], front.at[1], back.at[0], back.at[1], nxt)):
         widen(field, index, line[...], 8)
-    for i, ref in ((0, front.at[0]), (1, back.at[1])):
-        narrow = lambda t, ref=ref: ref[:, t * LANES : (t + 1) * LANES]
+    ends = [front.at[0], back.at[1]]
+    narrow = lambda i: lambda t: ends[i][:, t * LANES : (t + 1) * LANES]
+    for i in range(2):
+        difference(across[i], steps, narrow(i))
+    for i in range(2):
         shift = shear[me * slices + i * (slices - 1)]
-        shade_slice(field, moved_v, moved_s, 1 + 3 * i, shift, i, 0, narrow)
+        shade(field, moved_v, moved_s, across[i], 1 + 3 * i, shift, i, narrow(i))
 
     def column(first, count):
         rate = rates(absorb, footprint, first, count)
@@ -224,42 +246,6 @@
     over_columns(outs, me, inner, column)
 
 
-def full_kernel(absorb, inner, strip_of, strips, shear, footprint, vol, up, down, prev, nxt, *refs):
-    edges, outs, (field, moved_v, moved_s) = refs[: -3 - inner], refs[-3 - inner : -3], refs[-3:]
-    slices = vol.shape[0]
-    me = lax.axis_index("depth")
-    flip = shear[0] > shear[shear.shape[0] - 1]
-    clear_edges(moved_v, moved_s)
-    centre = [(s + 1, s, s) for s in range(slices)]
-    set_edges(field, centre, strip_of(pl.program_id(0)), strips, up, down, edges)
-
-    def widen_step(s, carry):
-        widen(field, s + 1, vol[s], 8)
-        return carry
-
-    lax.fori_loop(0, slices, widen_step, 0)
-    widen(field, 0, prev[...], 8)
-    widen(field, slices + 1, nxt[...], 8)
-
-    def shade_step(i, carry):
-        narrow = lambda t: vol[i, :, t * LANES : (t + 1) * LANES]
-        shade_slice(field, moved_v, moved_s, i + 1, shear[me * slices + i], i, 0, narrow)
-        return carry
-
-    lax.fori_loop(0, slices, shade_step, 0)
-
-    def column(first, count):
-        rate = rates(absorb, footprint, first, count)
-        state = fresh(count)
-        for step in range(slices):
-            i = jnp.where(flip, slices - 1 - step, step)
-            shift = shear[me * slices + i]
-            state = blend(state, moved_v, moved_s, i, shift, first, count, rate)
-        return state
-
-    over_columns(outs, me, inner, column)
-
-
 def encode(x):
     x = jnp.maximum(x, 1e-30)
     code = (x * lax.rsqrt(x) * 65535.0 + 0.5).astype(jnp.int32) - 32768
@@ -345,8 +331,10 @@
     depth_up, depth_down = line(bricks)
     row_up, row_down = line(crosswise)
 
-    parts = [(1, strips - 2)] if strips > 2 else []
-    parts += [(s, 1) for s in sorted({0, strips - 1})]
+    batches = [(1, 1, strips - 2)] if strips > 2 else []
+    batches += [(0, max(strips - 1, 1), min(strips, 2))]
+    parts = [(1, strips - 2, 0, 0)] if strips > 2 else []
+    parts += [(s, 1, len(batches) - 1, i) for i, s in enumerate(sorted({0, strips - 1}))]
 
     prev = lax.ppermute(volume[slices - 1], "depth", depth_up)
     nxt = lax.ppermute(volume[0], "depth", depth_down)
@@ -358,71 +346,67 @@
     anywhere = pl.BlockSpec(memory_space=pl.ANY)
     moved = lambda n: pltpu.VMEM((n, tiles + 2, ROWS, LANES), jnp.float32)
     field = lambda n: pltpu.VMEM((n, tiles, ROWS + 20, LANES), jnp.float32)
+    across = pltpu.VMEM((tiles, ROWS, LANES), jnp.float32)
+    steps = pltpu.VMEM((4 * LANES, 2 * LANES), jnp.bfloat16)
+
+    def slab(strip_of, size, s, move=0):
+        if move == 0:
+            return pl.BlockSpec((size, ROWS, ny), lambda i: (s, strip_of(i), 0))
+        offset = -1 if move < 0 else ROWS // 8
+
+        def index(i):
+            return s, jnp.clip(strip_of(i) * (ROWS // 8) + offset, 0, rows // 8 - 1), 0
+
+        return pl.BlockSpec((size, 8, ny), index)
+
+    def cost(chunk, per):
+        return pl.CostEstimate(
+            flops=per * chunk * ny, bytes_accessed=chunk * ny * 32, transcendentals=0
+        )
+
+    mids = []
+    for first, step, count in batches:
+        strip_of = lambda i, first=first, step=step: first + step * i
+        edges = [above, below] if first == 0 else []
+        mid = pl.pallas_call(
+            functools.partial(inner_kernel, absorb, strip_of, strips),
+            out_shape=jax.ShapeDtypeStruct((4, count * ROWS, ny), jnp.float32),
+            grid=(count,),
+            in_specs=[smem, smem]
+            + [slab(strip_of, slices, 0, move) for move in (0, -1, 1)]
+            + [vmem] * len(edges),
+            out_specs=pl.BlockSpec((4, ROWS, ny), lambda i: (0, i, 0)),
+            scratch_shapes=[field(slices), moved(slices - 2), moved(slices - 2)]
+            + [across, across, steps],
+            cost_estimate=cost(count * ROWS, 800),
+            compiler_params=params(INNER_MIB),
+            name="inner",
+        )(shear, footprint, *[volume] * 3, *edges)
+        mids.append(mid)
+
     received = []
-    for part in parts:
-        first, count = part
+    for first, count, batch, place in parts:
         chunk = count * ROWS
         strip_of = lambda i, first=first: first + i
+        edges = [above, below] if first == 0 or first + count == strips else []
         flat = pl.BlockSpec((ROWS, ny), lambda i, first=first: (first + i, 0))
-        edges = [above, below] if first == 0 or first + count == strips else []
-
-        def slab(size, s, move=0, strip_of=strip_of):
-            if move == 0:
-                return pl.BlockSpec((size, ROWS, ny), lambda i: (s, strip_of(i), 0))
-            offset = -1 if move < 0 else ROWS // 8
-
-            def index(i):
-                return s, jnp.clip(strip_of(i) * (ROWS // 8) + offset, 0, rows // 8 - 1), 0
-
-            return pl.BlockSpec((size, 8, ny), index)
-
-        def cost(per, chunk=chunk):
-            return pl.CostEstimate(
-                flops=per * chunk * ny, bytes_accessed=chunk * ny * 32, transcendentals=0
-            )
-
-        side_shape = [jax.ShapeDtypeStruct((groups, 4, chunk, width), jnp.bfloat16)] * inner
-        side_spec = [pl.BlockSpec((groups, 4, ROWS, width), lambda i: (0, 0, i, 0))] * inner
-        whole = [slab(slices, 0), slab(slices, 0, -1), slab(slices, 0, 1)]
-        if not edges:
-            middle = pl.BlockSpec((4, ROWS, ny), lambda i: (0, i, 0))
-            mid = pl.pallas_call(
-                functools.partial(inner_kernel, absorb, strip_of, strips),
-                out_shape=jax.ShapeDtypeStruct((4, chunk, ny), jnp.float32),
-                grid=(count,),
-                in_specs=[smem, smem] + whole + [vmem] * len(edges),
-                out_specs=middle,
-                scratch_shapes=[field(slices), moved(slices - 2), moved(slices - 2)],
-                cost_estimate=cost(800),
-                compiler_params=params(INNER_MIB),
-                name="inner",
-            )(shear, footprint, *[volume] * 3, *edges)
-            sides = pl.pallas_call(
-                functools.partial(outer_kernel, absorb, inner, strip_of, strips),
-                out_shape=side_shape,
-                grid=(count,),
-                in_specs=[smem, smem, slab(2, 0), slab(2, slices // 2 - 1)]
-                + [slab(1, 0, -1), slab(1, 0, 1), slab(1, slices - 1, -1), slab(1, slices - 1, 1)]
-                + [flat, flat, middle]
-                + [vmem] * len(edges),
-                out_specs=side_spec,
-                scratch_shapes=[field(6), moved(2), moved(2)],
-                cost_estimate=cost(400),
-                compiler_params=params(OUTER_MIB),
-                name="outer",
-            )(shear, footprint, *[volume] * 6, prev, nxt, mid, *edges)
-        else:
-            sides = pl.pallas_call(
-                functools.partial(full_kernel, absorb, inner, strip_of, strips),
-                out_shape=side_shape,
-                grid=(count,),
-                in_specs=[smem, smem] + whole + [flat, flat] + [vmem] * len(edges),
-                out_specs=side_spec,
-                scratch_shapes=[field(slices + 2), moved(slices), moved(slices)],
-                cost_estimate=cost(1100),
-                compiler_params=params(OUTER_MIB),
-                name="full",
-            )(shear, footprint, *[volume] * 3, prev, nxt, *edges)
+        ends = [(2, 0, 0), (2, slices // 2 - 1, 0)]
+        ends += [(1, s, move) for s in (0, slices - 1) for move in (-1, 1)]
+        sides = pl.pallas_call(
+            functools.partial(outer_kernel, absorb, inner, strip_of, strips),
+            out_shape=[jax.ShapeDtypeStruct((groups, 4, chunk, width), jnp.bfloat16)] * inner,
+            grid=(count,),
+            in_specs=[smem, smem]
+            + [slab(strip_of, *end) for end in ends]
+            + [flat, flat]
+            + [pl.BlockSpec((4, ROWS, ny), lambda i, place=place: (0, place + i, 0))]
+            + [vmem] * len(edges),
+            out_specs=[pl.BlockSpec((groups, 4, ROWS, width), lambda i: (0, 0, i, 0))] * inner,
+            scratch_shapes=[field(6), moved(2), moved(2), across, across, steps],
+            cost_estimate=cost(chunk, 400),
+            compiler_params=params(OUTER_MIB),
+            name="outer",
+        )(shear, footprint, *[volume] * 6, prev, nxt, mids[batch], *edges)
         sides = list(sides)
         for k in range(1, inner):
             pairs = [
@@ -434,7 +418,7 @@
         received.append(sides)
 
     frame = None
-    for (first, count), sides in zip(parts, received):
+    for (first, count, _, _), sides in zip(parts, received):
         chunk = count * ROWS
         pieces = pl.pallas_call(
             functools.partial(group_kernel, inner),

time: 89 us -> 89.6 us (level)
  Pallas kernels: 34 us -> 32.7 us
  starting transfers between devices: 28.7 us -> 29.9 us
    pallas_call x2 -> x0, Pallas kernels: 12.4 us -> none  [shards(): pl.pallas_call(functools.partial(full_kernel, absorb, inner, strip_of, st...]
    pallas_call x1 -> x2, Pallas kernels: 10.2 us -> 17.4 us  [shards(): pl.pallas_call(functools.partial(inner_kernel, absorb, strip_of, strips),...]
    pallas_call x1 -> x3, Pallas kernels: 4.25 us -> 8.2 us  [shards(): pl.pallas_call(functools.partial(outer_kernel, absorb, inner, strip_of, s...]
    ppermute x1, waiting for transfers between devices: 8.67 us -> 10.2 us  [shards(): prev = lax.ppermute(volume[slices - 1], 'depth', depth_up)]
    ppermute x9, waiting for transfers between devices: 9.81 us -> 8.38 us  [shards(): pieces[k] = lax.ppermute(pieces[k], 'depth', pairs)]
    ppermute x9, starting transfers between devices: 12.5 us -> 13.5 us  [shards(): pieces[k] = lax.ppermute(pieces[k], 'depth', pairs)]
  transfers between devices with their start and end apart: 16 -> 16, of which waited for: 4 -> 5; matrix products, arithmetic and copies ran while one was open for 0% -> 0% of each run, Pallas kernels for 32% -> 31%
where the time goes in v1:
time: 89.6 us; the launch traced here: 88.8 us
  Pallas kernels  32.7 us (36%)
  starting transfers between devices  29.9 us (33%)
  waiting for transfers between devices  23 us (26%)
  local copies, waits for them, and re-layouts  3 us (3%)
    pallas_call x2, Pallas kernels, shards(): pl.pallas_call(functools.partial(inner_kernel, absorb, strip_of, strips),...  17.4 us
    ppermute x9, starting transfers between devices, shards(): pieces[k] = lax.ppermute(pieces[k], 'depth', pairs)  13.5 us
    ppermute x1, waiting for transfers between devices, shards(): prev = lax.ppermute(volume[slices - 1], 'depth', depth_up)  10.2 us
    ppermute x9, waiting for transfers between devices, shards(): pieces[k] = lax.ppermute(pieces[k], 'depth', pairs)  8.38 us
    pallas_call x3, Pallas kernels, shards(): pl.pallas_call(functools.partial(outer_kernel, absorb, inner, strip_of, s...  8.2 us
    ppermute x1, starting transfers between devices, shards(): above = lax.ppermute(volume[:, rows - 1, :], 'tile', row_up)  4.83 us
    pallas_call x3, Pallas kernels, shards(): pl.pallas_call(functools.partial(frame_kernel, inner, frame is not None),...  4.35 us
    ppermute x1, starting transfers between devices, shards(): prev = lax.ppermute(volume[slices - 1], 'depth', depth_up)  3.97 us
  transfers between devices with their start and end apart: 16, of which 5 were waited for; matrix products, arithmetic and copies ran while one was open for 0% of the time, Pallas kernels for 31%

profile of v1, /device:TPU:1, one launch (start us, length us, event | category | flops | bytes accessed | tf_op | source)
XLA Modules:
  0.0 88.8 jit_solution(17538355559019534352)
XLA Ops:
  0.0 1.3 %slice_bitcast_fusion = (bf16[64,4096]{1,0:T(8,128)(2,1)S(1)}, bf16[64,4096]{1,0:T(8,128)(2,1)S(1)}) fusion(bf16[8,64,4096]{2,1,0:T(8,128)(2,1)} %refs_5_.5), kind=kLoop, calls=%fused_computation | loop fusion | bytes 2097152 | tf_op jit(solution)/shard_map/squeeze | solution.py:340
  1.3 4.0 %collective-permute-start = (bf16[64,4096]{1,0:T(8,128)(2,1)S(1)}, bf16[64,4096]{1,0:T(8,128)(2,1)S(1)}, u32[]{:S(2)}, u32[]{:S(2)}) collective-permute-start(bf16[64,4096]{1,0:T(8,128)(2,1)S(1)} %get-tuple-element.44), channel_id=1, source_target_pairs={{0,4},{4,8},{8,12},{12,16},{16,20},{20,24},{24,28},{1,5},{5,9},{9,... | collective-permute-start | bytes 1572872 | tf_op jit(solution)/shard_map/ppermute | solution.py:339
  5.2 0.0 copy-start
  5.3 1.6 %collective-permute-start.1 = (bf16[64,4096]{1,0:T(8,128)(2,1)S(1)}, bf16[64,4096]{1,0:T(8,128)(2,1)S(1)}, u32[]{:S(2)}, u32[]{:S(2)}) collective-permute-start(bf16[64,4096]{1,0:T(8,128)(2,1)S(1)} %get-tuple-element.43), channel_id=1, source_target_pairs={{4,0},{8,4},{12,8},{16,12},{20,16},{24,20},{28,24},{5,1},{9,5},{13... | collective-permute-start | bytes 1572872 | tf_op jit(solution)/shard_map/ppermute | solution.py:340
  6.8 0.0 copy-start.2
  6.8 0.6 copy-done.2
  7.5 0.7 copy-done.3
  8.1 8.6 %inner.3.refs_8_ = f32[4,32,4096]{2,1,0:T(8,128)S(1)} custom-call(s32[64]{0:T(128)S(1)} %copy-done.2, s32[1,2]{1,0:T(1,128)S(1)} %copy-done.3, bf16[8,64,4096]{2,1,0:T(8,128)(2,1)} %refs_5_.5, bf16[8,64,4096]{2,1,0:T(8,128)(2,1)} %refs_5_.5, bf16[8,64,4096]{2,1,0:T(8,128)(2,1)} %refs_5_.5), custom_call_target="tpu_custom_call" | custom-call | flops 104857600 | bytes 4194304 | tf_op jit(solution)/shard_map/inner/pallas_call | solution.py:371
  16.8 10.2 %collective-permute-done.refs_6_ = bf16[64,4096]{1,0:T(8,128)(2,1)S(1)} collective-permute-done((bf16[64,4096]{1,0:T(8,128)(2,1)S(1)}, bf16[64,4096]{1,0:T(8,128)(2,1)S(1)}, u32[]{:S(2)}, u32[]{:S(2)}) %collective-permute-start) | collective-permute-done | bytes 524320 | tf_op jit(solution)/shard_map/ppermute | solution.py:339
  27.0 0.0 collective-permute-done.1.refs_7_
  27.0 4.0 %outer.5 = (bf16[4,4,32,512]{3,2,1,0:T(8,128)(2,1)S(1)}, bf16[4,4,32,512]{3,2,1,0:T(8,128)(2,1)S(1)}) custom-call(s32[64]{0:T(128)S(1)} %copy-done.2, s32[1,2]{1,0:T(1,128)S(1)} %copy-done.3, bf16[8,64,4096]{2,1,0:T(8,128)(2,1)S(1)} %copy-done, bf16[8,64,4096]{2,1,0:T(8,128)(2,1)S(1)} %copy-done, bf16[8,64,4096]{2,1,0:T(8,128)(2,1)S(1)} %copy-done, ...), custom_call_target="tpu_custom_call" | custom-call | flops 52428800 | bytes 4194304 | tf_op jit(solution)/shard_map/outer/pallas_call | solution.py:395
  31.0 2.3 %collective-permute-start.12 = (bf16[4,4,32,512]{3,2,1,0:T(8,128)(2,1)S(1)}, bf16[4,4,32,512]{3,2,1,0:T(8,128)(2,1)S(1)}, u32[]{:S(2)}, u32[]{:S(2)}) collective-permute-start(bf16[4,4,32,512]{3,2,1,0:T(8,128)(2,1)S(1)} %get-tuple-element.36), channel_id=1, source_target_pairs={{0,4},{4,0},{8,12},{12,8},{16,20},{20,16},{24,28},{28,24},{1,5},{5... | collective-permute-start | bytes 1572872 | tf_op jit(solution)/shard_map/ppermute | solution.py:417
  33.3 0.3 fusion
  33.6 0.1 copy.13
  33.7 4.8 %collective-permute-start.2 = (bf16[8,4096]{1,0:T(8,128)(2,1)S(1)}, bf16[8,4096]{1,0:T(8,128)(2,1)S(1)}, u32[]{:S(2)}, u32[]{:S(2)}) collective-permute-start(bf16[8,4096]{1,0:T(8,128)(2,1)S(1)} %bitcast.10), channel_id=1, source_target_pairs={{0,1},{1,2},{2,3},{4,5},{5,6},{6,7},{8,9},{9,10},{10,11},{12,13},{... | collective-permute-start | bytes 196616 | tf_op jit(solution)/shard_map/ppermute | solution.py:341
  38.5 0.1 copy.12
  38.6 0.0 copy-start.1
  38.6 2.2 %collective-permute-start.3 = (bf16[8,4096]{1,0:T(8,128)(2,1)S(1)}, bf16[8,4096]{1,0:T(8,128)(2,1)S(1)}, u32[]{:S(2)}, u32[]{:S(2)}) collective-permute-start(bf16[8,4096]{1,0:T(8,128)(2,1)S(1)} %bitcast.11), channel_id=1, source_target_pairs={{1,0},{2,1},{3,2},{5,4},{6,5},{7,6},{9,8},{10,9},{11,10},{13,12},{... | collective-permute-start | bytes 196616 | tf_op jit(solution)/shard_map/ppermute | solution.py:342
  40.8 3.9 %collective-permute-done.3.refs_1_.refs_10_ = bf16[8,4096]{1,0:T(8,128)(2,1)S(1)} collective-permute-done((bf16[8,4096]{1,0:T(8,128)(2,1)S(1)}, bf16[8,4096]{1,0:T(8,128)(2,1)S(1)}, u32[]{:S(2)}, u32[]{:S(2)}) %collective-permute-start.3) | collective-permute-done | bytes 65568 | tf_op jit(solution)/shard_map/ppermute | solution.py:342
  44.7 8.8 %inner.2.refs_8_ = f32[4,32,4096]{2,1,0:T(8,128)S(1)} custom-call(s32[64]{0:T(128)S(1)} %copy-done.2, s32[1,2]{1,0:T(1,128)S(1)} %copy-done.3, bf16[8,64,4096]{2,1,0:T(8,128)(2,1)} %refs_5_.5, bf16[8,64,4096]{2,1,0:T(8,128)(2,1)} %refs_5_.5, bf16[8,64,4096]{2,1,0:T(8,128)(2,1)} %refs_5_.5, bf16[8,4096]{1,0:T(8,128)(2,1)S(1)} %collective-permute-done.2.refs_0_.refs_9_, ...), custom_call_target="tpu_custom_call" | custom-call | flops 104857600 | bytes 4194304 | tf_op jit(solution)/shard_map/inner/pallas_call | solution.py:371
  53.5 2.1 %outer.4 = (bf16[4,4,16,512]{3,2,1,0:T(8,128)(2,1)S(1)}, bf16[4,4,16,512]{3,2,1,0:T(8,128)(2,1)S(1)}) custom-call(s32[64]{0:T(128)S(1)} %copy-done.2, s32[1,2]{1,0:T(1,128)S(1)} %copy-done.3, bf16[8,64,4096]{2,1,0:T(8,128)(2,1)S(1)} %copy-done.1, bf16[8,64,4096]{2,1,0:T(8,128)(2,1)S(1)} %copy-done.1, bf16[8,64,4096]{2,1,0:T(8,128)(2,1)S(1)} %copy-done.1, ...), custom_call_target="tpu_custom_call" | custom-call | flops 26214400 | bytes 2097152 | tf_op jit(solution)/shard_map/outer/pallas_call | solution.py:395
  55.6 0.1 collective-permute-start.8
  55.7 2.1 %outer.3 = (bf16[4,4,16,512]{3,2,1,0:T(8,128)(2,1)S(1)}, bf16[4,4,16,512]{3,2,1,0:T(8,128)(2,1)S(1)}) custom-call(s32[64]{0:T(128)S(1)} %copy-done.2, s32[1,2]{1,0:T(1,128)S(1)} %copy-done.3, bf16[8,64,4096]{2,1,0:T(8,128)(2,1)S(1)} %copy-done.1, bf16[8,64,4096]{2,1,0:T(8,128)(2,1)S(1)} %copy-done.1, bf16[8,64,4096]{2,1,0:T(8,128)(2,1)S(1)} %copy-done.1, ...), custom_call_target="tpu_custom_call" | custom-call | flops 26214400 | bytes 2097152 | tf_op jit(solution)/shard_map/outer/pallas_call | solution.py:395
  57.8 1.5 %collective-permute-start.4 = (bf16[4,4,16,512]{3,2,1,0:T(8,128)(2,1)S(1)}, bf16[4,4,16,512]{3,2,1,0:T(8,128)(2,1)S(1)}, u32[]{:S(2)}, u32[]{:S(2)}) collective-permute-start(bf16[4,4,16,512]{3,2,1,0:T(8,128)(2,1)S(1)} %get-tuple-element.24), channel_id=1, source_target_pairs={{0,4},{4,0},{8,12},{12,8},{16,20},{20,16},{24,28},{28,24},{1,5},{5... | collective-permute-start | bytes 786440 | tf_op jit(solution)/shard_map/ppermute | solution.py:417
  59.3 0.0 collective-permute-done.12.refs_1_
  59.3 1.2 %group.5 = (s16[4,32,512]{2,1,0:T(8,128)(2,1)S(1)}, s16[4,32,512]{2,1,0:T(8,128)(2,1)S(1)}, s16[4,32,512]{2,1,0:T(8,128)(2,1)S(1)}, s16[4,32,512]{2,1,0:T(8,128)(2,1)S(1)}) custom-call(s32[64]{0:T(128)S(1)} %copy-done.2, bf16[4,4,32,512]{3,2,1,0:T(8,128)(2,1)S(1)} %get-tuple-element.35.refs_0_, bf16[4,4,32,512]{3,2,1,0:T(8,128)(2,1)S(1)} %collective-permute-done.12.refs_1_), custom_call_target="tpu_custom_call" | custom-call | flops 2621440 | bytes 2097152 | tf_op jit(solution)/shard_map/group/pallas_call | solution.py:423
  60.5 1.3 %collective-permute-start.13 = (s16[4,32,512]{2,1,0:T(8,128)(2,1)S(1)}, s16[4,32,512]{2,1,0:T(8,128)(2,1)S(1)}, u32[]{:S(2)}, u32[]{:S(2)}) collective-permute-start(s16[4,32,512]{2,1,0:T(8,128)(2,1)S(1)} %get-tuple-element.38), channel_id=1, source_target_pairs={{0,8},{4,12},{8,16},{12,20},{16,24},{20,28},{24,0},{28,4},{1,9},{5... | collective-permute-start | bytes 393224 | tf_op jit(solution)/shard_map/ppermute | solution.py:443
  61.9 2.0 %collective-permute-start.14 = (s16[4,32,512]{2,1,0:T(8,128)(2,1)S(1)}, s16[4,32,512]{2,1,0:T(8,128)(2,1)S(1)}, u32[]{:S(2)}, u32[]{:S(2)}) collective-permute-start(s16[4,32,512]{2,1,0:T(8,128)(2,1)S(1)} %get-tuple-element.39), channel_id=1, source_target_pairs={{0,16},{4,20},{8,24},{12,28},{16,0},{20,4},{24,8},{28,12},{1,17},{... | collective-permute-start | bytes 393224 | tf_op jit(solution)/shard_map/ppermute | solution.py:443
  63.9 1.3 %collective-permute-start.15 = (s16[4,32,512]{2,1,0:T(8,128)(2,1)S(1)}, s16[4,32,512]{2,1,0:T(8,128)(2,1)S(1)}, u32[]{:S(2)}, u32[]{:S(2)}) collective-permute-start(s16[4,32,512]{2,1,0:T(8,128)(2,1)S(1)} %get-tuple-element.40), channel_id=1, source_target_pairs={{0,24},{4,28},{8,0},{12,4},{16,8},{20,12},{24,16},{28,20},{1,25},{... | collective-permute-start | bytes 393224 | tf_op jit(solution)/shard_map/ppermute | solution.py:443
  65.3 0.8 group.4
  66.1 0.9 collective-permute-start.10
  66.9 0.4 collective-permute-done.4.refs_1_
  67.4 2.7 %collective-permute-start.11 = (s16[4,16,512]{2,1,0:T(8,128)(2,1)S(1)}, s16[4,16,512]{2,1,0:T(8,128)(2,1)S(1)}, u32[]{:S(2)}, u32[]{:S(2)}) collective-permute-start(s16[4,16,512]{2,1,0:T(8,128)(2,1)S(1)} %get-tuple-element.34), channel_id=1, source_target_pairs={{0,24},{4,28},{8,0},{12,4},{16,8},{20,12},{24,16},{28,20},{1,25},{... | collective-permute-start | bytes 196616 | tf_op jit(solution)/shard_map/ppermute | solution.py:443
  70.1 0.8 group.3
  70.9 6.5 %collective-permute-done.10.refs_2_ = s16[4,16,512]{2,1,0:T(8,128)(2,1)S(1)} collective-permute-done((s16[4,16,512]{2,1,0:T(8,128)(2,1)S(1)}, s16[4,16,512]{2,1,0:T(8,128)(2,1)S(1)}, u32[]{:S(2)}, u32[]{:S(2)}) %collective-permute-start.10) | collective-permute-done | bytes 65568 | tf_op jit(solution)/shard_map/ppermute | solution.py:443
  77.4 0.0 collective-permute-start.9
  77.4 0.0 collective-permute-start.5
  77.5 0.0 collective-permute-done.14.refs_2_
  77.5 3.5 %collective-permute-start.6 = (s16[4,16,512]{2,1,0:T(8,128)(2,1)S(1)}, s16[4,16,512]{2,1,0:T(8,128)(2,1)S(1)}, u32[]{:S(2)}, u32[]{:S(2)}) collective-permute-start(s16[4,16,512]{2,1,0:T(8,128)(2,1)S(1)} %get-tuple-element.27), channel_id=1, source_target_pairs={{0,16},{4,20},{8,24},{12,28},{16,0},{20,4},{24,8},{28,12},{1,17},{... | collective-permute-start | bytes 196616 | tf_op jit(solution)/shard_map/ppermute | solution.py:443
  81.0 0.0 collective-permute-done.15.refs_3_
  81.0 1.6 %collective-permute-start.7 = (s16[4,16,512]{2,1,0:T(8,128)(2,1)S(1)}, s16[4,16,512]{2,1,0:T(8,128)(2,1)S(1)}, u32[]{:S(2)}, u32[]{:S(2)}) collective-permute-start(s16[4,16,512]{2,1,0:T(8,128)(2,1)S(1)} %get-tuple-element.28), channel_id=1, source_target_pairs={{0,24},{4,28},{8,0},{12,4},{16,8},{20,12},{24,16},{28,20},{1,25},{... | collective-permute-start | bytes 196616 | tf_op jit(solution)/shard_map/ppermute | solution.py:443
  82.6 1.6 %frame.3.refs_4_ = f32[4,64,512]{2,1,0:T(8,128)} custom-call(s32[64]{0:T(128)S(1)} %copy-done.2, s16[4,32,512]{2,1,0:T(8,128)(2,1)S(1)} %get-tuple-element.37.refs_0_, s16[4,32,512]{2,1,0:T(8,128)(2,1)S(1)} %collective-permute-done.13.refs_1_, s16[4,32,512]{2,1,0:T(8,128)(2,1)S(1)} %collective-permute-done.14.refs_2_, ...), custom_call_target="tpu_custom_call" | custom-call | flops 327680 | bytes 2097152 | tf_op jit(solution)/shard_map/frame/pallas_call | solution.py:444
  84.2 0.0 collective-permute-done.11.refs_3_
  84.2 0.0 collective-permute-done.9.refs_1_
  84.2 1.4 %frame.4.refs_4_ = f32[4,64,512]{2,1,0:T(8,128)} custom-call(s32[64]{0:T(128)S(1)} %copy-done.2, s16[4,16,512]{2,1,0:T(8,128)(2,1)S(1)} %get-tuple-element.31.refs_0_, s16[4,16,512]{2,1,0:T(8,128)(2,1)S(1)} %collective-permute-done.9.refs_1_, s16[4,16,512]{2,1,0:T(8,128)(2,1)S(1)} %collective-permute-done.10.refs_2_, ...), custom_call_target="tpu_custom_call", output_to_operand_aliasing={{}: (5, {})} | custom-call | flops 163840 | bytes 2097152 | tf_op jit(solution)/shard_map/frame/pallas_call | solution.py:444
  85.6 0.0 collective-permute-done.5.refs_1_
  85.6 1.9 %collective-permute-done.6.refs_2_ = s16[4,16,512]{2,1,0:T(8,128)(2,1)S(1)} collective-permute-done((s16[4,16,512]{2,1,0:T(8,128)(2,1)S(1)}, s16[4,16,512]{2,1,0:T(8,128)(2,1)S(1)}, u32[]{:S(2)}, u32[]{:S(2)}) %collective-permute-start.6) | collective-permute-done | bytes 65568 | tf_op jit(solution)/shard_map/ppermute | solution.py:443
  87.5 1.4 %frame.5 = f32[4,64,512]{2,1,0:T(8,128)} custom-call(s32[64]{0:T(128)S(1)} %copy-done.2, s16[4,16,512]{2,1,0:T(8,128)(2,1)S(1)} %get-tuple-element.25.refs_0_, s16[4,16,512]{2,1,0:T(8,128)(2,1)S(1)} %collective-permute-done.5.refs_1_, s16[4,16,512]{2,1,0:T(8,128)(2,1)S(1)} %collective-permute-done.6.refs_2_, ...), custom_call_target="tpu_custom_call", output_to_operand_aliasing={{}: (5, {})} | custom-call | flops 163840 | bytes 2097152 | tf_op jit(solution)/shard_map/frame/pallas_call | solution.py:444
  (7 shorter events, 0.0 us)
Async XLA Ops:
  1.3 25.8 %collective-permute-start = (bf16[64,4096]{1,0:T(8,128)(2,1)S(1)}, bf16[64,4096]{1,0:T(8,128)(2,1)S(1)}, u32[]{:S(2)}, u32[]{:S(2)}) collective-permute-start(bf16[64,4096]{1,0:T(8,128)(2,1)S(1)} %get-tuple-element.44), channel_id=1, source_target_pairs={{0,4},{4,8},{8,12},{12,16},{16,20},{20,24},{24,28},{1,5},{5,9},{9,... | collective-permute-start | bytes 1572872 | tf_op jit(solution)/shard_map/ppermute | solution.py:339
  5.2 21.8 %copy-start = (bf16[8,64,4096]{2,1,0:T(8,128)(2,1)S(1)}, bf16[8,64,4096]{2,1,0:T(8,128)(2,1)}, u32[]{:S(2)}) copy-start(bf16[8,64,4096]{2,1,0:T(8,128)(2,1)} %refs_5_.5) | copy-start | bytes 12582916
  5.3 21.8 %collective-permute-start.1 = (bf16[64,4096]{1,0:T(8,128)(2,1)S(1)}, bf16[64,4096]{1,0:T(8,128)(2,1)S(1)}, u32[]{:S(2)}, u32[]{:S(2)}) collective-permute-start(bf16[64,4096]{1,0:T(8,128)(2,1)S(1)} %get-tuple-element.43), channel_id=1, source_target_pairs={{4,0},{8,4},{12,8},{16,12},{20,16},{24,20},{28,24},{5,1},{9,5},{13... | collective-permute-start | bytes 1572872 | tf_op jit(solution)/shard_map/ppermute | solution.py:340
  6.8 0.7 copy-start.2
  7.5 0.7 copy-start.3
  31.0 28.3 %collective-permute-start.12 = (bf16[4,4,32,512]{3,2,1,0:T(8,128)(2,1)S(1)}, bf16[4,4,32,512]{3,2,1,0:T(8,128)(2,1)S(1)}, u32[]{:S(2)}, u32[]{:S(2)}) collective-permute-start(bf16[4,4,32,512]{3,2,1,0:T(8,128)(2,1)S(1)} %get-tuple-element.36), channel_id=1, source_target_pairs={{0,4},{4,0},{8,12},{12,8},{16,20},{20,16},{24,28},{28,24},{1,5},{5... | collective-permute-start | bytes 1572872 | tf_op jit(solution)/shard_map/ppermute | solution.py:417
  33.7 7.1 %collective-permute-start.2 = (bf16[8,4096]{1,0:T(8,128)(2,1)S(1)}, bf16[8,4096]{1,0:T(8,128)(2,1)S(1)}, u32[]{:S(2)}, u32[]{:S(2)}) collective-permute-start(bf16[8,4096]{1,0:T(8,128)(2,1)S(1)} %bitcast.10), channel_id=1, source_target_pairs={{0,1},{1,2},{2,3},{4,5},{5,6},{6,7},{8,9},{9,10},{10,11},{12,13},{... | collective-permute-start | bytes 196616 | tf_op jit(solution)/shard_map/ppermute | solution.py:341
  38.6 14.9 %copy-start.1 = (bf16[8,64,4096]{2,1,0:T(8,128)(2,1)S(1)}, bf16[8,64,4096]{2,1,0:T(8,128)(2,1)}, u32[]{:S(2)}) copy-start(bf16[8,64,4096]{2,1,0:T(8,128)(2,1)} %refs_5_.5) | copy-start | bytes 12582916
  38.6 6.1 %collective-permute-start.3 = (bf16[8,4096]{1,0:T(8,128)(2,1)S(1)}, bf16[8,4096]{1,0:T(8,128)(2,1)S(1)}, u32[]{:S(2)}, u32[]{:S(2)}) collective-permute-start(bf16[8,4096]{1,0:T(8,128)(2,1)S(1)} %bitcast.11), channel_id=1, source_target_pairs={{1,0},{2,1},{3,2},{5,4},{6,5},{7,6},{9,8},{10,9},{11,10},{13,12},{... | collective-permute-start | bytes 196616 | tf_op jit(solution)/shard_map/ppermute | solution.py:342
  55.6 9.6 %collective-permute-start.8 = (bf16[4,4,16,512]{3,2,1,0:T(8,128)(2,1)S(1)}, bf16[4,4,16,512]{3,2,1,0:T(8,128)(2,1)S(1)}, u32[]{:S(2)}, u32[]{:S(2)}) collective-permute-start(bf16[4,4,16,512]{3,2,1,0:T(8,128)(2,1)S(1)} %get-tuple-element.30), channel_id=1, source_target_pairs={{0,4},{4,0},{8,12},{12,8},{16,20},{20,16},{24,28},{28,24},{1,5},{5... | collective-permute-start | bytes 786440 | tf_op jit(solution)/shard_map/ppermute | solution.py:417
  57.8 9.6 %collective-permute-start.4 = (bf16[4,4,16,512]{3,2,1,0:T(8,128)(2,1)S(1)}, bf16[4,4,16,512]{3,2,1,0:T(8,128)(2,1)S(1)}, u32[]{:S(2)}, u32[]{:S(2)}) collective-permute-start(bf16[4,4,16,512]{3,2,1,0:T(8,128)(2,1)S(1)} %get-tuple-element.24), channel_id=1, source_target_pairs={{0,4},{4,0},{8,12},{12,8},{16,20},{20,16},{24,28},{28,24},{1,5},{5... | collective-permute-start | bytes 786440 | tf_op jit(solution)/shard_map/ppermute | solution.py:417
  60.5 16.9 %collective-permute-start.13 = (s16[4,32,512]{2,1,0:T(8,128)(2,1)S(1)}, s16[4,32,512]{2,1,0:T(8,128)(2,1)S(1)}, u32[]{:S(2)}, u32[]{:S(2)}) collective-permute-start(s16[4,32,512]{2,1,0:T(8,128)(2,1)S(1)} %get-tuple-element.38), channel_id=1, source_target_pairs={{0,8},{4,12},{8,16},{12,20},{16,24},{20,28},{24,0},{28,4},{1,9},{5... | collective-permute-start | bytes 393224 | tf_op jit(solution)/shard_map/ppermute | solution.py:443
  61.9 15.6 %collective-permute-start.14 = (s16[4,32,512]{2,1,0:T(8,128)(2,1)S(1)}, s16[4,32,512]{2,1,0:T(8,128)(2,1)S(1)}, u32[]{:S(2)}, u32[]{:S(2)}) collective-permute-start(s16[4,32,512]{2,1,0:T(8,128)(2,1)S(1)} %get-tuple-element.39), channel_id=1, source_target_pairs={{0,16},{4,20},{8,24},{12,28},{16,0},{20,4},{24,8},{28,12},{1,17},{... | collective-permute-start | bytes 393224 | tf_op jit(solution)/shard_map/ppermute | solution.py:443
  63.9 17.1 %collective-permute-start.15 = (s16[4,32,512]{2,1,0:T(8,128)(2,1)S(1)}, s16[4,32,512]{2,1,0:T(8,128)(2,1)S(1)}, u32[]{:S(2)}, u32[]{:S(2)}) collective-permute-start(s16[4,32,512]{2,1,0:T(8,128)(2,1)S(1)} %get-tuple-element.40), channel_id=1, source_target_pairs={{0,24},{4,28},{8,0},{12,4},{16,8},{20,12},{24,16},{28,20},{1,25},{... | collective-permute-start | bytes 393224 | tf_op jit(solution)/shard_map/ppermute | solution.py:443
  66.1 11.4 %collective-permute-start.10 = (s16[4,16,512]{2,1,0:T(8,128)(2,1)S(1)}, s16[4,16,512]{2,1,0:T(8,128)(2,1)S(1)}, u32[]{:S(2)}, u32[]{:S(2)}) collective-permute-start(s16[4,16,512]{2,1,0:T(8,128)(2,1)S(1)} %get-tuple-element.33), channel_id=1, source_target_pairs={{0,16},{4,20},{8,24},{12,28},{16,0},{20,4},{24,8},{28,12},{1,17},{... | collective-permute-start | bytes 196616 | tf_op jit(solution)/shard_map/ppermute | solution.py:443
  67.4 16.8 %collective-permute-start.11 = (s16[4,16,512]{2,1,0:T(8,128)(2,1)S(1)}, s16[4,16,512]{2,1,0:T(8,128)(2,1)S(1)}, u32[]{:S(2)}, u32[]{:S(2)}) collective-permute-start(s16[4,16,512]{2,1,0:T(8,128)(2,1)S(1)} %get-tuple-element.34), channel_id=1, source_target_pairs={{0,24},{4,28},{8,0},{12,4},{16,8},{20,12},{24,16},{28,20},{1,25},{... | collective-permute-start | bytes 196616 | tf_op jit(solution)/shard_map/ppermute | solution.py:443
  77.4 6.8 %collective-permute-start.9 = (s16[4,16,512]{2,1,0:T(8,128)(2,1)S(1)}, s16[4,16,512]{2,1,0:T(8,128)(2,1)S(1)}, u32[]{:S(2)}, u32[]{:S(2)}) collective-permute-start(s16[4,16,512]{2,1,0:T(8,128)(2,1)S(1)} %get-tuple-element.32), channel_id=1, source_target_pairs={{0,8},{4,12},{8,16},{12,20},{16,24},{20,28},{24,0},{28,4},{1,9},{5... | collective-permute-start | bytes 196616 | tf_op jit(solution)/shard_map/ppermute | solution.py:443
  77.4 8.2 %collective-permute-start.5 = (s16[4,16,512]{2,1,0:T(8,128)(2,1)S(1)}, s16[4,16,512]{2,1,0:T(8,128)(2,1)S(1)}, u32[]{:S(2)}, u32[]{:S(2)}) collective-permute-start(s16[4,16,512]{2,1,0:T(8,128)(2,1)S(1)} %get-tuple-element.26), channel_id=1, source_target_pairs={{0,8},{4,12},{8,16},{12,20},{16,24},{20,28},{24,0},{28,4},{1,9},{5... | collective-permute-start | bytes 196616 | tf_op jit(solution)/shard_map/ppermute | solution.py:443
  77.5 10.0 %collective-permute-start.6 = (s16[4,16,512]{2,1,0:T(8,128)(2,1)S(1)}, s16[4,16,512]{2,1,0:T(8,128)(2,1)S(1)}, u32[]{:S(2)}, u32[]{:S(2)}) collective-permute-start(s16[4,16,512]{2,1,0:T(8,128)(2,1)S(1)} %get-tuple-element.27), channel_id=1, source_target_pairs={{0,16},{4,20},{8,24},{12,28},{16,0},{20,4},{24,8},{28,12},{1,17},{... | collective-permute-start | bytes 196616 | tf_op jit(solution)/shard_map/ppermute | solution.py:443
  81.0 6.5 %collective-permute-start.7 = (s16[4,16,512]{2,1,0:T(8,128)(2,1)S(1)}, s16[4,16,512]{2,1,0:T(8,128)(2,1)S(1)}, u32[]{:S(2)}, u32[]{:S(2)}) collective-permute-start(s16[4,16,512]{2,1,0:T(8,128)(2,1)S(1)} %get-tuple-element.28), channel_id=1, source_target_pairs={{0,24},{4,28},{8,0},{12,4},{16,8},{20,12},{24,16},{28,20},{1,25},{... | collective-permute-start | bytes 196616 | tf_op jit(solution)/shard_map/ppermute | solution.py:443

commit v2 on v1

--- a/solution.py
+++ b/solution.py
@@ -285,14 +285,19 @@
     groups = len(outs)
 
     def body(order):
-        for k in range(groups):
-            target = lax.rem(lax.div(me, inner) + k, groups)
-            pieces = [
-                [sources[shift][target, c].astype(jnp.float32) for c in range(4)]
-                for shift in order
-            ]
-            for c, value in enumerate(over(pieces)):
-                outs[k][c] = encode(value)
+        def step(i, carry):
+            at = pl.ds(pl.multiple_of(i * ROWS, ROWS), ROWS)
+            for k in range(groups):
+                target = lax.rem(lax.div(me, inner) + k, groups)
+                pieces = [
+                    [sources[shift][target, c, at, :].astype(jnp.float32) for c in range(4)]
+                    for shift in order
+                ]
+                for c, value in enumerate(over(pieces)):
+                    outs[k][c, at, :] = encode(value)
+            return carry
+
+        lax.fori_loop(0, outs[0].shape[1] // ROWS, step, 0)
 
     ordered(inner, lax.rem(me, inner), flip, body)
 
@@ -304,8 +309,10 @@
     me = lax.axis_index("depth")
     flip = shear[0] > shear[shear.shape[0] - 1]
 
+    at = pl.ds(pl.multiple_of(pl.program_id(0) * ROWS, ROWS), ROWS)
+
     def body(order):
-        pieces = [[decode(sources[shift][c]) for c in range(4)] for shift in order]
+        pieces = [[decode(sources[shift][c, at, :]) for c in range(4)] for shift in order]
         for c, value in enumerate(over(pieces)):
             out[c] = value
 
@@ -333,8 +340,11 @@
 
     batches = [(1, 1, strips - 2)] if strips > 2 else []
     batches += [(0, max(strips - 1, 1), min(strips, 2))]
-    parts = [(1, strips - 2, 0, 0)] if strips > 2 else []
-    parts += [(s, 1, len(batches) - 1, i) for i, s in enumerate(sorted({0, strips - 1}))]
+    parts = [(*batches[-1], len(batches) - 1, 0)]
+    if strips > 2:
+        parts.insert(0, (1, 1, 1, 0, 0))
+    if strips > 3:
+        parts.append((2, 1, strips - 3, 0, 1))
 
     prev = lax.ppermute(volume[slices - 1], "depth", depth_up)
     nxt = lax.ppermute(volume[0], "depth", depth_down)
@@ -385,11 +395,11 @@
         mids.append(mid)
 
     received = []
-    for first, count, batch, place in parts:
+    for first, step, count, batch, place in parts:
         chunk = count * ROWS
-        strip_of = lambda i, first=first: first + i
-        edges = [above, below] if first == 0 or first + count == strips else []
-        flat = pl.BlockSpec((ROWS, ny), lambda i, first=first: (first + i, 0))
+        strip_of = lambda i, first=first, step=step: first + step * i
+        edges = [above, below] if first == 0 else []
+        flat = pl.BlockSpec((ROWS, ny), lambda i, strip_of=strip_of: (strip_of(i), 0))
         ends = [(2, 0, 0), (2, slices // 2 - 1, 0)]
         ends += [(1, s, move) for s in (0, slices - 1) for move in (-1, 1)]
         sides = pl.pallas_call(
@@ -418,15 +428,14 @@
         received.append(sides)
 
     frame = None
-    for (first, count, _, _), sides in zip(parts, received):
+    for number, sides in enumerate(received):
+        first, step, count, _, _ = parts[number]
         chunk = count * ROWS
         pieces = pl.pallas_call(
             functools.partial(group_kernel, inner),
             out_shape=[jax.ShapeDtypeStruct((4, chunk, width), LINK)] * groups,
-            grid=(count,),
-            in_specs=[smem]
-            + [pl.BlockSpec((groups, 4, ROWS, width), lambda i: (0, 0, i, 0))] * inner,
-            out_specs=[pl.BlockSpec((4, ROWS, width), lambda i: (0, i, 0))] * groups,
+            in_specs=[smem] + [vmem] * inner,
+            out_specs=[vmem] * groups,
             cost_estimate=pl.CostEstimate(
                 flops=20 * chunk * ny, bytes_accessed=2 << 20, transcendentals=0
             ),
@@ -446,10 +455,10 @@
             out_shape=jax.ShapeDtypeStruct((4, rows, width), jnp.float32),
             grid=(count,),
             in_specs=[smem]
-            + [pl.BlockSpec((4, ROWS, width), lambda i: (0, i, 0))] * groups
+            + [vmem] * groups
             + [anywhere] * (frame is not None),
             out_specs=pl.BlockSpec(
-                (4, ROWS, width), lambda i, first=first: (0, first + i, 0)
+                (4, ROWS, width), lambda i, first=first, step=step: (0, first + step * i, 0)
             ),
             input_output_aliases={} if frame is None else {1 + groups: 0},
             cost_estimate=pl.CostEstimate(

time: 89.6 us -> 85 us (0.949)
  waiting for transfers between devices: 23 us -> 18.3 us
  starting transfers between devices: 29.9 us -> 28.2 us
  local copies, waits for them, and re-layouts: 3 us -> 4.16 us
    ppermute x1, waiting for transfers between devices: 10.2 us -> 0.01 us  [shards(): prev = lax.ppermute(volume[slices - 1], 'depth', depth_up)]
    ppermute x3, waiting for transfers between devices: 0.45 us -> 3.93 us  [shards(): sides[k] = lax.ppermute(sides[k], 'depth', pairs)]
    ppermute x9, waiting for transfers between devices: 8.38 us -> 10.7 us  [shards(): pieces[k] = lax.ppermute(pieces[k], 'depth', pairs)]
    ppermute x9, starting transfers between devices: 13.5 us -> 11.6 us  [shards(): pieces[k] = lax.ppermute(pieces[k], 'depth', pairs)]
    slice x1, local copies, waits for them, and re-layouts: 0.25 us -> 1.41 us  [shards(): below = lax.ppermute(volume[:, 0, :], 'tile', row_down)]
  transfers between devices with their start and end apart: 16 -> 16, of which waited for: 5 -> 5; matrix products, arithmetic and copies ran while one was open for 0% -> 2% of each run, Pallas kernels for 31% -> 33%
where the time goes in v2:
time: 85 us; the launch traced here: 83.4 us
  Pallas kernels  32.5 us (38%)
  starting transfers between devices  28.2 us (33%)
  waiting for transfers between devices  18.3 us (22%)
  local copies, waits for them, and re-layouts  4.16 us (5%)
    pallas_call x2, Pallas kernels, shards(): pl.pallas_call(functools.partial(inner_kernel, absorb, strip_of, strips),...  17.4 us
    ppermute x9, starting transfers between devices, shards(): pieces[k] = lax.ppermute(pieces[k], 'depth', pairs)  11.6 us
    ppermute x9, waiting for transfers between devices, shards(): pieces[k] = lax.ppermute(pieces[k], 'depth', pairs)  10.7 us
    pallas_call x3, Pallas kernels, shards(): pl.pallas_call(functools.partial(outer_kernel, absorb, inner, strip_of, s...  8.21 us
    ppermute x1, starting transfers between devices, shards(): prev = lax.ppermute(volume[slices - 1], 'depth', depth_up)  4.59 us
    ppermute x1, starting transfers between devices, shards(): above = lax.ppermute(volume[:, rows - 1, :], 'tile', row_up)  4.51 us
    pallas_call x3, Pallas kernels, shards(): pl.pallas_call(functools.partial(frame_kernel, inner, frame is not None),...  4.31 us
    ppermute x3, starting transfers between devices, shards(): sides[k] = lax.ppermute(sides[k], 'depth', pairs)  4.03 us
  transfers between devices with their start and end apart: 16, of which 5 were waited for; matrix products, arithmetic and copies ran while one was open for 2% of the time, Pallas kernels for 33%

profile of v2, /device:TPU:1, one launch (start us, length us, event | category | flops | bytes accessed | tf_op | source)
XLA Modules:
  0.0 83.4 jit_solution(619431657685218027)
XLA Ops:
  0.0 1.3 %slice_bitcast_fusion = (bf16[64,4096]{1,0:T(8,128)(2,1)S(1)}, bf16[64,4096]{1,0:T(8,128)(2,1)S(1)}) fusion(bf16[8,64,4096]{2,1,0:T(8,128)(2,1)} %refs_5_.5), kind=kLoop, calls=%fused_computation | loop fusion | bytes 2097152 | tf_op jit(solution)/shard_map/squeeze | solution.py:350
  1.3 1.3 %collective-permute-start.1 = (bf16[64,4096]{1,0:T(8,128)(2,1)S(1)}, bf16[64,4096]{1,0:T(8,128)(2,1)S(1)}, u32[]{:S(2)}, u32[]{:S(2)}) collective-permute-start(bf16[64,4096]{1,0:T(8,128)(2,1)S(1)} %get-tuple-element.43), channel_id=1, source_target_pairs={{4,0},{8,4},{12,8},{16,12},{20,16},{24,20},{28,24},{5,1},{9,5},{13... | collective-permute-start | bytes 1572872 | tf_op jit(solution)/shard_map/ppermute | solution.py:350
  2.6 4.6 %collective-permute-start = (bf16[64,4096]{1,0:T(8,128)(2,1)S(1)}, bf16[64,4096]{1,0:T(8,128)(2,1)S(1)}, u32[]{:S(2)}, u32[]{:S(2)}) collective-permute-start(bf16[64,4096]{1,0:T(8,128)(2,1)S(1)} %get-tuple-element.44), channel_id=1, source_target_pairs={{0,4},{4,8},{8,12},{12,16},{16,20},{20,24},{24,28},{1,5},{5,9},{9,... | collective-permute-start | bytes 1572872 | tf_op jit(solution)/shard_map/ppermute | solution.py:349
  7.2 1.4 %fusion = (bf16[8,1,4096]{2,1,0:T(2,128)(2,1)S(1)}, bf16[8,1,4096]{2,1,0:T(2,128)(2,1)S(1)}) fusion(bf16[8,64,4096]{2,1,0:T(8,128)(2,1)} %refs_5_.5), kind=kLoop, calls=%fused_computation.4 | loop fusion | bytes 262144 | tf_op jit(solution)/shard_map/slice | solution.py:352
  8.6 0.1 copy.13
  8.7 4.5 %collective-permute-start.6 = (bf16[8,4096]{1,0:T(8,128)(2,1)S(1)}, bf16[8,4096]{1,0:T(8,128)(2,1)S(1)}, u32[]{:S(2)}, u32[]{:S(2)}) collective-permute-start(bf16[8,4096]{1,0:T(8,128)(2,1)S(1)} %bitcast.10), channel_id=1, source_target_pairs={{0,1},{1,2},{2,3},{4,5},{5,6},{6,7},{8,9},{9,10},{10,11},{12,13},{... | collective-permute-start | bytes 196616 | tf_op jit(solution)/shard_map/ppermute | solution.py:351
  13.2 0.1 copy.12
  13.3 0.0 copy-start
  13.3 2.2 %collective-permute-start.7 = (bf16[8,4096]{1,0:T(8,128)(2,1)S(1)}, bf16[8,4096]{1,0:T(8,128)(2,1)S(1)}, u32[]{:S(2)}, u32[]{:S(2)}) collective-permute-start(bf16[8,4096]{1,0:T(8,128)(2,1)S(1)} %bitcast.11), channel_id=1, source_target_pairs={{1,0},{2,1},{3,2},{5,4},{6,5},{7,6},{9,8},{10,9},{11,10},{13,12},{... | collective-permute-start | bytes 196616 | tf_op jit(solution)/shard_map/ppermute | solution.py:352
  15.5 0.0 collective-permute-done.6.refs_0_.refs_9_
  15.5 3.6 %collective-permute-done.7.refs_1_.refs_10_ = bf16[8,4096]{1,0:T(8,128)(2,1)S(1)} collective-permute-done((bf16[8,4096]{1,0:T(8,128)(2,1)S(1)}, bf16[8,4096]{1,0:T(8,128)(2,1)S(1)}, u32[]{:S(2)}, u32[]{:S(2)}) %collective-permute-start.7) | collective-permute-done | bytes 65568 | tf_op jit(solution)/shard_map/ppermute | solution.py:352
  19.1 0.7 copy-done.2
  19.8 0.7 copy-done.3
  20.4 8.8 %inner.3.refs_8_ = f32[4,32,4096]{2,1,0:T(8,128)S(1)} custom-call(s32[64]{0:T(128)S(1)} %copy-done.2, s32[1,2]{1,0:T(1,128)S(1)} %copy-done.3, bf16[8,64,4096]{2,1,0:T(8,128)(2,1)} %refs_5_.5, bf16[8,64,4096]{2,1,0:T(8,128)(2,1)} %refs_5_.5, bf16[8,64,4096]{2,1,0:T(8,128)(2,1)} %refs_5_.5, bf16[8,4096]{1,0:T(8,128)(2,1)S(1)} %collective-permute-done.6.refs_0_.refs_9_, ...), custom_call_target="tpu_custom_call" | custom-call | flops 104857600 | bytes 4194304 | tf_op jit(solution)/shard_map/inner/pallas_call | solution.py:381
  29.2 0.0 collective-permute-done.1.refs_7_
  29.2 0.0 collective-permute-done.refs_6_
  29.3 4.0 %outer.4 = (bf16[4,4,32,512]{3,2,1,0:T(8,128)(2,1)S(1)}, bf16[4,4,32,512]{3,2,1,0:T(8,128)(2,1)S(1)}) custom-call(s32[64]{0:T(128)S(1)} %copy-done.2, s32[1,2]{1,0:T(1,128)S(1)} %copy-done.3, bf16[8,64,4096]{2,1,0:T(8,128)(2,1)S(1)} %copy-done, bf16[8,64,4096]{2,1,0:T(8,128)(2,1)S(1)} %copy-done, bf16[8,64,4096]{2,1,0:T(8,128)(2,1)S(1)} %copy-done, ...), custom_call_target="tpu_custom_call" | custom-call | flops 52428800 | bytes 4194304 | tf_op jit(solution)/shard_map/outer/pallas_call | solution.py:405
  33.3 0.0 copy-start.1
  33.3 2.4 %collective-permute-start.8 = (bf16[4,4,32,512]{3,2,1,0:T(8,128)(2,1)S(1)}, bf16[4,4,32,512]{3,2,1,0:T(8,128)(2,1)S(1)}, u32[]{:S(2)}, u32[]{:S(2)}) collective-permute-start(bf16[4,4,32,512]{3,2,1,0:T(8,128)(2,1)S(1)} %get-tuple-element.30), channel_id=1, source_target_pairs={{0,4},{4,0},{8,12},{12,8},{16,20},{20,16},{24,28},{28,24},{1,5},{5... | collective-permute-start | bytes 1572872 | tf_op jit(solution)/shard_map/ppermute | solution.py:427
  35.7 8.6 %inner.2.refs_8_ = f32[4,32,4096]{2,1,0:T(8,128)S(1)} custom-call(s32[64]{0:T(128)S(1)} %copy-done.2, s32[1,2]{1,0:T(1,128)S(1)} %copy-done.3, bf16[8,64,4096]{2,1,0:T(8,128)(2,1)} %refs_5_.5, bf16[8,64,4096]{2,1,0:T(8,128)(2,1)} %refs_5_.5, bf16[8,64,4096]{2,1,0:T(8,128)(2,1)} %refs_5_.5), custom_call_target="tpu_custom_call" | custom-call | flops 104857600 | bytes 4194304 | tf_op jit(solution)/shard_map/inner/pallas_call | solution.py:381
  44.4 2.1 %outer.5 = (bf16[4,4,16,512]{3,2,1,0:T(8,128)(2,1)S(1)}, bf16[4,4,16,512]{3,2,1,0:T(8,128)(2,1)S(1)}) custom-call(s32[64]{0:T(128)S(1)} %copy-done.2, s32[1,2]{1,0:T(1,128)S(1)} %copy-done.3, bf16[8,64,4096]{2,1,0:T(8,128)(2,1)S(1)} %copy-done.1, bf16[8,64,4096]{2,1,0:T(8,128)(2,1)S(1)} %copy-done.1, bf16[8,64,4096]{2,1,0:T(8,128)(2,1)S(1)} %copy-done.1, ...), custom_call_target="tpu_custom_call" | custom-call | flops 26214400 | bytes 2097152 | tf_op jit(solution)/shard_map/outer/pallas_call | solution.py:405
  46.5 0.3 collective-permute-start.12
  46.8 2.1 %outer.3 = (bf16[4,4,16,512]{3,2,1,0:T(8,128)(2,1)S(1)}, bf16[4,4,16,512]{3,2,1,0:T(8,128)(2,1)S(1)}) custom-call(s32[64]{0:T(128)S(1)} %copy-done.2, s32[1,2]{1,0:T(1,128)S(1)} %copy-done.3, bf16[8,64,4096]{2,1,0:T(8,128)(2,1)S(1)} %copy-done.1, bf16[8,64,4096]{2,1,0:T(8,128)(2,1)S(1)} %copy-done.1, bf16[8,64,4096]{2,1,0:T(8,128)(2,1)S(1)} %copy-done.1, ...), custom_call_target="tpu_custom_call" | custom-call | flops 26214400 | bytes 2097152 | tf_op jit(solution)/shard_map/outer/pallas_call | solution.py:405
  48.9 1.3 %collective-permute-start.2 = (bf16[4,4,16,512]{3,2,1,0:T(8,128)(2,1)S(1)}, bf16[4,4,16,512]{3,2,1,0:T(8,128)(2,1)S(1)}, u32[]{:S(2)}, u32[]{:S(2)}) collective-permute-start(bf16[4,4,16,512]{3,2,1,0:T(8,128)(2,1)S(1)} %get-tuple-element.24), channel_id=1, source_target_pairs={{0,4},{4,0},{8,12},{12,8},{16,20},{20,16},{24,28},{28,24},{1,5},{5... | collective-permute-start | bytes 786440 | tf_op jit(solution)/shard_map/ppermute | solution.py:427
  50.2 3.9 %collective-permute-done.12.refs_1_ = bf16[4,4,16,512]{3,2,1,0:T(8,128)(2,1)S(1)} collective-permute-done((bf16[4,4,16,512]{3,2,1,0:T(8,128)(2,1)S(1)}, bf16[4,4,16,512]{3,2,1,0:T(8,128)(2,1)S(1)}, u32[]{:S(2)}, u32[]{:S(2)}) %collective-permute-start.12) | collective-permute-done | bytes 262176 | tf_op jit(solution)/shard_map/ppermute | solution.py:427
  54.1 0.8 group.5
  54.9 1.4 %collective-permute-start.13 = (s16[4,16,512]{2,1,0:T(8,128)(2,1)S(1)}, s16[4,16,512]{2,1,0:T(8,128)(2,1)S(1)}, u32[]{:S(2)}, u32[]{:S(2)}) collective-permute-start(s16[4,16,512]{2,1,0:T(8,128)(2,1)S(1)} %get-tuple-element.38), channel_id=1, source_target_pairs={{0,8},{4,12},{8,16},{12,20},{16,24},{20,28},{24,0},{28,4},{1,9},{5... | collective-permute-start | bytes 196616 | tf_op jit(solution)/shard_map/ppermute | solution.py:452
  56.3 0.0 collective-permute-done.8.refs_1_
  56.3 1.0 %group.4 = (s16[4,32,512]{2,1,0:T(8,128)(2,1)S(1)}, s16[4,32,512]{2,1,0:T(8,128)(2,1)S(1)}, s16[4,32,512]{2,1,0:T(8,128)(2,1)S(1)}, s16[4,32,512]{2,1,0:T(8,128)(2,1)S(1)}) custom-call(s32[64]{0:T(128)S(1)} %copy-done.2, bf16[4,4,32,512]{3,2,1,0:T(8,128)(2,1)S(1)} %get-tuple-element.29.refs_0_, bf16[4,4,32,512]{3,2,1,0:T(8,128)(2,1)S(1)} %collective-permute-done.8.refs_1_), custom_call_target="tpu_custom_call" | custom-call | flops 2621440 | bytes 2097152 | tf_op jit(solution)/shard_map/group/pallas_call | solution.py:434
  57.3 1.3 %collective-permute-start.9 = (s16[4,32,512]{2,1,0:T(8,128)(2,1)S(1)}, s16[4,32,512]{2,1,0:T(8,128)(2,1)S(1)}, u32[]{:S(2)}, u32[]{:S(2)}) collective-permute-start(s16[4,32,512]{2,1,0:T(8,128)(2,1)S(1)} %get-tuple-element.32), channel_id=1, source_target_pairs={{0,8},{4,12},{8,16},{12,20},{16,24},{20,28},{24,0},{28,4},{1,9},{5... | collective-permute-start | bytes 393224 | tf_op jit(solution)/shard_map/ppermute | solution.py:452
  58.6 1.0 %collective-permute-start.14 = (s16[4,16,512]{2,1,0:T(8,128)(2,1)S(1)}, s16[4,16,512]{2,1,0:T(8,128)(2,1)S(1)}, u32[]{:S(2)}, u32[]{:S(2)}) collective-permute-start(s16[4,16,512]{2,1,0:T(8,128)(2,1)S(1)} %get-tuple-element.39), channel_id=1, source_target_pairs={{0,16},{4,20},{8,24},{12,28},{16,0},{20,4},{24,8},{28,12},{1,17},{... | collective-permute-start | bytes 196616 | tf_op jit(solution)/shard_map/ppermute | solution.py:452
  59.6 1.2 %collective-permute-start.15 = (s16[4,16,512]{2,1,0:T(8,128)(2,1)S(1)}, s16[4,16,512]{2,1,0:T(8,128)(2,1)S(1)}, u32[]{:S(2)}, u32[]{:S(2)}) collective-permute-start(s16[4,16,512]{2,1,0:T(8,128)(2,1)S(1)} %get-tuple-element.40), channel_id=1, source_target_pairs={{0,24},{4,28},{8,0},{12,4},{16,8},{20,12},{24,16},{28,20},{1,25},{... | collective-permute-start | bytes 196616 | tf_op jit(solution)/shard_map/ppermute | solution.py:452
  60.9 0.0 collective-permute-done.2.refs_1_
  60.9 1.3 %collective-permute-start.10 = (s16[4,32,512]{2,1,0:T(8,128)(2,1)S(1)}, s16[4,32,512]{2,1,0:T(8,128)(2,1)S(1)}, u32[]{:S(2)}, u32[]{:S(2)}) collective-permute-start(s16[4,32,512]{2,1,0:T(8,128)(2,1)S(1)} %get-tuple-element.33), channel_id=1, source_target_pairs={{0,16},{4,20},{8,24},{12,28},{16,0},{20,4},{24,8},{28,12},{1,17},{... | collective-permute-start | bytes 393224 | tf_op jit(solution)/shard_map/ppermute | solution.py:452
  62.1 1.0 %collective-permute-start.11 = (s16[4,32,512]{2,1,0:T(8,128)(2,1)S(1)}, s16[4,32,512]{2,1,0:T(8,128)(2,1)S(1)}, u32[]{:S(2)}, u32[]{:S(2)}) collective-permute-start(s16[4,32,512]{2,1,0:T(8,128)(2,1)S(1)} %get-tuple-element.34), channel_id=1, source_target_pairs={{0,24},{4,28},{8,0},{12,4},{16,8},{20,12},{24,16},{28,20},{1,25},{... | collective-permute-start | bytes 393224 | tf_op jit(solution)/shard_map/ppermute | solution.py:452
  63.2 0.8 group.3
  64.0 5.5 %collective-permute-done.14.refs_2_ = s16[4,16,512]{2,1,0:T(8,128)(2,1)S(1)} collective-permute-done((s16[4,16,512]{2,1,0:T(8,128)(2,1)S(1)}, s16[4,16,512]{2,1,0:T(8,128)(2,1)S(1)}, u32[]{:S(2)}, u32[]{:S(2)}) %collective-permute-start.14) | collective-permute-done | bytes 65568 | tf_op jit(solution)/shard_map/ppermute | solution.py:452
  69.4 0.0 collective-permute-done.15.refs_3_
  69.4 0.8 %collective-permute-start.4 = (s16[4,16,512]{2,1,0:T(8,128)(2,1)S(1)}, s16[4,16,512]{2,1,0:T(8,128)(2,1)S(1)}, u32[]{:S(2)}, u32[]{:S(2)}) collective-permute-start(s16[4,16,512]{2,1,0:T(8,128)(2,1)S(1)} %get-tuple-element.27), channel_id=1, source_target_pairs={{0,16},{4,20},{8,24},{12,28},{16,0},{20,4},{24,8},{28,12},{1,17},{... | collective-permute-start | bytes 196616 | tf_op jit(solution)/shard_map/ppermute | solution.py:452
  70.3 0.0 collective-permute-done.9.refs_1_
  70.3 3.6 %collective-permute-start.5 = (s16[4,16,512]{2,1,0:T(8,128)(2,1)S(1)}, s16[4,16,512]{2,1,0:T(8,128)(2,1)S(1)}, u32[]{:S(2)}, u32[]{:S(2)}) collective-permute-start(s16[4,16,512]{2,1,0:T(8,128)(2,1)S(1)} %get-tuple-element.28), channel_id=1, source_target_pairs={{0,24},{4,28},{8,0},{12,4},{16,8},{20,12},{24,16},{28,20},{1,25},{... | collective-permute-start | bytes 196616 | tf_op jit(solution)/shard_map/ppermute | solution.py:452
  73.9 1.4 %frame.3.refs_4_ = f32[4,64,512]{2,1,0:T(8,128)} custom-call(s32[64]{0:T(128)S(1)} %copy-done.2, s16[4,16,512]{2,1,0:T(8,128)(2,1)S(1)} %get-tuple-element.37.refs_0_, s16[4,16,512]{2,1,0:T(8,128)(2,1)S(1)} %collective-permute-done.13.refs_1_, s16[4,16,512]{2,1,0:T(8,128)(2,1)S(1)} %collective-permute-done.14.refs_2_, ...), custom_call_target="tpu_custom_call" | custom-call | flops 163840 | bytes 2097152 | tf_op jit(solution)/shard_map/frame/pallas_call | solution.py:453
  75.2 1.2 %collective-permute-done.10.refs_2_ = s16[4,32,512]{2,1,0:T(8,128)(2,1)S(1)} collective-permute-done((s16[4,32,512]{2,1,0:T(8,128)(2,1)S(1)}, s16[4,32,512]{2,1,0:T(8,128)(2,1)S(1)}, u32[]{:S(2)}, u32[]{:S(2)}) %collective-permute-start.10) | collective-permute-done | bytes 131104 | tf_op jit(solution)/shard_map/ppermute | solution.py:452
  76.5 1.6 %frame.4.refs_4_ = f32[4,64,512]{2,1,0:T(8,128)} custom-call(s32[64]{0:T(128)S(1)} %copy-done.2, s16[4,32,512]{2,1,0:T(8,128)(2,1)S(1)} %get-tuple-element.31.refs_0_, s16[4,32,512]{2,1,0:T(8,128)(2,1)S(1)} %collective-permute-done.9.refs_1_, s16[4,32,512]{2,1,0:T(8,128)(2,1)S(1)} %collective-permute-done.10.refs_2_, ...), custom_call_target="tpu_custom_call", output_to_operand_aliasing={{}: (5, {})} | custom-call | flops 327680 | bytes 2097152 | tf_op jit(solution)/shard_map/frame/pallas_call | solution.py:453
  78.0 0.0 collective-permute-done.3.refs_1_
  78.0 4.0 %collective-permute-done.4.refs_2_ = s16[4,16,512]{2,1,0:T(8,128)(2,1)S(1)} collective-permute-done((s16[4,16,512]{2,1,0:T(8,128)(2,1)S(1)}, s16[4,16,512]{2,1,0:T(8,128)(2,1)S(1)}, u32[]{:S(2)}, u32[]{:S(2)}) %collective-permute-start.4) | collective-permute-done | bytes 65568 | tf_op jit(solution)/shard_map/ppermute | solution.py:452
  82.0 0.0 collective-permute-done.5.refs_3_
  82.0 1.4 %frame.5 = f32[4,64,512]{2,1,0:T(8,128)} custom-call(s32[64]{0:T(128)S(1)} %copy-done.2, s16[4,16,512]{2,1,0:T(8,128)(2,1)S(1)} %get-tuple-element.25.refs_0_, s16[4,16,512]{2,1,0:T(8,128)(2,1)S(1)} %collective-permute-done.3.refs_1_, s16[4,16,512]{2,1,0:T(8,128)(2,1)S(1)} %collective-permute-done.4.refs_2_, ...), custom_call_target="tpu_custom_call", output_to_operand_aliasing={{}: (5, {})} | custom-call | flops 163840 | bytes 2097152 | tf_op jit(solution)/shard_map/frame/pallas_call | solution.py:453
  (7 shorter events, 0.0 us)
Async XLA Ops:
  1.3 28.0 %collective-permute-start.1 = (bf16[64,4096]{1,0:T(8,128)(2,1)S(1)}, bf16[64,4096]{1,0:T(8,128)(2,1)S(1)}, u32[]{:S(2)}, u32[]{:S(2)}) collective-permute-start(bf16[64,4096]{1,0:T(8,128)(2,1)S(1)} %get-tuple-element.43), channel_id=1, source_target_pairs={{4,0},{8,4},{12,8},{16,12},{20,16},{24,20},{28,24},{5,1},{9,5},{13... | collective-permute-start | bytes 1572872 | tf_op jit(solution)/shard_map/ppermute | solution.py:350
  2.6 26.7 %collective-permute-start = (bf16[64,4096]{1,0:T(8,128)(2,1)S(1)}, bf16[64,4096]{1,0:T(8,128)(2,1)S(1)}, u32[]{:S(2)}, u32[]{:S(2)}) collective-permute-start(bf16[64,4096]{1,0:T(8,128)(2,1)S(1)} %get-tuple-element.44), channel_id=1, source_target_pairs={{0,4},{4,8},{8,12},{12,16},{16,20},{20,24},{24,28},{1,5},{5,9},{9,... | collective-permute-start | bytes 1572872 | tf_op jit(solution)/shard_map/ppermute | solution.py:349
  8.7 6.8 %collective-permute-start.6 = (bf16[8,4096]{1,0:T(8,128)(2,1)S(1)}, bf16[8,4096]{1,0:T(8,128)(2,1)S(1)}, u32[]{:S(2)}, u32[]{:S(2)}) collective-permute-start(bf16[8,4096]{1,0:T(8,128)(2,1)S(1)} %bitcast.10), channel_id=1, source_target_pairs={{0,1},{1,2},{2,3},{4,5},{5,6},{6,7},{8,9},{9,10},{10,11},{12,13},{... | collective-permute-start | bytes 196616 | tf_op jit(solution)/shard_map/ppermute | solution.py:351
  13.3 16.0 %copy-start = (bf16[8,64,4096]{2,1,0:T(8,128)(2,1)S(1)}, bf16[8,64,4096]{2,1,0:T(8,128)(2,1)}, u32[]{:S(2)}) copy-start(bf16[8,64,4096]{2,1,0:T(8,128)(2,1)} %refs_5_.5) | copy-start | bytes 12582916
  13.3 5.8 %collective-permute-start.7 = (bf16[8,4096]{1,0:T(8,128)(2,1)S(1)}, bf16[8,4096]{1,0:T(8,128)(2,1)S(1)}, u32[]{:S(2)}, u32[]{:S(2)}) collective-permute-start(bf16[8,4096]{1,0:T(8,128)(2,1)S(1)} %bitcast.11), channel_id=1, source_target_pairs={{1,0},{2,1},{3,2},{5,4},{6,5},{7,6},{9,8},{10,9},{11,10},{13,12},{... | collective-permute-start | bytes 196616 | tf_op jit(solution)/shard_map/ppermute | solution.py:352
  19.1 0.7 copy-start.2
  19.8 0.7 copy-start.3
  33.3 11.1 %copy-start.1 = (bf16[8,64,4096]{2,1,0:T(8,128)(2,1)S(1)}, bf16[8,64,4096]{2,1,0:T(8,128)(2,1)}, u32[]{:S(2)}) copy-start(bf16[8,64,4096]{2,1,0:T(8,128)(2,1)} %refs_5_.5) | copy-start | bytes 12582916
  33.3 23.0 %collective-permute-start.8 = (bf16[4,4,32,512]{3,2,1,0:T(8,128)(2,1)S(1)}, bf16[4,4,32,512]{3,2,1,0:T(8,128)(2,1)S(1)}, u32[]{:S(2)}, u32[]{:S(2)}) collective-permute-start(bf16[4,4,32,512]{3,2,1,0:T(8,128)(2,1)S(1)} %get-tuple-element.30), channel_id=1, source_target_pairs={{0,4},{4,0},{8,12},{12,8},{16,20},{20,16},{24,28},{28,24},{1,5},{5... | collective-permute-start | bytes 1572872 | tf_op jit(solution)/shard_map/ppermute | solution.py:427
  46.5 7.6 %collective-permute-start.12 = (bf16[4,4,16,512]{3,2,1,0:T(8,128)(2,1)S(1)}, bf16[4,4,16,512]{3,2,1,0:T(8,128)(2,1)S(1)}, u32[]{:S(2)}, u32[]{:S(2)}) collective-permute-start(bf16[4,4,16,512]{3,2,1,0:T(8,128)(2,1)S(1)} %get-tuple-element.36), channel_id=1, source_target_pairs={{0,4},{4,0},{8,12},{12,8},{16,20},{20,16},{24,28},{28,24},{1,5},{5... | collective-permute-start | bytes 786440 | tf_op jit(solution)/shard_map/ppermute | solution.py:427
  48.9 12.0 %collective-permute-start.2 = (bf16[4,4,16,512]{3,2,1,0:T(8,128)(2,1)S(1)}, bf16[4,4,16,512]{3,2,1,0:T(8,128)(2,1)S(1)}, u32[]{:S(2)}, u32[]{:S(2)}) collective-permute-start(bf16[4,4,16,512]{3,2,1,0:T(8,128)(2,1)S(1)} %get-tuple-element.24), channel_id=1, source_target_pairs={{0,4},{4,0},{8,12},{12,8},{16,20},{20,16},{24,28},{28,24},{1,5},{5... | collective-permute-start | bytes 786440 | tf_op jit(solution)/shard_map/ppermute | solution.py:427
  54.9 7.2 %collective-permute-start.13 = (s16[4,16,512]{2,1,0:T(8,128)(2,1)S(1)}, s16[4,16,512]{2,1,0:T(8,128)(2,1)S(1)}, u32[]{:S(2)}, u32[]{:S(2)}) collective-permute-start(s16[4,16,512]{2,1,0:T(8,128)(2,1)S(1)} %get-tuple-element.38), channel_id=1, source_target_pairs={{0,8},{4,12},{8,16},{12,20},{16,24},{20,28},{24,0},{28,4},{1,9},{5... | collective-permute-start | bytes 196616 | tf_op jit(solution)/shard_map/ppermute | solution.py:452
  57.3 13.0 %collective-permute-start.9 = (s16[4,32,512]{2,1,0:T(8,128)(2,1)S(1)}, s16[4,32,512]{2,1,0:T(8,128)(2,1)S(1)}, u32[]{:S(2)}, u32[]{:S(2)}) collective-permute-start(s16[4,32,512]{2,1,0:T(8,128)(2,1)S(1)} %get-tuple-element.32), channel_id=1, source_target_pairs={{0,8},{4,12},{8,16},{12,20},{16,24},{20,28},{24,0},{28,4},{1,9},{5... | collective-permute-start | bytes 393224 | tf_op jit(solution)/shard_map/ppermute | solution.py:452
  58.6 10.8 %collective-permute-start.14 = (s16[4,16,512]{2,1,0:T(8,128)(2,1)S(1)}, s16[4,16,512]{2,1,0:T(8,128)(2,1)S(1)}, u32[]{:S(2)}, u32[]{:S(2)}) collective-permute-start(s16[4,16,512]{2,1,0:T(8,128)(2,1)S(1)} %get-tuple-element.39), channel_id=1, source_target_pairs={{0,16},{4,20},{8,24},{12,28},{16,0},{20,4},{24,8},{28,12},{1,17},{... | collective-permute-start | bytes 196616 | tf_op jit(solution)/shard_map/ppermute | solution.py:452
  59.6 9.8 %collective-permute-start.15 = (s16[4,16,512]{2,1,0:T(8,128)(2,1)S(1)}, s16[4,16,512]{2,1,0:T(8,128)(2,1)S(1)}, u32[]{:S(2)}, u32[]{:S(2)}) collective-permute-start(s16[4,16,512]{2,1,0:T(8,128)(2,1)S(1)} %get-tuple-element.40), channel_id=1, source_target_pairs={{0,24},{4,28},{8,0},{12,4},{16,8},{20,12},{24,16},{28,20},{1,25},{... | collective-permute-start | bytes 196616 | tf_op jit(solution)/shard_map/ppermute | solution.py:452
  60.9 15.6 %collective-permute-start.10 = (s16[4,32,512]{2,1,0:T(8,128)(2,1)S(1)}, s16[4,32,512]{2,1,0:T(8,128)(2,1)S(1)}, u32[]{:S(2)}, u32[]{:S(2)}) collective-permute-start(s16[4,32,512]{2,1,0:T(8,128)(2,1)S(1)} %get-tuple-element.33), channel_id=1, source_target_pairs={{0,16},{4,20},{8,24},{12,28},{16,0},{20,4},{24,8},{28,12},{1,17},{... | collective-permute-start | bytes 393224 | tf_op jit(solution)/shard_map/ppermute | solution.py:452
  62.1 14.3 %collective-permute-start.11 = (s16[4,32,512]{2,1,0:T(8,128)(2,1)S(1)}, s16[4,32,512]{2,1,0:T(8,128)(2,1)S(1)}, u32[]{:S(2)}, u32[]{:S(2)}) collective-permute-start(s16[4,32,512]{2,1,0:T(8,128)(2,1)S(1)} %get-tuple-element.34), channel_id=1, source_target_pairs={{0,24},{4,28},{8,0},{12,4},{16,8},{20,12},{24,16},{28,20},{1,25},{... | collective-permute-start | bytes 393224 | tf_op jit(solution)/shard_map/ppermute | solution.py:452
  69.4 8.6 %collective-permute-start.3 = (s16[4,16,512]{2,1,0:T(8,128)(2,1)S(1)}, s16[4,16,512]{2,1,0:T(8,128)(2,1)S(1)}, u32[]{:S(2)}, u32[]{:S(2)}) collective-permute-start(s16[4,16,512]{2,1,0:T(8,128)(2,1)S(1)} %get-tuple-element.26), channel_id=1, source_target_pairs={{0,8},{4,12},{8,16},{12,20},{16,24},{20,28},{24,0},{28,4},{1,9},{5... | collective-permute-start | bytes 196616 | tf_op jit(solution)/shard_map/ppermute | solution.py:452
  69.4 12.6 %collective-permute-start.4 = (s16[4,16,512]{2,1,0:T(8,128)(2,1)S(1)}, s16[4,16,512]{2,1,0:T(8,128)(2,1)S(1)}, u32[]{:S(2)}, u32[]{:S(2)}) collective-permute-start(s16[4,16,512]{2,1,0:T(8,128)(2,1)S(1)} %get-tuple-element.27), channel_id=1, source_target_pairs={{0,16},{4,20},{8,24},{12,28},{16,0},{20,4},{24,8},{28,12},{1,17},{... | collective-permute-start | bytes 196616 | tf_op jit(solution)/shard_map/ppermute | solution.py:452
  70.3 11.8 %collective-permute-start.5 = (s16[4,16,512]{2,1,0:T(8,128)(2,1)S(1)}, s16[4,16,512]{2,1,0:T(8,128)(2,1)S(1)}, u32[]{:S(2)}, u32[]{:S(2)}) collective-permute-start(s16[4,16,512]{2,1,0:T(8,128)(2,1)S(1)} %get-tuple-element.28), channel_id=1, source_target_pairs={{0,24},{4,28},{8,0},{12,4},{16,8},{20,12},{24,16},{28,20},{1,25},{... | collective-permute-start | bytes 196616 | tf_op jit(solution)/shard_map/ppermute | solution.py:452

commit v3 on v2

--- a/solution.py
+++ b/solution.py
@@ -279,25 +279,25 @@
 
 
 def group_kernel(inner, shear, *refs):
-    sources, outs = refs[:inner], refs[inner:]
+    groups = lax.axis_size("depth") // inner
+    sources, outs = refs[:-groups], refs[-groups:]
     me = lax.axis_index("depth")
     flip = shear[0] > shear[shear.shape[0] - 1]
-    groups = len(outs)
 
     def body(order):
-        def step(i, carry):
-            at = pl.ds(pl.multiple_of(i * ROWS, ROWS), ROWS)
+        for part in range(len(sources) // inner):
+            at = slice(part * ROWS, (part + 1) * ROWS)
             for k in range(groups):
                 target = lax.rem(lax.div(me, inner) + k, groups)
                 pieces = [
-                    [sources[shift][target, c, at, :].astype(jnp.float32) for c in range(4)]
+                    [
+                        sources[part * inner + shift][target, c].astype(jnp.float32)
+                        for c in range(4)
+                    ]
                     for shift in order
                 ]
                 for c, value in enumerate(over(pieces)):
                     outs[k][c, at, :] = encode(value)
-            return carry
-
-        lax.fori_loop(0, outs[0].shape[1] // ROWS, step, 0)
 
     ordered(inner, lax.rem(me, inner), flip, body)
 
@@ -338,13 +338,9 @@
     depth_up, depth_down = line(bricks)
     row_up, row_down = line(crosswise)
 
-    batches = [(1, 1, strips - 2)] if strips > 2 else []
-    batches += [(0, max(strips - 1, 1), min(strips, 2))]
-    parts = [(*batches[-1], len(batches) - 1, 0)]
-    if strips > 2:
-        parts.insert(0, (1, 1, 1, 0, 0))
-    if strips > 3:
-        parts.append((2, 1, strips - 3, 0, 1))
+    batches = [(1, strips - 2)] if strips > 2 else []
+    batches += [(s, 1) for s in sorted({0, strips - 1})]
+    parts = [(s, b, i) for b, (first, n) in enumerate(batches) for i, s in enumerate(range(first, first + n))]
 
     prev = lax.ppermute(volume[slices - 1], "depth", depth_up)
     nxt = lax.ppermute(volume[0], "depth", depth_down)
@@ -375,9 +371,9 @@
         )
 
     mids = []
-    for first, step, count in batches:
-        strip_of = lambda i, first=first, step=step: first + step * i
-        edges = [above, below] if first == 0 else []
+    for first, count in batches:
+        strip_of = lambda i, first=first: first + i
+        edges = [above, below] if first == 0 or first + count == strips else []
         mid = pl.pallas_call(
             functools.partial(inner_kernel, absorb, strip_of, strips),
             out_shape=jax.ShapeDtypeStruct((4, count * ROWS, ny), jnp.float32),
@@ -395,11 +391,11 @@
         mids.append(mid)
 
     received = []
-    for first, step, count, batch, place in parts:
-        chunk = count * ROWS
-        strip_of = lambda i, first=first, step=step: first + step * i
-        edges = [above, below] if first == 0 else []
-        flat = pl.BlockSpec((ROWS, ny), lambda i, strip_of=strip_of: (strip_of(i), 0))
+    count, chunk = 1, ROWS
+    for first, batch, place in parts:
+        strip_of = lambda i, first=first: first + i
+        edges = [above, below] if first in (0, strips - 1) else []
+        flat = pl.BlockSpec((ROWS, ny), lambda i, first=first: (first + i, 0))
         ends = [(2, 0, 0), (2, slices // 2 - 1, 0)]
         ends += [(1, s, move) for s in (0, slices - 1) for move in (-1, 1)]
         sides = pl.pallas_call(
@@ -428,13 +424,16 @@
         received.append(sides)
 
     frame = None
-    for number, sides in enumerate(received):
-        first, step, count, _, _ = parts[number]
+    middle = max(strips - 2, 0)
+    stages = ([range(middle)] if middle else []) + [[n] for n in range(middle, len(parts))]
+    for stage in stages:
+        first, count = parts[stage[0]][0], len(stage)
         chunk = count * ROWS
+        sides = [side for n in stage for side in received[n]]
         pieces = pl.pallas_call(
             functools.partial(group_kernel, inner),
             out_shape=[jax.ShapeDtypeStruct((4, chunk, width), LINK)] * groups,
-            in_specs=[smem] + [vmem] * inner,
+            in_specs=[smem] + [vmem] * len(sides),
             out_specs=[vmem] * groups,
             cost_estimate=pl.CostEstimate(
                 flops=20 * chunk * ny, bytes_accessed=2 << 20, transcendentals=0
@@ -458,7 +457,7 @@
             + [vmem] * groups
             + [anywhere] * (frame is not None),
             out_specs=pl.BlockSpec(
-                (4, ROWS, width), lambda i, first=first, step=step: (0, first + step * i, 0)
+                (4, ROWS, width), lambda i, first=first: (0, first + i, 0)
             ),
             input_output_aliases={} if frame is None else {1 + groups: 0},
             cost_estimate=pl.CostEstimate(

time: 85 us -> 81.5 us (0.959)
  waiting for transfers between devices: 18.3 us -> 15 us
  starting transfers between devices: 28.2 us -> 29.4 us
    ppermute x3 -> x4, waiting for transfers between devices: 3.93 us -> 0.01 us  [shards(): sides[k] = lax.ppermute(sides[k], 'depth', pairs)]
    ppermute x1, waiting for transfers between devices: 3.65 us -> 0.01 us  [shards(): below = lax.ppermute(volume[:, 0, :], 'tile', row_down)]
    ppermute x1, waiting for transfers between devices: 0.01 us -> 2.73 us  [shards(): prev = lax.ppermute(volume[slices - 1], 'depth', depth_up)]
    ppermute x9, starting transfers between devices: 11.6 us -> 14 us  [shards(): pieces[k] = lax.ppermute(pieces[k], 'depth', pairs)]
    ppermute x9, waiting for transfers between devices: 10.7 us -> 12.2 us  [shards(): pieces[k] = lax.ppermute(pieces[k], 'depth', pairs)]
    pallas_call x2 -> x3, Pallas kernels: 17.4 us -> 16.8 us  [shards(): pl.pallas_call(functools.partial(inner_kernel, absorb, strip_of, strips),...]
    pallas_call x3 -> x4, Pallas kernels: 8.21 us -> 8.4 us  [shards(): pl.pallas_call(functools.partial(outer_kernel, absorb, inner, strip_of, s...]
    ppermute x3 -> x4, starting transfers between devices: 4.03 us -> 3.95 us  [shards(): sides[k] = lax.ppermute(sides[k], 'depth', pairs)]
  transfers between devices with their start and end apart: 16 -> 17, of which waited for: 5 -> 3; matrix products, arithmetic and copies ran while one was open for 2% -> 2% of each run, Pallas kernels for 33% -> 38%
where the time goes in v3:
time: 81.5 us; the launch traced here: 80.7 us
  Pallas kernels  32.1 us (39%)
  starting transfers between devices  29.4 us (36%)
  waiting for transfers between devices  15 us (18%)
  local copies, waits for them, and re-layouts  4.15 us (5%)
    pallas_call x3, Pallas kernels, shards(): pl.pallas_call(functools.partial(inner_kernel, absorb, strip_of, strips),...  16.8 us
    ppermute x9, starting transfers between devices, shards(): pieces[k] = lax.ppermute(pieces[k], 'depth', pairs)  14 us
    ppermute x9, waiting for transfers between devices, shards(): pieces[k] = lax.ppermute(pieces[k], 'depth', pairs)  12.2 us
    pallas_call x4, Pallas kernels, shards(): pl.pallas_call(functools.partial(outer_kernel, absorb, inner, strip_of, s...  8.4 us
    pallas_call x3, Pallas kernels, shards(): pl.pallas_call(functools.partial(frame_kernel, inner, frame is not None),...  4.33 us
    ppermute x1, starting transfers between devices, shards(): above = lax.ppermute(volume[:, rows - 1, :], 'tile', row_up)  3.99 us
    ppermute x1, starting transfers between devices, shards(): prev = lax.ppermute(volume[slices - 1], 'depth', depth_up)  3.97 us
    ppermute x4, starting transfers between devices, shards(): sides[k] = lax.ppermute(sides[k], 'depth', pairs)  3.95 us
  transfers between devices with their start and end apart: 17, of which 3 were waited for; matrix products, arithmetic and copies ran while one was open for 2% of the time, Pallas kernels for 38%

profile of v3, /device:TPU:1, one launch (start us, length us, event | category | flops | bytes accessed | tf_op | source)
XLA Modules:
  0.0 80.7 jit_solution(410952392958230762)
XLA Ops:
  0.0 1.3 %slice_bitcast_fusion = (bf16[64,4096]{1,0:T(8,128)(2,1)S(1)}, bf16[64,4096]{1,0:T(8,128)(2,1)S(1)}) fusion(bf16[8,64,4096]{2,1,0:T(8,128)(2,1)} %refs_5_.7), kind=kLoop, calls=%fused_computation | loop fusion | bytes 2097152 | tf_op jit(solution)/shard_map/squeeze | solution.py:346
  1.3 4.0 %collective-permute-start = (bf16[64,4096]{1,0:T(8,128)(2,1)S(1)}, bf16[64,4096]{1,0:T(8,128)(2,1)S(1)}, u32[]{:S(2)}, u32[]{:S(2)}) collective-permute-start(bf16[64,4096]{1,0:T(8,128)(2,1)S(1)} %get-tuple-element.48), channel_id=1, source_target_pairs={{0,4},{4,8},{8,12},{12,16},{16,20},{20,24},{24,28},{1,5},{5,9},{9,... | collective-permute-start | bytes 1572872 | tf_op jit(solution)/shard_map/ppermute | solution.py:345
  5.2 1.3 %collective-permute-start.1 = (bf16[64,4096]{1,0:T(8,128)(2,1)S(1)}, bf16[64,4096]{1,0:T(8,128)(2,1)S(1)}, u32[]{:S(2)}, u32[]{:S(2)}) collective-permute-start(bf16[64,4096]{1,0:T(8,128)(2,1)S(1)} %get-tuple-element.47), channel_id=1, source_target_pairs={{4,0},{8,4},{12,8},{16,12},{20,16},{24,20},{28,24},{5,1},{9,5},{13... | collective-permute-start | bytes 1572872 | tf_op jit(solution)/shard_map/ppermute | solution.py:346
  6.5 1.4 %fusion = (bf16[8,1,4096]{2,1,0:T(2,128)(2,1)S(1)}, bf16[8,1,4096]{2,1,0:T(2,128)(2,1)S(1)}) fusion(bf16[8,64,4096]{2,1,0:T(8,128)(2,1)} %refs_5_.7), kind=kLoop, calls=%fused_computation.4 | loop fusion | bytes 262144 | tf_op jit(solution)/shard_map/slice | solution.py:348
  8.0 0.1 copy.13
  8.0 4.0 %collective-permute-start.2 = (bf16[8,4096]{1,0:T(8,128)(2,1)S(1)}, bf16[8,4096]{1,0:T(8,128)(2,1)S(1)}, u32[]{:S(2)}, u32[]{:S(2)}) collective-permute-start(bf16[8,4096]{1,0:T(8,128)(2,1)S(1)} %bitcast.10), channel_id=1, source_target_pairs={{0,1},{1,2},{2,3},{4,5},{5,6},{6,7},{8,9},{9,10},{10,11},{12,13},{... | collective-permute-start | bytes 196616 | tf_op jit(solution)/shard_map/ppermute | solution.py:347
  12.0 0.1 copy.12
  12.1 0.0 copy-start
  12.1 2.2 %collective-permute-start.3 = (bf16[8,4096]{1,0:T(8,128)(2,1)S(1)}, bf16[8,4096]{1,0:T(8,128)(2,1)S(1)}, u32[]{:S(2)}, u32[]{:S(2)}) collective-permute-start(bf16[8,4096]{1,0:T(8,128)(2,1)S(1)} %bitcast.11), channel_id=1, source_target_pairs={{1,0},{2,1},{3,2},{5,4},{6,5},{7,6},{9,8},{10,9},{11,10},{13,12},{... | collective-permute-start | bytes 196616 | tf_op jit(solution)/shard_map/ppermute | solution.py:348
  14.3 0.0 copy-start.1
  14.3 0.6 copy-done.1
  15.0 0.7 copy-done.2
  15.6 8.7 %inner.5.refs_8_ = f32[4,32,4096]{2,1,0:T(8,128)S(1)} custom-call(s32[64]{0:T(128)S(1)} %copy-done.1, s32[1,2]{1,0:T(1,128)S(1)} %copy-done.2, bf16[8,64,4096]{2,1,0:T(8,128)(2,1)} %refs_5_.7, bf16[8,64,4096]{2,1,0:T(8,128)(2,1)} %refs_5_.7, bf16[8,64,4096]{2,1,0:T(8,128)(2,1)} %refs_5_.7), custom_call_target="tpu_custom_call" | custom-call | flops 104857600 | bytes 4194304 | tf_op jit(solution)/shard_map/inner/pallas_call | solution.py:377
  24.3 2.7 %collective-permute-done.refs_6_ = bf16[64,4096]{1,0:T(8,128)(2,1)S(1)} collective-permute-done((bf16[64,4096]{1,0:T(8,128)(2,1)S(1)}, bf16[64,4096]{1,0:T(8,128)(2,1)S(1)}, u32[]{:S(2)}, u32[]{:S(2)}) %collective-permute-start) | collective-permute-done | bytes 524320 | tf_op jit(solution)/shard_map/ppermute | solution.py:345
  27.0 0.0 collective-permute-done.1.refs_7_
  27.0 2.1 %outer.6 = (bf16[4,4,16,512]{3,2,1,0:T(8,128)(2,1)S(1)}, bf16[4,4,16,512]{3,2,1,0:T(8,128)(2,1)S(1)}) custom-call(s32[64]{0:T(128)S(1)} %copy-done.1, s32[1,2]{1,0:T(1,128)S(1)} %copy-done.2, bf16[8,64,4096]{2,1,0:T(8,128)(2,1)S(1)} %copy-done, bf16[8,64,4096]{2,1,0:T(8,128)(2,1)S(1)} %copy-done, bf16[8,64,4096]{2,1,0:T(8,128)(2,1)S(1)} %copy-done, ...), custom_call_target="tpu_custom_call" | custom-call | flops 26214400 | bytes 2097152 | tf_op jit(solution)/shard_map/outer/pallas_call | solution.py:401
  29.1 2.3 %collective-permute-start.12 = (bf16[4,4,16,512]{3,2,1,0:T(8,128)(2,1)S(1)}, bf16[4,4,16,512]{3,2,1,0:T(8,128)(2,1)S(1)}, u32[]{:S(2)}, u32[]{:S(2)}) collective-permute-start(bf16[4,4,16,512]{3,2,1,0:T(8,128)(2,1)S(1)} %get-tuple-element.38), channel_id=1, source_target_pairs={{0,4},{4,0},{8,12},{12,8},{16,20},{20,16},{24,28},{28,24},{1,5},{5... | collective-permute-start | bytes 786440 | tf_op jit(solution)/shard_map/ppermute | solution.py:423
  31.4 2.1 %outer.7 = (bf16[4,4,16,512]{3,2,1,0:T(8,128)(2,1)S(1)}, bf16[4,4,16,512]{3,2,1,0:T(8,128)(2,1)S(1)}) custom-call(s32[64]{0:T(128)S(1)} %copy-done.1, s32[1,2]{1,0:T(1,128)S(1)} %copy-done.2, bf16[8,64,4096]{2,1,0:T(8,128)(2,1)S(1)} %copy-done, bf16[8,64,4096]{2,1,0:T(8,128)(2,1)S(1)} %copy-done, bf16[8,64,4096]{2,1,0:T(8,128)(2,1)S(1)} %copy-done, ...), custom_call_target="tpu_custom_call" | custom-call | flops 26214400 | bytes 2097152 | tf_op jit(solution)/shard_map/outer/pallas_call | solution.py:401
  33.5 0.1 collective-permute-start.13
  33.6 0.0 collective-permute-done.2.refs_0_.refs_9_
  33.6 0.0 collective-permute-done.3.refs_1_.refs_10_
  33.6 4.1 %inner.4.refs_8_ = f32[4,16,4096]{2,1,0:T(8,128)S(1)} custom-call(s32[64]{0:T(128)S(1)} %copy-done.1, s32[1,2]{1,0:T(1,128)S(1)} %copy-done.2, bf16[8,64,4096]{2,1,0:T(8,128)(2,1)S(1)} %copy-done, bf16[8,64,4096]{2,1,0:T(8,128)(2,1)S(1)} %copy-done, bf16[8,64,4096]{2,1,0:T(8,128)(2,1)S(1)} %copy-done, ...), custom_call_target="tpu_custom_call" | custom-call | flops 52428800 | bytes 2097152 | tf_op jit(solution)/shard_map/inner/pallas_call | solution.py:377
  37.7 2.1 %outer.5 = (bf16[4,4,16,512]{3,2,1,0:T(8,128)(2,1)S(1)}, bf16[4,4,16,512]{3,2,1,0:T(8,128)(2,1)S(1)}) custom-call(s32[64]{0:T(128)S(1)} %copy-done.1, s32[1,2]{1,0:T(1,128)S(1)} %copy-done.2, bf16[8,64,4096]{2,1,0:T(8,128)(2,1)S(1)} %copy-done, bf16[8,64,4096]{2,1,0:T(8,128)(2,1)S(1)} %copy-done, bf16[8,64,4096]{2,1,0:T(8,128)(2,1)S(1)} %copy-done, ...), custom_call_target="tpu_custom_call" | custom-call | flops 26214400 | bytes 2097152 | tf_op jit(solution)/shard_map/outer/pallas_call | solution.py:401
  39.8 1.5 %collective-permute-start.8 = (bf16[4,4,16,512]{3,2,1,0:T(8,128)(2,1)S(1)}, bf16[4,4,16,512]{3,2,1,0:T(8,128)(2,1)S(1)}, u32[]{:S(2)}, u32[]{:S(2)}) collective-permute-start(bf16[4,4,16,512]{3,2,1,0:T(8,128)(2,1)S(1)} %get-tuple-element.32), channel_id=1, source_target_pairs={{0,4},{4,0},{8,12},{12,8},{16,20},{20,16},{24,28},{28,24},{1,5},{5... | collective-permute-start | bytes 786440 | tf_op jit(solution)/shard_map/ppermute | solution.py:423
  41.3 4.1 %inner.3.refs_8_ = f32[4,16,4096]{2,1,0:T(8,128)S(1)} custom-call(s32[64]{0:T(128)S(1)} %copy-done.1, s32[1,2]{1,0:T(1,128)S(1)} %copy-done.2, bf16[8,64,4096]{2,1,0:T(8,128)(2,1)S(1)} %copy-done, bf16[8,64,4096]{2,1,0:T(8,128)(2,1)S(1)} %copy-done, bf16[8,64,4096]{2,1,0:T(8,128)(2,1)S(1)} %copy-done, ...), custom_call_target="tpu_custom_call" | custom-call | flops 52428800 | bytes 2097152 | tf_op jit(solution)/shard_map/inner/pallas_call | solution.py:377
  45.3 2.1 %outer.4 = (bf16[4,4,16,512]{3,2,1,0:T(8,128)(2,1)S(1)}, bf16[4,4,16,512]{3,2,1,0:T(8,128)(2,1)S(1)}) custom-call(s32[64]{0:T(128)S(1)} %copy-done.1, s32[1,2]{1,0:T(1,128)S(1)} %copy-done.2, bf16[8,64,4096]{2,1,0:T(8,128)(2,1)S(1)} %copy-done, bf16[8,64,4096]{2,1,0:T(8,128)(2,1)S(1)} %copy-done, bf16[8,64,4096]{2,1,0:T(8,128)(2,1)S(1)} %copy-done, ...), custom_call_target="tpu_custom_call" | custom-call | flops 26214400 | bytes 2097152 | tf_op jit(solution)/shard_map/outer/pallas_call | solution.py:401
  47.5 0.1 collective-permute-start.4
  47.6 0.0 collective-permute-done.12.refs_1_
  47.6 0.0 collective-permute-done.13.refs_3_
  47.6 1.0 %group.5 = (s16[4,32,512]{2,1,0:T(8,128)(2,1)S(1)}, s16[4,32,512]{2,1,0:T(8,128)(2,1)S(1)}, s16[4,32,512]{2,1,0:T(8,128)(2,1)S(1)}, s16[4,32,512]{2,1,0:T(8,128)(2,1)S(1)}) custom-call(s32[64]{0:T(128)S(1)} %copy-done.1, bf16[4,4,16,512]{3,2,1,0:T(8,128)(2,1)S(1)} %get-tuple-element.37.refs_0_, bf16[4,4,16,512]{3,2,1,0:T(8,128)(2,1)S(1)} %collective-permute-done.12.refs_1_, ...), custom_call_target="tpu_custom_call" | custom-call | flops 2621440 | bytes 2097152 | tf_op jit(solution)/shard_map/group/pallas_call | solution.py:433
  48.6 3.5 %collective-permute-start.14 = (s16[4,32,512]{2,1,0:T(8,128)(2,1)S(1)}, s16[4,32,512]{2,1,0:T(8,128)(2,1)S(1)}, u32[]{:S(2)}, u32[]{:S(2)}) collective-permute-start(s16[4,32,512]{2,1,0:T(8,128)(2,1)S(1)} %get-tuple-element.42), channel_id=1, source_target_pairs={{0,8},{4,12},{8,16},{12,20},{16,24},{20,28},{24,0},{28,4},{1,9},{5... | collective-permute-start | bytes 393224 | tf_op jit(solution)/shard_map/ppermute | solution.py:451
  52.1 2.3 %collective-permute-start.15 = (s16[4,32,512]{2,1,0:T(8,128)(2,1)S(1)}, s16[4,32,512]{2,1,0:T(8,128)(2,1)S(1)}, u32[]{:S(2)}, u32[]{:S(2)}) collective-permute-start(s16[4,32,512]{2,1,0:T(8,128)(2,1)S(1)} %get-tuple-element.43), channel_id=1, source_target_pairs={{0,16},{4,20},{8,24},{12,28},{16,0},{20,4},{24,8},{28,12},{1,17},{... | collective-permute-start | bytes 393224 | tf_op jit(solution)/shard_map/ppermute | solution.py:451
  54.4 1.1 %collective-permute-start.16 = (s16[4,32,512]{2,1,0:T(8,128)(2,1)S(1)}, s16[4,32,512]{2,1,0:T(8,128)(2,1)S(1)}, u32[]{:S(2)}, u32[]{:S(2)}) collective-permute-start(s16[4,32,512]{2,1,0:T(8,128)(2,1)S(1)} %get-tuple-element.44), channel_id=1, source_target_pairs={{0,24},{4,28},{8,0},{12,4},{16,8},{20,12},{24,16},{28,20},{1,25},{... | collective-permute-start | bytes 393224 | tf_op jit(solution)/shard_map/ppermute | solution.py:451
  55.5 0.0 collective-permute-done.8.refs_1_
  55.5 0.8 group.4
  56.3 0.3 collective-permute-start.10
  56.5 3.3 %collective-permute-start.11 = (s16[4,16,512]{2,1,0:T(8,128)(2,1)S(1)}, s16[4,16,512]{2,1,0:T(8,128)(2,1)S(1)}, u32[]{:S(2)}, u32[]{:S(2)}) collective-permute-start(s16[4,16,512]{2,1,0:T(8,128)(2,1)S(1)} %get-tuple-element.36), channel_id=1, source_target_pairs={{0,24},{4,28},{8,0},{12,4},{16,8},{20,12},{24,16},{28,20},{1,25},{... | collective-permute-start | bytes 196616 | tf_op jit(solution)/shard_map/ppermute | solution.py:451
  59.8 0.8 group.3
  60.6 8.7 %collective-permute-done.10.refs_2_ = s16[4,16,512]{2,1,0:T(8,128)(2,1)S(1)} collective-permute-done((s16[4,16,512]{2,1,0:T(8,128)(2,1)S(1)}, s16[4,16,512]{2,1,0:T(8,128)(2,1)S(1)}, u32[]{:S(2)}, u32[]{:S(2)}) %collective-permute-start.10) | collective-permute-done | bytes 65568 | tf_op jit(solution)/shard_map/ppermute | solution.py:451
  69.3 0.0 collective-permute-done.15.refs_2_
  69.4 3.5 %collective-permute-start.6 = (s16[4,16,512]{2,1,0:T(8,128)(2,1)S(1)}, s16[4,16,512]{2,1,0:T(8,128)(2,1)S(1)}, u32[]{:S(2)}, u32[]{:S(2)}) collective-permute-start(s16[4,16,512]{2,1,0:T(8,128)(2,1)S(1)} %get-tuple-element.29), channel_id=1, source_target_pairs={{0,16},{4,20},{8,24},{12,28},{16,0},{20,4},{24,8},{28,12},{1,17},{... | collective-permute-start | bytes 196616 | tf_op jit(solution)/shard_map/ppermute | solution.py:451
  72.9 1.6 %frame.3.refs_4_ = f32[4,64,512]{2,1,0:T(8,128)} custom-call(s32[64]{0:T(128)S(1)} %copy-done.1, s16[4,32,512]{2,1,0:T(8,128)(2,1)S(1)} %get-tuple-element.41.refs_0_, s16[4,32,512]{2,1,0:T(8,128)(2,1)S(1)} %collective-permute-done.14.refs_1_, s16[4,32,512]{2,1,0:T(8,128)(2,1)S(1)} %collective-permute-done.15.refs_2_, ...), custom_call_target="tpu_custom_call" | custom-call | flops 327680 | bytes 2097152 | tf_op jit(solution)/shard_map/frame/pallas_call | solution.py:452
  74.5 0.0 collective-permute-done.9.refs_1_
  74.5 1.4 %frame.4.refs_4_ = f32[4,64,512]{2,1,0:T(8,128)} custom-call(s32[64]{0:T(128)S(1)} %copy-done.1, s16[4,16,512]{2,1,0:T(8,128)(2,1)S(1)} %get-tuple-element.33.refs_0_, s16[4,16,512]{2,1,0:T(8,128)(2,1)S(1)} %collective-permute-done.9.refs_1_, s16[4,16,512]{2,1,0:T(8,128)(2,1)S(1)} %collective-permute-done.10.refs_2_, ...), custom_call_target="tpu_custom_call", output_to_operand_aliasing={{}: (5, {})} | custom-call | flops 163840 | bytes 2097152 | tf_op jit(solution)/shard_map/frame/pallas_call | solution.py:452
  75.9 0.0 collective-permute-done.5.refs_1_
  75.9 3.5 %collective-permute-done.6.refs_2_ = s16[4,16,512]{2,1,0:T(8,128)(2,1)S(1)} collective-permute-done((s16[4,16,512]{2,1,0:T(8,128)(2,1)S(1)}, s16[4,16,512]{2,1,0:T(8,128)(2,1)S(1)}, u32[]{:S(2)}, u32[]{:S(2)}) %collective-permute-start.6) | collective-permute-done | bytes 65568 | tf_op jit(solution)/shard_map/ppermute | solution.py:451
  79.4 0.0 collective-permute-done.7.refs_3_
  79.4 1.4 %frame.5 = f32[4,64,512]{2,1,0:T(8,128)} custom-call(s32[64]{0:T(128)S(1)} %copy-done.1, s16[4,16,512]{2,1,0:T(8,128)(2,1)S(1)} %get-tuple-element.27.refs_0_, s16[4,16,512]{2,1,0:T(8,128)(2,1)S(1)} %collective-permute-done.5.refs_1_, s16[4,16,512]{2,1,0:T(8,128)(2,1)S(1)} %collective-permute-done.6.refs_2_, ...), custom_call_target="tpu_custom_call", output_to_operand_aliasing={{}: (5, {})} | custom-call | flops 163840 | bytes 2097152 | tf_op jit(solution)/shard_map/frame/pallas_call | solution.py:452
  (9 shorter events, 0.0 us)
Async XLA Ops:
  1.3 25.8 %collective-permute-start = (bf16[64,4096]{1,0:T(8,128)(2,1)S(1)}, bf16[64,4096]{1,0:T(8,128)(2,1)S(1)}, u32[]{:S(2)}, u32[]{:S(2)}) collective-permute-start(bf16[64,4096]{1,0:T(8,128)(2,1)S(1)} %get-tuple-element.48), channel_id=1, source_target_pairs={{0,4},{4,8},{8,12},{12,16},{16,20},{20,24},{24,28},{1,5},{5,9},{9,... | collective-permute-start | bytes 1572872 | tf_op jit(solution)/shard_map/ppermute | solution.py:345
  5.2 21.8 %collective-permute-start.1 = (bf16[64,4096]{1,0:T(8,128)(2,1)S(1)}, bf16[64,4096]{1,0:T(8,128)(2,1)S(1)}, u32[]{:S(2)}, u32[]{:S(2)}) collective-permute-start(bf16[64,4096]{1,0:T(8,128)(2,1)S(1)} %get-tuple-element.47), channel_id=1, source_target_pairs={{4,0},{8,4},{12,8},{16,12},{20,16},{24,20},{28,24},{5,1},{9,5},{13... | collective-permute-start | bytes 1572872 | tf_op jit(solution)/shard_map/ppermute | solution.py:346
  8.0 25.6 %collective-permute-start.2 = (bf16[8,4096]{1,0:T(8,128)(2,1)S(1)}, bf16[8,4096]{1,0:T(8,128)(2,1)S(1)}, u32[]{:S(2)}, u32[]{:S(2)}) collective-permute-start(bf16[8,4096]{1,0:T(8,128)(2,1)S(1)} %bitcast.10), channel_id=1, source_target_pairs={{0,1},{1,2},{2,3},{4,5},{5,6},{6,7},{8,9},{9,10},{10,11},{12,13},{... | collective-permute-start | bytes 196616 | tf_op jit(solution)/shard_map/ppermute | solution.py:347
  12.1 14.9 %copy-start = (bf16[8,64,4096]{2,1,0:T(8,128)(2,1)S(1)}, bf16[8,64,4096]{2,1,0:T(8,128)(2,1)}, u32[]{:S(2)}) copy-start(bf16[8,64,4096]{2,1,0:T(8,128)(2,1)} %refs_5_.7) | copy-start | bytes 12582916
  12.1 21.5 %collective-permute-start.3 = (bf16[8,4096]{1,0:T(8,128)(2,1)S(1)}, bf16[8,4096]{1,0:T(8,128)(2,1)S(1)}, u32[]{:S(2)}, u32[]{:S(2)}) collective-permute-start(bf16[8,4096]{1,0:T(8,128)(2,1)S(1)} %bitcast.11), channel_id=1, source_target_pairs={{1,0},{2,1},{3,2},{5,4},{6,5},{7,6},{9,8},{10,9},{11,10},{13,12},{... | collective-permute-start | bytes 196616 | tf_op jit(solution)/shard_map/ppermute | solution.py:348
  14.3 0.7 copy-start.1
  15.0 0.7 copy-start.2
  29.1 18.4 %collective-permute-start.12 = (bf16[4,4,16,512]{3,2,1,0:T(8,128)(2,1)S(1)}, bf16[4,4,16,512]{3,2,1,0:T(8,128)(2,1)S(1)}, u32[]{:S(2)}, u32[]{:S(2)}) collective-permute-start(bf16[4,4,16,512]{3,2,1,0:T(8,128)(2,1)S(1)} %get-tuple-element.38), channel_id=1, source_target_pairs={{0,4},{4,0},{8,12},{12,8},{16,20},{20,16},{24,28},{28,24},{1,5},{5... | collective-permute-start | bytes 786440 | tf_op jit(solution)/shard_map/ppermute | solution.py:423
  33.5 14.1 %collective-permute-start.13 = (bf16[4,4,16,512]{3,2,1,0:T(8,128)(2,1)S(1)}, bf16[4,4,16,512]{3,2,1,0:T(8,128)(2,1)S(1)}, u32[]{:S(2)}, u32[]{:S(2)}) collective-permute-start(bf16[4,4,16,512]{3,2,1,0:T(8,128)(2,1)S(1)} %get-tuple-element.40), channel_id=1, source_target_pairs={{0,4},{4,0},{8,12},{12,8},{16,20},{20,16},{24,28},{28,24},{1,5},{5... | collective-permute-start | bytes 786440 | tf_op jit(solution)/shard_map/ppermute | solution.py:423
  39.8 15.7 %collective-permute-start.8 = (bf16[4,4,16,512]{3,2,1,0:T(8,128)(2,1)S(1)}, bf16[4,4,16,512]{3,2,1,0:T(8,128)(2,1)S(1)}, u32[]{:S(2)}, u32[]{:S(2)}) collective-permute-start(bf16[4,4,16,512]{3,2,1,0:T(8,128)(2,1)S(1)} %get-tuple-element.32), channel_id=1, source_target_pairs={{0,4},{4,0},{8,12},{12,8},{16,20},{20,16},{24,28},{28,24},{1,5},{5... | collective-permute-start | bytes 786440 | tf_op jit(solution)/shard_map/ppermute | solution.py:423
  47.5 9.1 %collective-permute-start.4 = (bf16[4,4,16,512]{3,2,1,0:T(8,128)(2,1)S(1)}, bf16[4,4,16,512]{3,2,1,0:T(8,128)(2,1)S(1)}, u32[]{:S(2)}, u32[]{:S(2)}) collective-permute-start(bf16[4,4,16,512]{3,2,1,0:T(8,128)(2,1)S(1)} %get-tuple-element.26), channel_id=1, source_target_pairs={{0,4},{4,0},{8,12},{12,8},{16,20},{20,16},{24,28},{28,24},{1,5},{5... | collective-permute-start | bytes 786440 | tf_op jit(solution)/shard_map/ppermute | solution.py:423
  48.6 20.8 %collective-permute-start.14 = (s16[4,32,512]{2,1,0:T(8,128)(2,1)S(1)}, s16[4,32,512]{2,1,0:T(8,128)(2,1)S(1)}, u32[]{:S(2)}, u32[]{:S(2)}) collective-permute-start(s16[4,32,512]{2,1,0:T(8,128)(2,1)S(1)} %get-tuple-element.42), channel_id=1, source_target_pairs={{0,8},{4,12},{8,16},{12,20},{16,24},{20,28},{24,0},{28,4},{1,9},{5... | collective-permute-start | bytes 393224 | tf_op jit(solution)/shard_map/ppermute | solution.py:451
  52.1 17.3 %collective-permute-start.15 = (s16[4,32,512]{2,1,0:T(8,128)(2,1)S(1)}, s16[4,32,512]{2,1,0:T(8,128)(2,1)S(1)}, u32[]{:S(2)}, u32[]{:S(2)}) collective-permute-start(s16[4,32,512]{2,1,0:T(8,128)(2,1)S(1)} %get-tuple-element.43), channel_id=1, source_target_pairs={{0,16},{4,20},{8,24},{12,28},{16,0},{20,4},{24,8},{28,12},{1,17},{... | collective-permute-start | bytes 393224 | tf_op jit(solution)/shard_map/ppermute | solution.py:451
  54.4 18.5 %collective-permute-start.16 = (s16[4,32,512]{2,1,0:T(8,128)(2,1)S(1)}, s16[4,32,512]{2,1,0:T(8,128)(2,1)S(1)}, u32[]{:S(2)}, u32[]{:S(2)}) collective-permute-start(s16[4,32,512]{2,1,0:T(8,128)(2,1)S(1)} %get-tuple-element.44), channel_id=1, source_target_pairs={{0,24},{4,28},{8,0},{12,4},{16,8},{20,12},{24,16},{28,20},{1,25},{... | collective-permute-start | bytes 393224 | tf_op jit(solution)/shard_map/ppermute | solution.py:451
  56.3 13.1 %collective-permute-start.10 = (s16[4,16,512]{2,1,0:T(8,128)(2,1)S(1)}, s16[4,16,512]{2,1,0:T(8,128)(2,1)S(1)}, u32[]{:S(2)}, u32[]{:S(2)}) collective-permute-start(s16[4,16,512]{2,1,0:T(8,128)(2,1)S(1)} %get-tuple-element.35), channel_id=1, source_target_pairs={{0,16},{4,20},{8,24},{12,28},{16,0},{20,4},{24,8},{28,12},{1,17},{... | collective-permute-start | bytes 196616 | tf_op jit(solution)/shard_map/ppermute | solution.py:451
  56.5 18.0 %collective-permute-start.11 = (s16[4,16,512]{2,1,0:T(8,128)(2,1)S(1)}, s16[4,16,512]{2,1,0:T(8,128)(2,1)S(1)}, u32[]{:S(2)}, u32[]{:S(2)}) collective-permute-start(s16[4,16,512]{2,1,0:T(8,128)(2,1)S(1)} %get-tuple-element.36), channel_id=1, source_target_pairs={{0,24},{4,28},{8,0},{12,4},{16,8},{20,12},{24,16},{28,20},{1,25},{... | collective-permute-start | bytes 196616 | tf_op jit(solution)/shard_map/ppermute | solution.py:451
  69.3 5.2 %collective-permute-start.9 = (s16[4,16,512]{2,1,0:T(8,128)(2,1)S(1)}, s16[4,16,512]{2,1,0:T(8,128)(2,1)S(1)}, u32[]{:S(2)}, u32[]{:S(2)}) collective-permute-start(s16[4,16,512]{2,1,0:T(8,128)(2,1)S(1)} %get-tuple-element.34), channel_id=1, source_target_pairs={{0,8},{4,12},{8,16},{12,20},{16,24},{20,28},{24,0},{28,4},{1,9},{5... | collective-permute-start | bytes 196616 | tf_op jit(solution)/shard_map/ppermute | solution.py:451
  69.3 6.5 %collective-permute-start.5 = (s16[4,16,512]{2,1,0:T(8,128)(2,1)S(1)}, s16[4,16,512]{2,1,0:T(8,128)(2,1)S(1)}, u32[]{:S(2)}, u32[]{:S(2)}) collective-permute-start(s16[4,16,512]{2,1,0:T(8,128)(2,1)S(1)} %get-tuple-element.28), channel_id=1, source_target_pairs={{0,8},{4,12},{8,16},{12,20},{16,24},{20,28},{24,0},{28,4},{1,9},{5... | collective-permute-start | bytes 196616 | tf_op jit(solution)/shard_map/ppermute | solution.py:451
  69.4 10.0 %collective-permute-start.6 = (s16[4,16,512]{2,1,0:T(8,128)(2,1)S(1)}, s16[4,16,512]{2,1,0:T(8,128)(2,1)S(1)}, u32[]{:S(2)}, u32[]{:S(2)}) collective-permute-start(s16[4,16,512]{2,1,0:T(8,128)(2,1)S(1)} %get-tuple-element.29), channel_id=1, source_target_pairs={{0,16},{4,20},{8,24},{12,28},{16,0},{20,4},{24,8},{28,12},{1,17},{... | collective-permute-start | bytes 196616 | tf_op jit(solution)/shard_map/ppermute | solution.py:451
  72.9 6.5 %collective-permute-start.7 = (s16[4,16,512]{2,1,0:T(8,128)(2,1)S(1)}, s16[4,16,512]{2,1,0:T(8,128)(2,1)S(1)}, u32[]{:S(2)}, u32[]{:S(2)}) collective-permute-start(s16[4,16,512]{2,1,0:T(8,128)(2,1)S(1)} %get-tuple-element.30), channel_id=1, source_target_pairs={{0,24},{4,28},{8,0},{12,4},{16,8},{20,12},{24,16},{28,20},{1,25},{... | collective-permute-start | bytes 196616 | tf_op jit(solution)/shard_map/ppermute | solution.py:451

commit v4 on v3

--- a/solution.py
+++ b/solution.py
@@ -149,7 +149,7 @@
 def over_columns(outs, me, inner, body):
     groups, _, _, width = outs[0].shape
     per = width // LANES
-    count = min(2, per)
+    count = min(4, per)
     for slot in range(inner):
         column = lax.rem(lax.rem(me, inner) + slot, inner)
 
@@ -279,25 +279,25 @@
 
 
 def group_kernel(inner, shear, *refs):
-    groups = lax.axis_size("depth") // inner
-    sources, outs = refs[:-groups], refs[-groups:]
+    sources, outs = refs[:inner], refs[inner:]
     me = lax.axis_index("depth")
     flip = shear[0] > shear[shear.shape[0] - 1]
+    groups = len(outs)
 
     def body(order):
-        for part in range(len(sources) // inner):
-            at = slice(part * ROWS, (part + 1) * ROWS)
+        def step(i, carry):
+            at = pl.ds(pl.multiple_of(i * ROWS, ROWS), ROWS)
             for k in range(groups):
                 target = lax.rem(lax.div(me, inner) + k, groups)
                 pieces = [
-                    [
-                        sources[part * inner + shift][target, c].astype(jnp.float32)
-                        for c in range(4)
-                    ]
+                    [sources[shift][target, c, at, :].astype(jnp.float32) for c in range(4)]
                     for shift in order
                 ]
                 for c, value in enumerate(over(pieces)):
                     outs[k][c, at, :] = encode(value)
+            return carry
+
+        lax.fori_loop(0, outs[0].shape[1] // ROWS, step, 0)
 
     ordered(inner, lax.rem(me, inner), flip, body)
 
@@ -424,16 +424,12 @@
         received.append(sides)
 
     frame = None
-    middle = max(strips - 2, 0)
-    stages = ([range(middle)] if middle else []) + [[n] for n in range(middle, len(parts))]
-    for stage in stages:
-        first, count = parts[stage[0]][0], len(stage)
-        chunk = count * ROWS
-        sides = [side for n in stage for side in received[n]]
+    for number, sides in enumerate(received):
+        first = parts[number][0]
         pieces = pl.pallas_call(
             functools.partial(group_kernel, inner),
             out_shape=[jax.ShapeDtypeStruct((4, chunk, width), LINK)] * groups,
-            in_specs=[smem] + [vmem] * len(sides),
+            in_specs=[smem] + [vmem] * inner,
             out_specs=[vmem] * groups,
             cost_estimate=pl.CostEstimate(
                 flops=20 * chunk * ny, bytes_accessed=2 << 20, transcendentals=0

time: 81.5 us -> 83.7 us (1.027)
  the two profiles are of different devices: /device:TPU:1 before, /device:TPU:0 now
where the time goes in v4:
time: 83.7 us; the launch traced here: 83.5 us
  starting transfers between devices  38.2 us (46%)
  Pallas kernels  33.3 us (40%)
  waiting for transfers between devices  7.61 us (9%)
  local copies, waits for them, and re-layouts  4.15 us (5%)
    ppermute x12, starting transfers between devices, shards(): pieces[k] = lax.ppermute(pieces[k], 'depth', pairs)  24.2 us
    pallas_call x3, Pallas kernels, shards(): pl.pallas_call(functools.partial(inner_kernel, absorb, strip_of, strips),...  16.8 us
    pallas_call x4, Pallas kernels, shards(): pl.pallas_call(functools.partial(outer_kernel, absorb, inner, strip_of, s...  7.77 us
    ppermute x1, waiting for transfers between devices, shards(): prev = lax.ppermute(volume[slices - 1], 'depth', depth_up)  6.47 us
    pallas_call x4, Pallas kernels, shards(): pl.pallas_call(functools.partial(frame_kernel, inner, frame is not None),...  5.64 us
    ppermute x1, starting transfers between devices, shards(): prev = lax.ppermute(volume[slices - 1], 'depth', depth_up)  4.9 us
    ppermute x4, starting transfers between devices, shards(): sides[k] = lax.ppermute(sides[k], 'depth', pairs)  4.79 us
    pallas_call x4, Pallas kernels, shards(): pl.pallas_call(functools.partial(group_kernel, inner), out_shape=[jax.Sha...  3.16 us
  transfers between devices with their start and end apart: 20, of which 3 were waited for; matrix products, arithmetic and copies ran while one was open for 2% of the time, Pallas kernels for 38%

profile of v4, /device:TPU:0, one launch (start us, length us, event | category | flops | bytes accessed | tf_op | source)
XLA Modules:
  0.0 83.5 jit_solution(5798286392573961591)
XLA Ops:
  0.0 1.3 %slice_bitcast_fusion = (bf16[64,4096]{1,0:T(8,128)(2,1)S(1)}, bf16[64,4096]{1,0:T(8,128)(2,1)S(1)}) fusion(bf16[8,64,4096]{2,1,0:T(8,128)(2,1)} %refs_5_.7), kind=kLoop, calls=%fused_computation | loop fusion | bytes 2097152 | tf_op jit(solution)/shard_map/squeeze | solution.py:346
  1.3 4.9 %collective-permute-start = (bf16[64,4096]{1,0:T(8,128)(2,1)S(1)}, bf16[64,4096]{1,0:T(8,128)(2,1)S(1)}, u32[]{:S(2)}, u32[]{:S(2)}) collective-permute-start(bf16[64,4096]{1,0:T(8,128)(2,1)S(1)} %get-tuple-element.56), channel_id=1, source_target_pairs={{0,4},{4,8},{8,12},{12,16},{16,20},{20,24},{24,28},{1,5},{5,9},{9,... | collective-permute-start | bytes 1572872 | tf_op jit(solution)/shard_map/ppermute | solution.py:345
  6.2 1.3 %collective-permute-start.1 = (bf16[64,4096]{1,0:T(8,128)(2,1)S(1)}, bf16[64,4096]{1,0:T(8,128)(2,1)S(1)}, u32[]{:S(2)}, u32[]{:S(2)}) collective-permute-start(bf16[64,4096]{1,0:T(8,128)(2,1)S(1)} %get-tuple-element.55), channel_id=1, source_target_pairs={{4,0},{8,4},{12,8},{16,12},{20,16},{24,20},{28,24},{5,1},{9,5},{13... | collective-permute-start | bytes 1572872 | tf_op jit(solution)/shard_map/ppermute | solution.py:346
  7.5 1.4 %fusion = (bf16[8,1,4096]{2,1,0:T(2,128)(2,1)S(1)}, bf16[8,1,4096]{2,1,0:T(2,128)(2,1)S(1)}) fusion(bf16[8,64,4096]{2,1,0:T(8,128)(2,1)} %refs_5_.7), kind=kLoop, calls=%fused_computation.4 | loop fusion | bytes 262144 | tf_op jit(solution)/shard_map/slice | solution.py:348
  8.9 0.1 copy.14
  9.0 1.5 %collective-permute-start.2 = (bf16[8,4096]{1,0:T(8,128)(2,1)S(1)}, bf16[8,4096]{1,0:T(8,128)(2,1)S(1)}, u32[]{:S(2)}, u32[]{:S(2)}) collective-permute-start(bf16[8,4096]{1,0:T(8,128)(2,1)S(1)} %bitcast.10), channel_id=1, source_target_pairs={{0,1},{1,2},{2,3},{4,5},{5,6},{6,7},{8,9},{9,10},{10,11},{12,13},{... | collective-permute-start | bytes 196616 | tf_op jit(solution)/shard_map/ppermute | solution.py:347
  10.5 0.1 copy.13
  10.5 0.0 copy-start
  10.5 1.6 %collective-permute-start.3 = (bf16[8,4096]{1,0:T(8,128)(2,1)S(1)}, bf16[8,4096]{1,0:T(8,128)(2,1)S(1)}, u32[]{:S(2)}, u32[]{:S(2)}) collective-permute-start(bf16[8,4096]{1,0:T(8,128)(2,1)S(1)} %bitcast.11), channel_id=1, source_target_pairs={{1,0},{2,1},{3,2},{5,4},{6,5},{7,6},{9,8},{10,9},{11,10},{13,12},{... | collective-permute-start | bytes 196616 | tf_op jit(solution)/shard_map/ppermute | solution.py:348
  12.1 0.0 copy-start.1
  12.1 0.6 copy-done.1
  12.8 0.7 copy-done.2
  13.4 8.7 %inner.5.refs_8_ = f32[4,32,4096]{2,1,0:T(8,128)S(1)} custom-call(s32[64]{0:T(128)S(1)} %copy-done.1, s32[1,2]{1,0:T(1,128)S(1)} %copy-done.2, bf16[8,64,4096]{2,1,0:T(8,128)(2,1)} %refs_5_.7, bf16[8,64,4096]{2,1,0:T(8,128)(2,1)} %refs_5_.7, bf16[8,64,4096]{2,1,0:T(8,128)(2,1)} %refs_5_.7), custom_call_target="tpu_custom_call" | custom-call | flops 104857600 | bytes 4194304 | tf_op jit(solution)/shard_map/inner/pallas_call | solution.py:377
  22.1 6.5 %collective-permute-done.refs_6_ = bf16[64,4096]{1,0:T(8,128)(2,1)S(1)} collective-permute-done((bf16[64,4096]{1,0:T(8,128)(2,1)S(1)}, bf16[64,4096]{1,0:T(8,128)(2,1)S(1)}, u32[]{:S(2)}, u32[]{:S(2)}) %collective-permute-start) | collective-permute-done | bytes 524320 | tf_op jit(solution)/shard_map/ppermute | solution.py:345
  28.6 0.0 collective-permute-done.1.refs_7_
  28.6 1.9 %outer.7 = (bf16[4,4,16,512]{3,2,1,0:T(8,128)(2,1)S(1)}, bf16[4,4,16,512]{3,2,1,0:T(8,128)(2,1)S(1)}) custom-call(s32[64]{0:T(128)S(1)} %copy-done.1, s32[1,2]{1,0:T(1,128)S(1)} %copy-done.2, bf16[8,64,4096]{2,1,0:T(8,128)(2,1)S(1)} %copy-done, bf16[8,64,4096]{2,1,0:T(8,128)(2,1)S(1)} %copy-done, bf16[8,64,4096]{2,1,0:T(8,128)(2,1)S(1)} %copy-done, ...), custom_call_target="tpu_custom_call" | custom-call | flops 26214400 | bytes 2097152 | tf_op jit(solution)/shard_map/outer/pallas_call | solution.py:401
  30.5 2.5 %collective-permute-start.16 = (bf16[4,4,16,512]{3,2,1,0:T(8,128)(2,1)S(1)}, bf16[4,4,16,512]{3,2,1,0:T(8,128)(2,1)S(1)}, u32[]{:S(2)}, u32[]{:S(2)}) collective-permute-start(bf16[4,4,16,512]{3,2,1,0:T(8,128)(2,1)S(1)} %get-tuple-element.48), channel_id=1, source_target_pairs={{0,4},{4,0},{8,12},{12,8},{16,20},{20,16},{24,28},{28,24},{1,5},{5... | collective-permute-start | bytes 786440 | tf_op jit(solution)/shard_map/ppermute | solution.py:423
  33.1 0.0 collective-permute-done.2.refs_0_.refs_9_
  33.1 4.1 %inner.4.refs_8_ = f32[4,16,4096]{2,1,0:T(8,128)S(1)} custom-call(s32[64]{0:T(128)S(1)} %copy-done.1, s32[1,2]{1,0:T(1,128)S(1)} %copy-done.2, bf16[8,64,4096]{2,1,0:T(8,128)(2,1)S(1)} %copy-done, bf16[8,64,4096]{2,1,0:T(8,128)(2,1)S(1)} %copy-done, bf16[8,64,4096]{2,1,0:T(8,128)(2,1)S(1)} %copy-done, ...), custom_call_target="tpu_custom_call" | custom-call | flops 52428800 | bytes 2097152 | tf_op jit(solution)/shard_map/inner/pallas_call | solution.py:377
  37.1 4.0 %inner.3.refs_8_ = f32[4,16,4096]{2,1,0:T(8,128)S(1)} custom-call(s32[64]{0:T(128)S(1)} %copy-done.1, s32[1,2]{1,0:T(1,128)S(1)} %copy-done.2, bf16[8,64,4096]{2,1,0:T(8,128)(2,1)S(1)} %copy-done, bf16[8,64,4096]{2,1,0:T(8,128)(2,1)S(1)} %copy-done, bf16[8,64,4096]{2,1,0:T(8,128)(2,1)S(1)} %copy-done, ...), custom_call_target="tpu_custom_call" | custom-call | flops 52428800 | bytes 2097152 | tf_op jit(solution)/shard_map/inner/pallas_call | solution.py:377
  41.2 1.9 %outer.6 = (bf16[4,4,16,512]{3,2,1,0:T(8,128)(2,1)S(1)}, bf16[4,4,16,512]{3,2,1,0:T(8,128)(2,1)S(1)}) custom-call(s32[64]{0:T(128)S(1)} %copy-done.1, s32[1,2]{1,0:T(1,128)S(1)} %copy-done.2, bf16[8,64,4096]{2,1,0:T(8,128)(2,1)S(1)} %copy-done, bf16[8,64,4096]{2,1,0:T(8,128)(2,1)S(1)} %copy-done, bf16[8,64,4096]{2,1,0:T(8,128)(2,1)S(1)} %copy-done, ...), custom_call_target="tpu_custom_call" | custom-call | flops 26214400 | bytes 2097152 | tf_op jit(solution)/shard_map/outer/pallas_call | solution.py:401
  43.1 0.1 collective-permute-start.12
  43.2 1.9 %outer.5 = (bf16[4,4,16,512]{3,2,1,0:T(8,128)(2,1)S(1)}, bf16[4,4,16,512]{3,2,1,0:T(8,128)(2,1)S(1)}) custom-call(s32[64]{0:T(128)S(1)} %copy-done.1, s32[1,2]{1,0:T(1,128)S(1)} %copy-done.2, bf16[8,64,4096]{2,1,0:T(8,128)(2,1)S(1)} %copy-done, bf16[8,64,4096]{2,1,0:T(8,128)(2,1)S(1)} %copy-done, bf16[8,64,4096]{2,1,0:T(8,128)(2,1)S(1)} %copy-done, ...), custom_call_target="tpu_custom_call" | custom-call | flops 26214400 | bytes 2097152 | tf_op jit(solution)/shard_map/outer/pallas_call | solution.py:401
  45.2 2.1 %collective-permute-start.8 = (bf16[4,4,16,512]{3,2,1,0:T(8,128)(2,1)S(1)}, bf16[4,4,16,512]{3,2,1,0:T(8,128)(2,1)S(1)}, u32[]{:S(2)}, u32[]{:S(2)}) collective-permute-start(bf16[4,4,16,512]{3,2,1,0:T(8,128)(2,1)S(1)} %get-tuple-element.36), channel_id=1, source_target_pairs={{0,4},{4,0},{8,12},{12,8},{16,20},{20,16},{24,28},{28,24},{1,5},{5... | collective-permute-start | bytes 786440 | tf_op jit(solution)/shard_map/ppermute | solution.py:423
  47.2 1.9 %outer.4 = (bf16[4,4,16,512]{3,2,1,0:T(8,128)(2,1)S(1)}, bf16[4,4,16,512]{3,2,1,0:T(8,128)(2,1)S(1)}) custom-call(s32[64]{0:T(128)S(1)} %copy-done.1, s32[1,2]{1,0:T(1,128)S(1)} %copy-done.2, bf16[8,64,4096]{2,1,0:T(8,128)(2,1)S(1)} %copy-done, bf16[8,64,4096]{2,1,0:T(8,128)(2,1)S(1)} %copy-done, bf16[8,64,4096]{2,1,0:T(8,128)(2,1)S(1)} %copy-done, ...), custom_call_target="tpu_custom_call" | custom-call | flops 26214400 | bytes 2097152 | tf_op jit(solution)/shard_map/outer/pallas_call | solution.py:401
  49.2 0.1 collective-permute-start.4
  49.3 0.8 group.7
  50.1 3.0 %collective-permute-start.17 = (s16[4,16,512]{2,1,0:T(8,128)(2,1)S(1)}, s16[4,16,512]{2,1,0:T(8,128)(2,1)S(1)}, u32[]{:S(2)}, u32[]{:S(2)}) collective-permute-start(s16[4,16,512]{2,1,0:T(8,128)(2,1)S(1)} %get-tuple-element.50), channel_id=1, source_target_pairs={{0,8},{4,12},{8,16},{12,20},{16,24},{20,28},{24,0},{28,4},{1,9},{5... | collective-permute-start | bytes 196616 | tf_op jit(solution)/shard_map/ppermute | solution.py:447
  53.1 2.6 %collective-permute-start.18 = (s16[4,16,512]{2,1,0:T(8,128)(2,1)S(1)}, s16[4,16,512]{2,1,0:T(8,128)(2,1)S(1)}, u32[]{:S(2)}, u32[]{:S(2)}) collective-permute-start(s16[4,16,512]{2,1,0:T(8,128)(2,1)S(1)} %get-tuple-element.51), channel_id=1, source_target_pairs={{0,16},{4,20},{8,24},{12,28},{16,0},{20,4},{24,8},{28,12},{1,17},{... | collective-permute-start | bytes 196616 | tf_op jit(solution)/shard_map/ppermute | solution.py:447
  55.7 1.4 %collective-permute-start.19 = (s16[4,16,512]{2,1,0:T(8,128)(2,1)S(1)}, s16[4,16,512]{2,1,0:T(8,128)(2,1)S(1)}, u32[]{:S(2)}, u32[]{:S(2)}) collective-permute-start(s16[4,16,512]{2,1,0:T(8,128)(2,1)S(1)} %get-tuple-element.52), channel_id=1, source_target_pairs={{0,24},{4,28},{8,0},{12,4},{16,8},{20,12},{24,16},{28,20},{1,25},{... | collective-permute-start | bytes 196616 | tf_op jit(solution)/shard_map/ppermute | solution.py:447
  57.1 0.8 group.6
  57.9 0.1 collective-permute-done.8.refs_1_
  58.0 1.6 %collective-permute-start.13 = (s16[4,16,512]{2,1,0:T(8,128)(2,1)S(1)}, s16[4,16,512]{2,1,0:T(8,128)(2,1)S(1)}, u32[]{:S(2)}, u32[]{:S(2)}) collective-permute-start(s16[4,16,512]{2,1,0:T(8,128)(2,1)S(1)} %get-tuple-element.44), channel_id=1, source_target_pairs={{0,8},{4,12},{8,16},{12,20},{16,24},{20,28},{24,0},{28,4},{1,9},{5... | collective-permute-start | bytes 196616 | tf_op jit(solution)/shard_map/ppermute | solution.py:447
  59.6 0.8 group.5
  60.4 1.0 %collective-permute-done.4.refs_1_ = bf16[4,4,16,512]{3,2,1,0:T(8,128)(2,1)S(1)} collective-permute-done((bf16[4,4,16,512]{3,2,1,0:T(8,128)(2,1)S(1)}, bf16[4,4,16,512]{3,2,1,0:T(8,128)(2,1)S(1)}, u32[]{:S(2)}, u32[]{:S(2)}) %collective-permute-start.4) | collective-permute-done | bytes 262176 | tf_op jit(solution)/shard_map/ppermute | solution.py:423
  61.3 3.3 %collective-permute-start.14 = (s16[4,16,512]{2,1,0:T(8,128)(2,1)S(1)}, s16[4,16,512]{2,1,0:T(8,128)(2,1)S(1)}, u32[]{:S(2)}, u32[]{:S(2)}) collective-permute-start(s16[4,16,512]{2,1,0:T(8,128)(2,1)S(1)} %get-tuple-element.45), channel_id=1, source_target_pairs={{0,16},{4,20},{8,24},{12,28},{16,0},{20,4},{24,8},{28,12},{1,17},{... | collective-permute-start | bytes 196616 | tf_op jit(solution)/shard_map/ppermute | solution.py:447
  64.7 1.3 %collective-permute-start.15 = (s16[4,16,512]{2,1,0:T(8,128)(2,1)S(1)}, s16[4,16,512]{2,1,0:T(8,128)(2,1)S(1)}, u32[]{:S(2)}, u32[]{:S(2)}) collective-permute-start(s16[4,16,512]{2,1,0:T(8,128)(2,1)S(1)} %get-tuple-element.46), channel_id=1, source_target_pairs={{0,24},{4,28},{8,0},{12,4},{16,8},{20,12},{24,16},{28,20},{1,25},{... | collective-permute-start | bytes 196616 | tf_op jit(solution)/shard_map/ppermute | solution.py:447
  66.0 1.7 %collective-permute-start.10 = (s16[4,16,512]{2,1,0:T(8,128)(2,1)S(1)}, s16[4,16,512]{2,1,0:T(8,128)(2,1)S(1)}, u32[]{:S(2)}, u32[]{:S(2)}) collective-permute-start(s16[4,16,512]{2,1,0:T(8,128)(2,1)S(1)} %get-tuple-element.39), channel_id=1, source_target_pairs={{0,16},{4,20},{8,24},{12,28},{16,0},{20,4},{24,8},{28,12},{1,17},{... | collective-permute-start | bytes 196616 | tf_op jit(solution)/shard_map/ppermute | solution.py:447
  67.7 0.8 group.4
  68.5 1.4 %collective-permute-start.11 = (s16[4,16,512]{2,1,0:T(8,128)(2,1)S(1)}, s16[4,16,512]{2,1,0:T(8,128)(2,1)S(1)}, u32[]{:S(2)}, u32[]{:S(2)}) collective-permute-start(s16[4,16,512]{2,1,0:T(8,128)(2,1)S(1)} %get-tuple-element.40), channel_id=1, source_target_pairs={{0,24},{4,28},{8,0},{12,4},{16,8},{20,12},{24,16},{28,20},{1,25},{... | collective-permute-start | bytes 196616 | tf_op jit(solution)/shard_map/ppermute | solution.py:447
  69.9 0.7 collective-permute-start.9
  70.6 1.4 %collective-permute-start.5 = (s16[4,16,512]{2,1,0:T(8,128)(2,1)S(1)}, s16[4,16,512]{2,1,0:T(8,128)(2,1)S(1)}, u32[]{:S(2)}, u32[]{:S(2)}) collective-permute-start(s16[4,16,512]{2,1,0:T(8,128)(2,1)S(1)} %get-tuple-element.32), channel_id=1, source_target_pairs={{0,8},{4,12},{8,16},{12,20},{16,24},{20,28},{24,0},{28,4},{1,9},{5... | collective-permute-start | bytes 196616 | tf_op jit(solution)/shard_map/ppermute | solution.py:447
  72.0 3.5 %collective-permute-start.6 = (s16[4,16,512]{2,1,0:T(8,128)(2,1)S(1)}, s16[4,16,512]{2,1,0:T(8,128)(2,1)S(1)}, u32[]{:S(2)}, u32[]{:S(2)}) collective-permute-start(s16[4,16,512]{2,1,0:T(8,128)(2,1)S(1)} %get-tuple-element.33), channel_id=1, source_target_pairs={{0,16},{4,20},{8,24},{12,28},{16,0},{20,4},{24,8},{28,12},{1,17},{... | collective-permute-start | bytes 196616 | tf_op jit(solution)/shard_map/ppermute | solution.py:447
  75.5 2.2 %collective-permute-start.7 = (s16[4,16,512]{2,1,0:T(8,128)(2,1)S(1)}, s16[4,16,512]{2,1,0:T(8,128)(2,1)S(1)}, u32[]{:S(2)}, u32[]{:S(2)}) collective-permute-start(s16[4,16,512]{2,1,0:T(8,128)(2,1)S(1)} %get-tuple-element.34), channel_id=1, source_target_pairs={{0,24},{4,28},{8,0},{12,4},{16,8},{20,12},{24,16},{28,20},{1,25},{... | collective-permute-start | bytes 196616 | tf_op jit(solution)/shard_map/ppermute | solution.py:447
  77.8 1.5 %frame.4.refs_4_ = f32[4,64,512]{2,1,0:T(8,128)} custom-call(s32[64]{0:T(128)S(1)} %copy-done.1, s16[4,16,512]{2,1,0:T(8,128)(2,1)S(1)} %get-tuple-element.49.refs_0_, s16[4,16,512]{2,1,0:T(8,128)(2,1)S(1)} %collective-permute-done.17.refs_1_, s16[4,16,512]{2,1,0:T(8,128)(2,1)S(1)} %collective-permute-done.18.refs_2_, ...), custom_call_target="tpu_custom_call" | custom-call | flops 163840 | bytes 2097152 | tf_op jit(solution)/shard_map/frame/pallas_call | solution.py:448
  79.3 1.4 %frame.5.refs_4_ = f32[4,64,512]{2,1,0:T(8,128)} custom-call(s32[64]{0:T(128)S(1)} %copy-done.1, s16[4,16,512]{2,1,0:T(8,128)(2,1)S(1)} %get-tuple-element.43.refs_0_, s16[4,16,512]{2,1,0:T(8,128)(2,1)S(1)} %collective-permute-done.13.refs_1_, s16[4,16,512]{2,1,0:T(8,128)(2,1)S(1)} %collective-permute-done.14.refs_2_, ...), custom_call_target="tpu_custom_call", output_to_operand_aliasing={{}: (5, {})} | custom-call | flops 163840 | bytes 2097152 | tf_op jit(solution)/shard_map/frame/pallas_call | solution.py:448
  80.7 1.4 %frame.6.refs_4_ = f32[4,64,512]{2,1,0:T(8,128)} custom-call(s32[64]{0:T(128)S(1)} %copy-done.1, s16[4,16,512]{2,1,0:T(8,128)(2,1)S(1)} %get-tuple-element.37.refs_0_, s16[4,16,512]{2,1,0:T(8,128)(2,1)S(1)} %collective-permute-done.9.refs_1_, s16[4,16,512]{2,1,0:T(8,128)(2,1)S(1)} %collective-permute-done.10.refs_2_, ...), custom_call_target="tpu_custom_call", output_to_operand_aliasing={{}: (5, {})} | custom-call | flops 163840 | bytes 2097152 | tf_op jit(solution)/shard_map/frame/pallas_call | solution.py:448
  82.1 1.4 %frame.7 = f32[4,64,512]{2,1,0:T(8,128)} custom-call(s32[64]{0:T(128)S(1)} %copy-done.1, s16[4,16,512]{2,1,0:T(8,128)(2,1)S(1)} %get-tuple-element.31.refs_0_, s16[4,16,512]{2,1,0:T(8,128)(2,1)S(1)} %collective-permute-done.5.refs_1_, s16[4,16,512]{2,1,0:T(8,128)(2,1)S(1)} %collective-permute-done.6.refs_2_, ...), custom_call_target="tpu_custom_call", output_to_operand_aliasing={{}: (5, {})} | custom-call | flops 163840 | bytes 2097152 | tf_op jit(solution)/shard_map/frame/pallas_call | solution.py:448
  (17 shorter events, 0.0 us)
Async XLA Ops:
  1.3 27.3 %collective-permute-start = (bf16[64,4096]{1,0:T(8,128)(2,1)S(1)}, bf16[64,4096]{1,0:T(8,128)(2,1)S(1)}, u32[]{:S(2)}, u32[]{:S(2)}) collective-permute-start(bf16[64,4096]{1,0:T(8,128)(2,1)S(1)} %get-tuple-element.56), channel_id=1, source_target_pairs={{0,4},{4,8},{8,12},{12,16},{16,20},{20,24},{24,28},{1,5},{5,9},{9,... | collective-permute-start | bytes 1572872 | tf_op jit(solution)/shard_map/ppermute | solution.py:345
  6.2 22.4 %collective-permute-start.1 = (bf16[64,4096]{1,0:T(8,128)(2,1)S(1)}, bf16[64,4096]{1,0:T(8,128)(2,1)S(1)}, u32[]{:S(2)}, u32[]{:S(2)}) collective-permute-start(bf16[64,4096]{1,0:T(8,128)(2,1)S(1)} %get-tuple-element.55), channel_id=1, source_target_pairs={{4,0},{8,4},{12,8},{16,12},{20,16},{24,20},{28,24},{5,1},{9,5},{13... | collective-permute-start | bytes 1572872 | tf_op jit(solution)/shard_map/ppermute | solution.py:346
  9.0 24.1 %collective-permute-start.2 = (bf16[8,4096]{1,0:T(8,128)(2,1)S(1)}, bf16[8,4096]{1,0:T(8,128)(2,1)S(1)}, u32[]{:S(2)}, u32[]{:S(2)}) collective-permute-start(bf16[8,4096]{1,0:T(8,128)(2,1)S(1)} %bitcast.10), channel_id=1, source_target_pairs={{0,1},{1,2},{2,3},{4,5},{5,6},{6,7},{8,9},{9,10},{10,11},{12,13},{... | collective-permute-start | bytes 196616 | tf_op jit(solution)/shard_map/ppermute | solution.py:347
  10.5 18.0 %copy-start = (bf16[8,64,4096]{2,1,0:T(8,128)(2,1)S(1)}, bf16[8,64,4096]{2,1,0:T(8,128)(2,1)}, u32[]{:S(2)}) copy-start(bf16[8,64,4096]{2,1,0:T(8,128)(2,1)} %refs_5_.7) | copy-start | bytes 12582916
  10.5 22.5 %collective-permute-start.3 = (bf16[8,4096]{1,0:T(8,128)(2,1)S(1)}, bf16[8,4096]{1,0:T(8,128)(2,1)S(1)}, u32[]{:S(2)}, u32[]{:S(2)}) collective-permute-start(bf16[8,4096]{1,0:T(8,128)(2,1)S(1)} %bitcast.11), channel_id=1, source_target_pairs={{1,0},{2,1},{3,2},{5,4},{6,5},{7,6},{9,8},{10,9},{11,10},{13,12},{... | collective-permute-start | bytes 196616 | tf_op jit(solution)/shard_map/ppermute | solution.py:348
  12.1 0.7 copy-start.1
  12.8 0.7 copy-start.2
  30.5 18.8 %collective-permute-start.16 = (bf16[4,4,16,512]{3,2,1,0:T(8,128)(2,1)S(1)}, bf16[4,4,16,512]{3,2,1,0:T(8,128)(2,1)S(1)}, u32[]{:S(2)}, u32[]{:S(2)}) collective-permute-start(bf16[4,4,16,512]{3,2,1,0:T(8,128)(2,1)S(1)} %get-tuple-element.48), channel_id=1, source_target_pairs={{0,4},{4,0},{8,12},{12,8},{16,20},{20,16},{24,28},{28,24},{1,5},{5... | collective-permute-start | bytes 786440 | tf_op jit(solution)/shard_map/ppermute | solution.py:423
  43.1 12.6 %collective-permute-start.12 = (bf16[4,4,16,512]{3,2,1,0:T(8,128)(2,1)S(1)}, bf16[4,4,16,512]{3,2,1,0:T(8,128)(2,1)S(1)}, u32[]{:S(2)}, u32[]{:S(2)}) collective-permute-start(bf16[4,4,16,512]{3,2,1,0:T(8,128)(2,1)S(1)} %get-tuple-element.42), channel_id=1, source_target_pairs={{0,4},{4,0},{8,12},{12,8},{16,20},{20,16},{24,28},{28,24},{1,5},{5... | collective-permute-start | bytes 786440 | tf_op jit(solution)/shard_map/ppermute | solution.py:423
  45.2 12.8 %collective-permute-start.8 = (bf16[4,4,16,512]{3,2,1,0:T(8,128)(2,1)S(1)}, bf16[4,4,16,512]{3,2,1,0:T(8,128)(2,1)S(1)}, u32[]{:S(2)}, u32[]{:S(2)}) collective-permute-start(bf16[4,4,16,512]{3,2,1,0:T(8,128)(2,1)S(1)} %get-tuple-element.36), channel_id=1, source_target_pairs={{0,4},{4,0},{8,12},{12,8},{16,20},{20,16},{24,28},{28,24},{1,5},{5... | collective-permute-start | bytes 786440 | tf_op jit(solution)/shard_map/ppermute | solution.py:423
  49.2 12.1 %collective-permute-start.4 = (bf16[4,4,16,512]{3,2,1,0:T(8,128)(2,1)S(1)}, bf16[4,4,16,512]{3,2,1,0:T(8,128)(2,1)S(1)}, u32[]{:S(2)}, u32[]{:S(2)}) collective-permute-start(bf16[4,4,16,512]{3,2,1,0:T(8,128)(2,1)S(1)} %get-tuple-element.30), channel_id=1, source_target_pairs={{0,4},{4,0},{8,12},{12,8},{16,20},{20,16},{24,28},{28,24},{1,5},{5... | collective-permute-start | bytes 786440 | tf_op jit(solution)/shard_map/ppermute | solution.py:423
  50.1 14.6 %collective-permute-start.17 = (s16[4,16,512]{2,1,0:T(8,128)(2,1)S(1)}, s16[4,16,512]{2,1,0:T(8,128)(2,1)S(1)}, u32[]{:S(2)}, u32[]{:S(2)}) collective-permute-start(s16[4,16,512]{2,1,0:T(8,128)(2,1)S(1)} %get-tuple-element.50), channel_id=1, source_target_pairs={{0,8},{4,12},{8,16},{12,20},{16,24},{20,28},{24,0},{28,4},{1,9},{5... | collective-permute-start | bytes 196616 | tf_op jit(solution)/shard_map/ppermute | solution.py:447
  53.1 12.9 %collective-permute-start.18 = (s16[4,16,512]{2,1,0:T(8,128)(2,1)S(1)}, s16[4,16,512]{2,1,0:T(8,128)(2,1)S(1)}, u32[]{:S(2)}, u32[]{:S(2)}) collective-permute-start(s16[4,16,512]{2,1,0:T(8,128)(2,1)S(1)} %get-tuple-element.51), channel_id=1, source_target_pairs={{0,16},{4,20},{8,24},{12,28},{16,0},{20,4},{24,8},{28,12},{1,17},{... | collective-permute-start | bytes 196616 | tf_op jit(solution)/shard_map/ppermute | solution.py:447
  55.7 12.8 %collective-permute-start.19 = (s16[4,16,512]{2,1,0:T(8,128)(2,1)S(1)}, s16[4,16,512]{2,1,0:T(8,128)(2,1)S(1)}, u32[]{:S(2)}, u32[]{:S(2)}) collective-permute-start(s16[4,16,512]{2,1,0:T(8,128)(2,1)S(1)} %get-tuple-element.52), channel_id=1, source_target_pairs={{0,24},{4,28},{8,0},{12,4},{16,8},{20,12},{24,16},{28,20},{1,25},{... | collective-permute-start | bytes 196616 | tf_op jit(solution)/shard_map/ppermute | solution.py:447
  58.0 12.0 %collective-permute-start.13 = (s16[4,16,512]{2,1,0:T(8,128)(2,1)S(1)}, s16[4,16,512]{2,1,0:T(8,128)(2,1)S(1)}, u32[]{:S(2)}, u32[]{:S(2)}) collective-permute-start(s16[4,16,512]{2,1,0:T(8,128)(2,1)S(1)} %get-tuple-element.44), channel_id=1, source_target_pairs={{0,8},{4,12},{8,16},{12,20},{16,24},{20,28},{24,0},{28,4},{1,9},{5... | collective-permute-start | bytes 196616 | tf_op jit(solution)/shard_map/ppermute | solution.py:447
  61.3 9.3 %collective-permute-start.14 = (s16[4,16,512]{2,1,0:T(8,128)(2,1)S(1)}, s16[4,16,512]{2,1,0:T(8,128)(2,1)S(1)}, u32[]{:S(2)}, u32[]{:S(2)}) collective-permute-start(s16[4,16,512]{2,1,0:T(8,128)(2,1)S(1)} %get-tuple-element.45), channel_id=1, source_target_pairs={{0,16},{4,20},{8,24},{12,28},{16,0},{20,4},{24,8},{28,12},{1,17},{... | collective-permute-start | bytes 196616 | tf_op jit(solution)/shard_map/ppermute | solution.py:447
  64.7 7.3 %collective-permute-start.15 = (s16[4,16,512]{2,1,0:T(8,128)(2,1)S(1)}, s16[4,16,512]{2,1,0:T(8,128)(2,1)S(1)}, u32[]{:S(2)}, u32[]{:S(2)}) collective-permute-start(s16[4,16,512]{2,1,0:T(8,128)(2,1)S(1)} %get-tuple-element.46), channel_id=1, source_target_pairs={{0,24},{4,28},{8,0},{12,4},{16,8},{20,12},{24,16},{28,20},{1,25},{... | collective-permute-start | bytes 196616 | tf_op jit(solution)/shard_map/ppermute | solution.py:447
  66.0 9.5 %collective-permute-start.10 = (s16[4,16,512]{2,1,0:T(8,128)(2,1)S(1)}, s16[4,16,512]{2,1,0:T(8,128)(2,1)S(1)}, u32[]{:S(2)}, u32[]{:S(2)}) collective-permute-start(s16[4,16,512]{2,1,0:T(8,128)(2,1)S(1)} %get-tuple-element.39), channel_id=1, source_target_pairs={{0,16},{4,20},{8,24},{12,28},{16,0},{20,4},{24,8},{28,12},{1,17},{... | collective-permute-start | bytes 196616 | tf_op jit(solution)/shard_map/ppermute | solution.py:447
  68.5 12.2 %collective-permute-start.11 = (s16[4,16,512]{2,1,0:T(8,128)(2,1)S(1)}, s16[4,16,512]{2,1,0:T(8,128)(2,1)S(1)}, u32[]{:S(2)}, u32[]{:S(2)}) collective-permute-start(s16[4,16,512]{2,1,0:T(8,128)(2,1)S(1)} %get-tuple-element.40), channel_id=1, source_target_pairs={{0,24},{4,28},{8,0},{12,4},{16,8},{20,12},{24,16},{28,20},{1,25},{... | collective-permute-start | bytes 196616 | tf_op jit(solution)/shard_map/ppermute | solution.py:447
  69.9 10.8 %collective-permute-start.9 = (s16[4,16,512]{2,1,0:T(8,128)(2,1)S(1)}, s16[4,16,512]{2,1,0:T(8,128)(2,1)S(1)}, u32[]{:S(2)}, u32[]{:S(2)}) collective-permute-start(s16[4,16,512]{2,1,0:T(8,128)(2,1)S(1)} %get-tuple-element.38), channel_id=1, source_target_pairs={{0,8},{4,12},{8,16},{12,20},{16,24},{20,28},{24,0},{28,4},{1,9},{5... | collective-permute-start | bytes 196616 | tf_op jit(solution)/shard_map/ppermute | solution.py:447
  70.6 11.4 %collective-permute-start.5 = (s16[4,16,512]{2,1,0:T(8,128)(2,1)S(1)}, s16[4,16,512]{2,1,0:T(8,128)(2,1)S(1)}, u32[]{:S(2)}, u32[]{:S(2)}) collective-permute-start(s16[4,16,512]{2,1,0:T(8,128)(2,1)S(1)} %get-tuple-element.32), channel_id=1, source_target_pairs={{0,8},{4,12},{8,16},{12,20},{16,24},{20,28},{24,0},{28,4},{1,9},{5... | collective-permute-start | bytes 196616 | tf_op jit(solution)/shard_map/ppermute | solution.py:447
  72.0 10.1 %collective-permute-start.6 = (s16[4,16,512]{2,1,0:T(8,128)(2,1)S(1)}, s16[4,16,512]{2,1,0:T(8,128)(2,1)S(1)}, u32[]{:S(2)}, u32[]{:S(2)}) collective-permute-start(s16[4,16,512]{2,1,0:T(8,128)(2,1)S(1)} %get-tuple-element.33), channel_id=1, source_target_pairs={{0,16},{4,20},{8,24},{12,28},{16,0},{20,4},{24,8},{28,12},{1,17},{... | collective-permute-start | bytes 196616 | tf_op jit(solution)/shard_map/ppermute | solution.py:447
  75.5 6.5 %collective-permute-start.7 = (s16[4,16,512]{2,1,0:T(8,128)(2,1)S(1)}, s16[4,16,512]{2,1,0:T(8,128)(2,1)S(1)}, u32[]{:S(2)}, u32[]{:S(2)}) collective-permute-start(s16[4,16,512]{2,1,0:T(8,128)(2,1)S(1)} %get-tuple-element.34), channel_id=1, source_target_pairs={{0,24},{4,28},{8,0},{12,4},{16,8},{20,12},{24,16},{28,20},{1,25},{... | collective-permute-start | bytes 196616 | tf_op jit(solution)/shard_map/ppermute | solution.py:447
